TPU v7x, 256 devices: a whole 4x4x8 slice. The times are simulated.
256 devices in a mesh: dp: 8 (over z), replica: 4 (over y), fsdp: 8 (over x, core).
Axes of the slice: x: 4, y: 4, z: 8, core: 2. Of those that a mesh axis runs over, the one named last changes fastest.
Arguments:
- x_tokens: bfloat16 [32768, 1024], P(('dp', 'replica', 'fsdp'))
- dy_tokens: bfloat16 [32768, 1024], P(('dp', 'replica', 'fsdp'))
- w_gate: bfloat16 [3, 1024, 4096], P(None, 'fsdp')
- w_up: bfloat16 [3, 1024, 4096], P(None, 'fsdp')
- w_down: bfloat16 [3, 4096, 1024], P(None, 'fsdp')
- norm_gain: float32 [3, 1024], replicated
Outputs:
- output 1: bfloat16 [32768, 1024], P(('dp', 'replica', 'fsdp'))
- output 2: float32 [3, 1024, 4096], P(None, 'fsdp')
- output 3: float32 [3, 1024, 4096], P(None, 'fsdp')
- output 4: float32 [3, 4096, 1024], P(None, 'fsdp')
- output 5: float32 [3, 1024], replicated
All inputs are finite; a program needn't handle non-finite values.
Results may differ from a plain program's by a relative error of at most 0.02.
Values are sent between devices in bfloat16 or wider.
A program may use at most 768 MiB of HBM per device.

v0:
```python
import jax
import jax.numpy as jnp
from jax import lax
from jax.sharding import PartitionSpec as P

NORM_EPS = 1e-6
TOKEN_AXES = ("dp", "replica", "fsdp")
COPY_AXES = ("dp", "replica")
CONTRACT_ROWS = (((0,), (0,)), ((), ()))
CONTRACT_COLS = (((1,), (1,)), ((), ()))


def layer_forward(hidden, w_gate, w_up, w_down, gain_row):
    hidden_f = hidden.astype(jnp.float32)
    inv_rms = lax.rsqrt(jnp.mean(hidden_f * hidden_f, axis=-1, keepdims=True) + NORM_EPS)
    normed = (hidden_f * inv_rms * gain_row).astype(jnp.bfloat16)
    gate_act = jnp.dot(normed, w_gate, preferred_element_type=jnp.float32).astype(jnp.bfloat16)
    up_act = jnp.dot(normed, w_up, preferred_element_type=jnp.float32).astype(jnp.bfloat16)
    prod_act = (jax.nn.silu(gate_act.astype(jnp.float32)) * up_act.astype(jnp.float32)).astype(jnp.bfloat16)
    layer_out = (hidden_f + jnp.dot(prod_act, w_down, preferred_element_type=jnp.float32)).astype(jnp.bfloat16)
    return layer_out, (hidden, inv_rms, normed, gate_act, up_act, prod_act)


def layer_backward(cot_out, saved_vals, w_gate, w_up, w_down, gain_row):
    hidden, inv_rms, normed, gate_act, up_act, prod_act = saved_vals
    dw_down = lax.dot_general(prod_act, cot_out, CONTRACT_ROWS, preferred_element_type=jnp.float32)
    d_prod = lax.dot_general(cot_out, w_down, CONTRACT_COLS, preferred_element_type=jnp.float32).astype(jnp.bfloat16).astype(jnp.float32)
    gate_f = gate_act.astype(jnp.float32)
    sig_gate = jax.nn.sigmoid(gate_f)
    d_gate = (d_prod * up_act.astype(jnp.float32) * sig_gate * (1.0 + gate_f * (1.0 - sig_gate))).astype(jnp.bfloat16)
    d_up = (d_prod * gate_f * sig_gate).astype(jnp.bfloat16)
    dw_gate = lax.dot_general(normed, d_gate, CONTRACT_ROWS, preferred_element_type=jnp.float32)
    dw_up = lax.dot_general(normed, d_up, CONTRACT_ROWS, preferred_element_type=jnp.float32)
    d_normed = (lax.dot_general(d_gate, w_gate, CONTRACT_COLS, preferred_element_type=jnp.float32) + lax.dot_general(d_up, w_up, CONTRACT_COLS, preferred_element_type=jnp.float32)).astype(jnp.bfloat16).astype(jnp.float32)
    hidden_f = hidden.astype(jnp.float32)
    d_gain = jnp.sum(d_normed * hidden_f * inv_rms, axis=0)
    scaled = d_normed * gain_row
    d_hidden = cot_out.astype(jnp.float32) + inv_rms * scaled - hidden_f * (inv_rms * inv_rms * inv_rms) * jnp.mean(scaled * hidden_f, axis=-1, keepdims=True)
    return d_hidden.astype(jnp.bfloat16), dw_gate, dw_up, dw_down, d_gain


def solution(mesh):
    tok_spec = P(TOKEN_AXES, None)
    shard_spec = P(None, "fsdp", None)
    full_spec = P(None, None)

    def gather_layer(w_gate_sh, w_up_sh, w_down_sh, layer_idx):
        gate_full = lax.all_gather(w_gate_sh[layer_idx], "fsdp", axis=0, tiled=True)
        up_full = lax.all_gather(w_up_sh[layer_idx], "fsdp", axis=0, tiled=True)
        down_full = lax.all_gather(w_down_sh[layer_idx], "fsdp", axis=0, tiled=True)
        return gate_full, up_full, down_full

    def reduce_grad(grad_local):
        grad_shard = lax.psum_scatter(grad_local, "fsdp", scatter_dimension=0, tiled=True)
        return lax.psum(grad_shard, COPY_AXES)

    def device_step(x_local, dy_local, w_gate_sh, w_up_sh, w_down_sh, norm_gain):
        num_layers = w_gate_sh.shape[0]
        hidden = x_local
        saved_list = []
        for layer_idx in range(num_layers):
            gate_full, up_full, down_full = gather_layer(w_gate_sh, w_up_sh, w_down_sh, layer_idx)
            hidden, saved_vals = layer_forward(hidden, gate_full, up_full, down_full, norm_gain[layer_idx])
            saved_list.append(saved_vals)
        cot_out = dy_local
        grad_map = {}
        for layer_idx in reversed(range(num_layers)):
            gate_full, up_full, down_full = gather_layer(w_gate_sh, w_up_sh, w_down_sh, layer_idx)
            cot_out, dw_gate, dw_up, dw_down, d_gain = layer_backward(cot_out, saved_list[layer_idx], gate_full, up_full, down_full, norm_gain[layer_idx])
            grad_map[layer_idx] = (reduce_grad(dw_gate), reduce_grad(dw_up), reduce_grad(dw_down), d_gain)
        stacked = [jnp.stack([grad_map[layer_idx][part_idx] for layer_idx in range(num_layers)]) for part_idx in range(4)]
        gain_sum = lax.psum(stacked[3], TOKEN_AXES)
        return (hidden, stacked[0], stacked[1], stacked[2], gain_sum)

    return jax.shard_map(device_step, mesh=mesh, in_specs=(tok_spec, tok_spec, shard_spec, shard_spec, shard_spec, full_spec), out_specs=(tok_spec, shard_spec, shard_spec, shard_spec, full_spec), check_vma=False)
```

profile of v0, /device:TPU:1, one launch (start us, length us, event | category | flops | bytes accessed | tf_op | source)
XLA Modules:
  0.0 1787.3 jit_solution(13611314641196788288)
XLA Ops:
  7.2 3.8 fusion.160
  12.9 3.5 fusion.159
  20.7 46.7 %all-gather.19.cloned.1.call-done = bf16[1,1024,4096]{2,1,0:T(8,128)(2,1)} async-done(((bf16[1,128,4096]{2,1,0:T(8,128)(2,1)}), bf16[1,1024,4096]{2,1,0:T(8,128)(2,1)}) %all-gather.19.cloned.1.call-update) | async-done | bytes 8388624 | tf_op jit(solution)/shard_map/all_gather | solution.py:48
  67.4 6.0 fusion.39
  73.4 48.8 %all-gather.21.cloned.1.call-done = bf16[1,1024,4096]{2,1,0:T(8,128)(2,1)} async-done(((bf16[1,128,4096]{2,1,0:T(8,128)(2,1)}), bf16[1,1024,4096]{2,1,0:T(8,128)(2,1)}) %all-gather.21.cloned.1.call-update) | async-done | bytes 8388624 | tf_op jit(solution)/shard_map/all_gather | solution.py:49
  122.2 7.0 multiply_convert_fusion.8
  129.1 47.3 %all-gather.23.cloned.1.call-done = bf16[1,4096,1024]{2,1,0:T(8,128)(2,1)} async-done(((bf16[1,512,1024]{2,1,0:T(8,128)(2,1)}), bf16[1,4096,1024]{2,1,0:T(8,128)(2,1)}) %all-gather.23.cloned.1.call-update) | async-done | bytes 8388624 | tf_op jit(solution)/shard_map/all_gather | solution.py:50
  176.4 4.7 multiply_reduce_fusion.5
  181.2 49.8 %all-gather.25.cloned.1.call-done = bf16[1,1024,4096]{2,1,0:T(8,128)(2,1)} async-done(((bf16[1,128,4096]{2,1,0:T(8,128)(2,1)}), bf16[1,1024,4096]{2,1,0:T(8,128)(2,1)}) %all-gather.25.cloned.1.call-update) | async-done | bytes 8388624 | tf_op jit(solution)/shard_map/all_gather | solution.py:48
  231.0 6.0 fusion.57
  237.0 48.1 %all-gather.27.cloned.1.call-done = bf16[1,1024,4096]{2,1,0:T(8,128)(2,1)} async-done(((bf16[1,128,4096]{2,1,0:T(8,128)(2,1)}), bf16[1,1024,4096]{2,1,0:T(8,128)(2,1)}) %all-gather.27.cloned.1.call-update) | async-done | bytes 8388624 | tf_op jit(solution)/shard_map/all_gather | solution.py:49
  285.1 6.9 multiply_convert_fusion.7
  292.0 47.2 %all-gather.29.cloned.1.call-done = bf16[1,4096,1024]{2,1,0:T(8,128)(2,1)} async-done(((bf16[1,512,1024]{2,1,0:T(8,128)(2,1)}), bf16[1,4096,1024]{2,1,0:T(8,128)(2,1)}) %all-gather.29.cloned.1.call-update) | async-done | bytes 8388624 | tf_op jit(solution)/shard_map/all_gather | solution.py:50
  339.1 4.7 multiply_reduce_fusion.4
  344.0 49.3 %all-gather.33.cloned.1.call-done = bf16[1,1024,4096]{2,1,0:T(8,128)(2,1)} async-done(((bf16[1,128,4096]{2,1,0:T(8,128)(2,1)}), bf16[1,1024,4096]{2,1,0:T(8,128)(2,1)}) %all-gather.33.cloned.1.call-update) | async-done | bytes 8388624 | tf_op jit(solution)/shard_map/all_gather | solution.py:49
  393.3 6.0 fusion.81
  399.3 48.2 %all-gather.31.cloned.1.call-done = bf16[1,1024,4096]{2,1,0:T(8,128)(2,1)} async-done(((bf16[1,128,4096]{2,1,0:T(8,128)(2,1)}), bf16[1,1024,4096]{2,1,0:T(8,128)(2,1)}) %all-gather.31.cloned.1.call-update) | async-done | bytes 8388624 | tf_op jit(solution)/shard_map/all_gather | solution.py:48
  447.6 6.0 fusion.75
  453.5 48.2 %all-gather.35.cloned.1.call-done = bf16[1,4096,1024]{2,1,0:T(8,128)(2,1)} async-done(((bf16[1,512,1024]{2,1,0:T(8,128)(2,1)}), bf16[1,4096,1024]{2,1,0:T(8,128)(2,1)}) %all-gather.35.cloned.1.call-update) | async-done | bytes 8388624 | tf_op jit(solution)/shard_map/all_gather | solution.py:50
  501.8 8.4 multiply_convert_fusion.4
  510.2 7.0 fusion.4
  520.6 7.9 multiply_convert_fusion.2
  536.0 8.1 fusion.167
  544.2 9.4 fusion.168
  554.5 8.8 multiply_convert_fusion
  564.3 8.2 fusion.155
  572.8 9.4 fusion.153
  582.2 9.4 fusion.163
  591.7 9.4 fusion.165
  601.2 8.1 fusion.169
  609.4 9.3 fusion.164
  619.1 9.4 fusion.166
  628.5 9.6 reduce-scatter.22.cloned.1.call-done
  638.1 96.7 %reduce-scatter.24.cloned.1.call-done = f32[512,1024]{1,0:T(8,128)} async-done(((f32[4096,1024]{1,0:T(8,128)}), f32[512,1024]{1,0:T(8,128)}) %reduce-scatter.24.cloned.1.call-update) | async-done | bytes 2097168 | tf_op jit(solution)/shard_map/reduce_scatter | solution.py:54
  734.8 96.6 %reduce-scatter.10.cloned.1.call-done = f32[128,4096]{1,0:T(8,128)} async-done(((f32[1024,4096]{1,0:T(8,128)}), f32[128,4096]{1,0:T(8,128)}) %reduce-scatter.10.cloned.1.call-update) | async-done | bytes 2097168 | tf_op jit(solution)/shard_map/reduce_scatter | solution.py:54
  831.4 96.7 %reduce-scatter.16.cloned.1.call-done = f32[128,4096]{1,0:T(8,128)} async-done(((f32[1024,4096]{1,0:T(8,128)}), f32[128,4096]{1,0:T(8,128)}) %reduce-scatter.16.cloned.1.call-update) | async-done | bytes 2097168 | tf_op jit(solution)/shard_map/reduce_scatter | solution.py:54
  928.1 96.6 %reduce-scatter.12.cloned.1.call-done = f32[128,4096]{1,0:T(8,128)} async-done(((f32[1024,4096]{1,0:T(8,128)}), f32[128,4096]{1,0:T(8,128)}) %reduce-scatter.12.cloned.1.call-update) | async-done | bytes 2097168 | tf_op jit(solution)/shard_map/reduce_scatter | solution.py:54
  1024.7 96.6 %reduce-scatter.18.cloned.1.call-done = f32[128,4096]{1,0:T(8,128)} async-done(((f32[1024,4096]{1,0:T(8,128)}), f32[128,4096]{1,0:T(8,128)}) %reduce-scatter.18.cloned.1.call-update) | async-done | bytes 2097168 | tf_op jit(solution)/shard_map/reduce_scatter | solution.py:54
  1121.2 96.6 %reduce-scatter.26.cloned.1.call-done = f32[512,1024]{1,0:T(8,128)} async-done(((f32[4096,1024]{1,0:T(8,128)}), f32[512,1024]{1,0:T(8,128)}) %reduce-scatter.26.cloned.1.call-update) | async-done | bytes 2097168 | tf_op jit(solution)/shard_map/reduce_scatter | solution.py:54
  1217.8 96.6 %reduce-scatter.14.cloned.1.call-done = f32[128,4096]{1,0:T(8,128)} async-done(((f32[1024,4096]{1,0:T(8,128)}), f32[128,4096]{1,0:T(8,128)}) %reduce-scatter.14.cloned.1.call-update) | async-done | bytes 2097168 | tf_op jit(solution)/shard_map/reduce_scatter | solution.py:54
  1314.4 96.6 %reduce-scatter.20.cloned.1.call-done = f32[128,4096]{1,0:T(8,128)} async-done(((f32[1024,4096]{1,0:T(8,128)}), f32[128,4096]{1,0:T(8,128)}) %reduce-scatter.20.cloned.1.call-update) | async-done | bytes 2097168 | tf_op jit(solution)/shard_map/reduce_scatter | solution.py:54
  1411.0 6.7 fusion.28
  1417.7 6.4 fusion.147
  1424.1 79.9 %psum.79 = f32[3,1024]{1,0:T(4,128)} all-reduce(f32[3,1024]{1,0:T(4,128)S(1)} %pad_maximum_fusion.3), channel_id=1, replica_groups=mesh['dp'=8,'replica'=4,'fsdp'=8] {'dp','replica','fsdp'}, use_global_device_ids=true, to_apply=%region_26.27 | all-reduce | flops 3072 | bytes 24576 | tf_op jit(solution)/shard_map/psum | solution.py:72
  1503.9 5.3 fusion.108
  1509.3 257.1 %all-reduce.3.cloned.1.call-done = (f32[1,128,4096]{2,1,0:T(8,128)}, f32[1,128,4096]{2,1,0:T(8,128)}, f32[1,128,4096]{2,1,0:T(8,128)}, f32[1,128,4096]{2,1,0:T(8...) async-done(((f32[1,128,4096]{2,1,0:T(8,128)}, ...) | async-done | bytes 18874384 | tf_op jit(solution)/shard_map/psum | solution.py:55
  1766.4 7.3 pad_maximum_fusion.2
  1775.2 5.1 pad_maximum_fusion
  (108 shorter events, 21.2 us)
Async XLA Ops:
  7.2 60.2 %all-gather.19.cloned.1.call-start = ((), (), s32[]{:S(2)}) async-start(), calls=%async_computation.18 | async-start | bytes 9437184 | tf_op jit(solution)/shard_map/all_gather | solution.py:48
  7.2 3.8 copy-start.11
  11.0 111.2 %all-gather.21.cloned.1.call-start = ((), (), s32[]{:S(2)}) async-start(), calls=%async_computation.19 | async-start | bytes 9437184 | tf_op jit(solution)/shard_map/all_gather | solution.py:49
  12.9 163.5 %all-gather.23.cloned.1.call-start = ((), (), s32[]{:S(2)}) async-start(), calls=%async_computation.20 | async-start | bytes 9437184 | tf_op jit(solution)/shard_map/all_gather | solution.py:50
  16.5 214.5 %all-gather.25.cloned.1.call-start = ((), (), s32[]{:S(2)}) async-start(), calls=%async_computation.21 | async-start | bytes 9437184 | tf_op jit(solution)/shard_map/all_gather | solution.py:48
  17.1 268.0 %all-gather.27.cloned.1.call-start = ((), (), s32[]{:S(2)}) async-start(), calls=%async_computation.22 | async-start | bytes 9437184 | tf_op jit(solution)/shard_map/all_gather | solution.py:49
  17.6 321.5 %all-gather.29.cloned.1.call-start = ((), (), s32[]{:S(2)}) async-start(), calls=%async_computation.23 | async-start | bytes 9437184 | tf_op jit(solution)/shard_map/all_gather | solution.py:50
  17.7 2.8 copy-start.1
  17.7 3.0 copy-start.21
  18.2 375.1 %all-gather.33.cloned.1.call-start = ((), (), s32[]{:S(2)}) async-start(), calls=%async_computation.25 | async-start | bytes 9437184 | tf_op jit(solution)/shard_map/all_gather | solution.py:49
  19.0 428.6 %all-gather.31.cloned.1.call-start = ((), (), s32[]{:S(2)}) async-start(), calls=%async_computation.24 | async-start | bytes 9437184 | tf_op jit(solution)/shard_map/all_gather | solution.py:48
  19.7 482.0 %all-gather.35.cloned.1.call-start = ((), (), s32[]{:S(2)}) async-start(), calls=%async_computation.26 | async-start | bytes 9437184 | tf_op jit(solution)/shard_map/all_gather | solution.py:50
  20.5 617.6 %reduce-scatter.22.cloned.1.call-start = ((), (), s32[]{:S(2)}) async-start(), calls=%async_computation.15 | async-start | bytes 18874368 | tf_op jit(solution)/shard_map/reduce_scatter | solution.py:54
  129.1 52.0 %copy-start.3 = (bf16[128,4096]{1,0:T(8,128)(2,1)}, bf16[128,4096]{1,0:T(8,128)(2,1)S(1)}, u32[]{:S(2)}) copy-start(bf16[128,4096]{1,0:T(8,128)(2,1)S(1)} %get-tuple-element.41) | copy-start | bytes 3145732
  292.0 51.9 %copy-start.2 = (bf16[128,4096]{1,0:T(8,128)(2,1)}, bf16[128,4096]{1,0:T(8,128)(2,1)S(1)}, u32[]{:S(2)}) copy-start(bf16[128,4096]{1,0:T(8,128)(2,1)S(1)} %get-tuple-element.45) | copy-start | bytes 3145732
  399.3 102.4 %copy-start.18 = (bf16[128,1024]{1,0:T(8,128)(2,1)S(1)}, bf16[128,1024]{1,0:T(8,128)(2,1)}, u32[]{:S(2)}) copy-start(bf16[128,1024]{1,0:T(8,128)(2,1)} %param.7) | copy-start | bytes 786436
  510.2 7.1 copy-start.5
  510.2 7.1 copy-start.6
  510.2 7.1 copy-start
  517.3 14.2 slice-start
  520.3 8.2 slice-start.2
  520.5 8.0 slice-start.3
  520.6 10.9 slice-start.1
  528.5 2.9 copy-start.7
  528.5 2.9 copy-start.8
  534.7 1.3 copy-start.4
  534.9 0.7 copy-start.19
  544.2 190.7 %reduce-scatter.24.cloned.1.call-start = ((), (), s32[]{:S(2)}) async-start(), calls=%async_computation.16 | async-start | bytes 18874368 | tf_op jit(solution)/shard_map/reduce_scatter | solution.py:54
  553.6 1.0 copy-start.20
  553.6 277.8 %reduce-scatter.10.cloned.1.call-start = ((), (), s32[]{:S(2)}) async-start(), calls=%async_computation.9 | async-start | bytes 18874368 | tf_op jit(solution)/shard_map/reduce_scatter | solution.py:54
  563.3 1.0 copy-start.9
  572.5 355.6 %reduce-scatter.16.cloned.1.call-start = ((), (), s32[]{:S(2)}) async-start(), calls=%async_computation.12 | async-start | bytes 18874368 | tf_op jit(solution)/shard_map/reduce_scatter | solution.py:54
  582.2 442.5 %reduce-scatter.12.cloned.1.call-start = ((), (), s32[]{:S(2)}) async-start(), calls=%async_computation.10 | async-start | bytes 18874368 | tf_op jit(solution)/shard_map/reduce_scatter | solution.py:54
  591.7 529.5 %reduce-scatter.18.cloned.1.call-start = ((), (), s32[]{:S(2)}) async-start(), calls=%async_computation.13 | async-start | bytes 18874368 | tf_op jit(solution)/shard_map/reduce_scatter | solution.py:54
  601.2 616.6 %reduce-scatter.26.cloned.1.call-start = ((), (), s32[]{:S(2)}) async-start(), calls=%async_computation.17 | async-start | bytes 18874368 | tf_op jit(solution)/shard_map/reduce_scatter | solution.py:54
  609.4 705.0 %reduce-scatter.14.cloned.1.call-start = ((), (), s32[]{:S(2)}) async-start(), calls=%async_computation.11 | async-start | bytes 18874368 | tf_op jit(solution)/shard_map/reduce_scatter | solution.py:54
  618.8 792.2 %reduce-scatter.20.cloned.1.call-start = ((), (), s32[]{:S(2)}) async-start(), calls=%async_computation.14 | async-start | bytes 18874368 | tf_op jit(solution)/shard_map/reduce_scatter | solution.py:54
  628.4 1138.0 %all-reduce.3.cloned.1.call-start = ((), (), s32[]{:S(2)}) async-start(), calls=%async_computation.27 | async-start | bytes 37748736 | tf_op jit(solution)/shard_map/psum | solution.py:55
  1411.0 6.7 copy-start.10
  1766.4 7.4 copy-start.12
  1766.4 7.4 copy-start.13
  1766.4 7.4 copy-start.14
  1766.4 7.4 copy-start.15
  1766.4 7.8 copy-start.16
  1766.4 8.8 copy-start.17
Sparse Core Ops, SparseCore 0:
  11.1 56.2 all-gather.18
  69.8 52.3 all-gather.20
  124.0 52.3 all-gather.22
  178.7 52.3 all-gather.24
  232.7 52.3 all-gather.26
  286.8 52.3 all-gather.28
  341.0 52.3 all-gather.32
  395.2 52.3 all-gather.30
  449.4 52.3 all-gather.34
  544.3 93.7 reduce-scatter.21
  640.7 94.0 reduce-scatter.23
  737.3 94.0 reduce-scatter.9
  834.0 94.0 reduce-scatter.15
  930.6 94.0 reduce-scatter.11
  1027.1 94.0 reduce-scatter.17
  1123.7 94.0 reduce-scatter.25
  1220.3 94.0 reduce-scatter.13
  1316.8 94.0 reduce-scatter.19
  1417.0 349.3 all-reduce.2
where the time goes:
time: 1800 us; the launch traced here: 1790 us
  waiting for transfers between devices  1480 us (82%)
  matrix products  188 us (10%)
  blocking collectives  79.9 us (4%)
    reduce_scatter x9, waiting for transfers between devices, reduce_grad(): lax.psum_scatter(grad_local, 'fsdp', scatter_dimension=0, tiled=True)  782 us
    psum x1, waiting for transfers between devices, reduce_grad(): return lax.psum(grad_shard, COPY_AXES)  257 us
    all_gather x3, waiting for transfers between devices, gather_layer(): up_full = lax.all_gather(w_up_sh[layer_idx], 'fsdp', axis=0, tiled=True)  146 us
    all_gather x3, waiting for transfers between devices, gather_layer(): gate_full = lax.all_gather(w_gate_sh[layer_idx], 'fsdp', axis=0, tiled=True)  145 us
    all_gather x3, waiting for transfers between devices, gather_layer(): down_full = lax.all_gather(w_down_sh[layer_idx], 'fsdp', axis=0, tiled=True)  143 us
    psum x1, blocking collectives, device_step(): gain_sum = lax.psum(stacked[3], TOKEN_AXES)  79.9 us
  transfers between devices with their start and end apart: 19, of which 19 were waited for; matrix products, arithmetic and copies ran while one was open for 9% of the time, Pallas kernels for 0%

commit v1 on v0

v1 whole, which is shorter than its diff:
```python
import functools
import jax
import jax.numpy as jnp
from jax import lax
from jax.sharding import PartitionSpec as P
from jax.experimental import pallas as pl
from jax.experimental.pallas import tpu as pltpu

F32 = jnp.float32
BF16 = jnp.bfloat16
MESH = pl.DeviceIdType.MESH
RS = 16
LN = 128


def wrap(value, size):
    return lax.rem(value + 4 * size, size)


def split_units(units):
    a = (units * 7 + 12) // 24
    b = (units - 2 * a) // 2
    sizes = (a, a, b, units - 2 * a - b)
    starts = (0, a, 2 * a, 2 * a + b)
    return tuple(zip(starts, sizes))


class Hop:
    def __init__(self, axis, size, pos, sign, chunk, stage, send, recv, base, layers):
        self.axis, self.size, self.pos, self.sign = axis, size, pos, sign
        self.chunk, self.stage, self.send_sem, self.recv_sem = chunk, stage, send, recv
        self.base, self.layers = base, layers

    def copy(self, step, layer, index, dst):
        slot = self.base + step * self.layers + layer
        return pltpu.make_async_remote_copy(
            src_ref=self.chunk(layer, index), dst_ref=dst,
            send_sem=self.send_sem.at[slot], recv_sem=self.recv_sem.at[slot],
            device_id={self.axis: wrap(self.pos + self.sign, self.size)}, device_id_type=MESH)

    def rs_copy(self, step, layer):
        return self.copy(step, layer, wrap(self.pos - self.sign * (step + 1), self.size), self.stage(step, layer))

    def rs_add(self, step, layer):
        self.rs_copy(step, layer).wait_recv()
        dst = self.chunk(layer, wrap(self.pos - self.sign * (step + 2), self.size))
        src = self.stage(step, layer)
        if len(dst.shape) == 4:
            def body(i, carry):
                dst[i] += src[i]
                return carry
            lax.fori_loop(0, dst.shape[0], body, 0)
        else:
            dst[...] += src[...]

    def ag_copy(self, step, layer):
        index = wrap(self.pos - self.sign * step, self.size)
        return self.copy(step, layer, index, self.chunk(layer, index))

    def ag_wait(self, step, layer):
        index = wrap(self.pos - self.sign * (step + 1), self.size)
        self.copy(step, layer, index, self.chunk(layer, index)).wait_recv()
        return self.chunk(layer, index)


def ar_kernel(dims, *refs):
    layers, ny, nz, nf = dims
    units = 3 * nf
    grads = refs[:3 * layers]
    gain_ref = refs[3 * layers]
    out_ref, gain_out = refs[3 * layers + 1:3 * layers + 3]
    (G, st_ay, st_bz, st_az, st_by, R, gain_buf, rs_send, rs_recv, ag_send, ag_recv,
     x_send, x_recv, g_send, g_recv, in_sem, out_sem, ready) = refs[3 * layers + 3:]
    y, z, f = lax.axis_index("replica"), lax.axis_index("dp"), lax.axis_index("fsdp")

    barrier = pltpu.get_barrier_semaphore()
    peers = [("fsdp", f, nf), ("replica", y, ny), ("dp", z, nz)]
    count = 0
    for axis, pos, size in peers:
        for j in range(1, size):
            pl.semaphore_signal(barrier, inc=1, device_id={axis: wrap(pos + j, size)}, device_id_type=MESH)
            count += 1

    def load(i, carry):
        yy, zz = i // nz, i % nz
        for layer in range(layers):
            for m in range(2):
                src = grads[3 * layer + m].at[:, zz, :, pl.ds(pl.multiple_of(yy * LN, LN), LN)]
                pltpu.make_async_copy(src, G.at[layer, yy, zz, pl.ds(m * nf, nf)], in_sem).start()
            for h in range(2):
                src = grads[3 * layer + 2].at[zz, :, :, pl.ds(pl.multiple_of((2 * yy + h) * LN, LN), LN)]
                pltpu.make_async_copy(src, G.at[layer, yy, zz, pl.ds(2 * nf + h * (nf // 2), nf // 2)], in_sem).start()
        return carry
    lax.fori_loop(0, ny * nz, load, 0)
    pl.semaphore_wait(barrier, count)
    pltpu.make_async_copy(out_ref, G, in_sem).wait()

    streams = split_units(units)
    hops, base = [], 0
    for phase in range(2):
        row = []
        for k, (start, size) in enumerate(streams):
            sign = 1 if k % 2 == 0 else -1
            first_y = k < 2
            along_y = first_y == (phase == 0)
            sub = pl.ds(start, size)
            if along_y:
                chunk = (lambda sub: lambda layer, i: G.at[layer, i, :, sub])(sub) if phase == 0 else (lambda sub: lambda layer, i: G.at[layer, i, z, sub])(sub)
            else:
                chunk = (lambda sub: lambda layer, i: G.at[layer, :, i, sub])(sub) if phase == 0 else (lambda sub: lambda layer, i: G.at[layer, y, i, sub])(sub)
            buf = ((st_ay, st_bz) if phase == 0 else (st_az, st_by))[0 if first_y else 1]
            stage = (lambda buf, d, size: lambda step, layer: buf.at[d, step, layer, :, pl.ds(0, size)] if len(buf.shape) == 7 else buf.at[d, step, layer, pl.ds(0, size)])(buf, k % 2, size)
            axis, n, pos = ("replica", ny, y) if along_y else ("dp", nz, z)
            row.append(Hop(axis, n, pos, sign, chunk, stage, rs_send, rs_recv, base, layers))
            base += (n - 1) * layers
        hops.append(row)

    def gain_copy(stage, axis, pos, size, j):
        return pltpu.make_async_remote_copy(
            src_ref=gain_buf.at[stage, pos], dst_ref=gain_buf.at[stage, pos],
            send_sem=g_send.at[stage, j], recv_sem=g_recv.at[stage, pos],
            device_id={axis: wrap(pos + j, size)}, device_id_type=MESH)

    def gain_send(stage, value):
        axis, pos, size = peers[stage]
        gain_buf[stage, pos] = value
        for j in range(1, size):
            gain_copy(stage, axis, pos, size, j).start()

    def gain_sum(stage):
        axis, pos, size = peers[stage]
        for j in range(1, size):
            other = wrap(pos + j, size)
            pltpu.make_async_remote_copy(
                src_ref=gain_buf.at[stage, other], dst_ref=gain_buf.at[stage, other],
                send_sem=g_send.at[stage, j], recv_sem=g_recv.at[stage, other],
                device_id={axis: other}, device_id_type=MESH).wait_recv()
        total = gain_buf[stage, 0]
        for i in range(1, size):
            total = total + gain_buf[stage, i]
        return total

    gain_send(0, gain_ref[...])

    def steps(rows, link_us, reduce):
        events = []
        for k, hop in enumerate(rows):
            for step in range(hop.size - 1):
                for layer in range(layers):
                    events.append(((step * layers + layer + 1) * link_us[k], k, step, layer))
        return sorted(events)

    big = [1.4 * ny * 0 + streams[k][1] * (nz if k < 2 else ny) for k in range(4)]
    small = [max(streams[k][1], 8) for k in range(4)]

    for hop in hops[0]:
        for layer in range(layers):
            hop.rs_copy(0, layer).start()
    for phase in range(2):
        order = steps(hops[phase], big if phase == 0 else small, True)
        for n, (_, k, step, layer) in enumerate(order):
            hop = hops[phase][k]
            hop.rs_add(step, layer)
            if step + 1 < hop.size - 1:
                hop.rs_copy(step + 1, layer).start()
            elif phase == 0:
                hops[1][k].rs_copy(0, layer).start()
            if phase == 0 and n == len(order) // 3:
                gain_send(1, gain_sum(0))
            if phase == 0 and n == 2 * len(order) // 3:
                gain_send(2, gain_sum(1))

    def x_copy(m, j, peer, sender):
        return pltpu.make_async_remote_copy(
            src_ref=G.at[:, y, z, m * nf + peer], dst_ref=R.at[:, m * nf + sender],
            send_sem=x_send.at[m, j], recv_sem=x_recv.at[m, sender],
            device_id={"fsdp": peer}, device_id_type=MESH)

    for j in range(1, nf):
        for m in range(2):
            x_copy(m, j, wrap(f + j, nf), f).start()
    for m in range(2):
        R[:, m * nf + f] = G[:, y, z, m * nf + f]
    gain_out[...] = gain_sum(2)
    for phase in range(2):
        for hop in hops[phase]:
            for step in range(hop.size - 1):
                for layer in range(layers):
                    hop.rs_copy(step, layer).wait_send()
    for axis, pos, size in peers[1:]:
        for sign in (1, -1):
            pl.semaphore_signal(ready, inc=1, device_id={axis: wrap(pos + sign, size)}, device_id_type=MESH)
    for j in range(1, nf):
        for m in range(2):
            x_copy(m, j, wrap(f + j, nf), f).wait_send()
            x_copy(m, j, wrap(f + j, nf), wrap(f + j, nf)).wait_recv()
    G[:, y, z, pl.ds(0, 2 * nf)] = R[...]
    pl.semaphore_wait(ready, 4)

    for row in hops:
        for hop in row:
            hop.send_sem, hop.recv_sem = ag_send, ag_recv

    pltpu.make_async_copy(G.at[:, y, z], out_ref.at[:, y, z], out_sem).start()

    def emit(hop, step, layer, k, phase):
        index = wrap(hop.pos - hop.sign * (step + 1), hop.size)
        sub = pl.ds(*streams[k])
        if phase == 0:
            dst = out_ref.at[layer, index, :, sub] if k < 2 else out_ref.at[layer, :, index, sub]
        else:
            dst = out_ref.at[layer, y, index, sub] if k < 2 else out_ref.at[layer, index, z, sub]
        pltpu.make_async_copy(hop.chunk(layer, index), dst, out_sem).start()

    for hop in hops[1]:
        for layer in range(layers):
            hop.ag_copy(0, layer).start()
    for phase in (1, 0):
        order = steps(hops[phase], big if phase == 0 else small, False)
        for _, k, step, layer in order:
            hop = hops[phase][k]
            hop.ag_wait(step, layer)
            if step + 1 < hop.size - 1:
                hop.ag_copy(step + 1, layer).start()
            elif phase == 1:
                hops[0][k].ag_copy(0, layer).start()
            emit(hop, step, layer, k, phase)
    for phase in range(2):
        for hop in hops[phase]:
            for step in range(hop.size - 1):
                for layer in range(layers):
                    hop.ag_copy(step, layer).wait_send()
    for stage, (axis, pos, size) in enumerate(peers):
        for j in range(1, size):
            gain_copy(stage, axis, pos, size, j).wait_send()
    pltpu.make_async_copy(G, out_ref, out_sem).wait()


def all_reduce(grads, gain, dims):
    layers, ny, nz, nf = dims
    units = 3 * nf
    streams = split_units(units)
    a, b = streams[0][1], max(streams[2][1], streams[3][1])
    copies = layers * 2 * 2 * ((ny - 1) + (nz - 1))
    views = []
    for i, g in enumerate(grads):
        if i % 3 < 2:
            views.append(g.reshape(nf, nz, RS, ny * LN))
        else:
            views.append(g.reshape(nz, nf // 2, RS, 2 * ny * LN))
    gr = gain.reshape(-1, LN)
    out, gain_out = pl.pallas_call(
        functools.partial(ar_kernel, dims),
        out_shape=(jax.ShapeDtypeStruct((layers, ny, nz, units, RS, LN), F32), jax.ShapeDtypeStruct(gr.shape, F32)),
        in_specs=[pl.BlockSpec(memory_space=pl.ANY)] * len(views) + [pl.BlockSpec(memory_space=pltpu.VMEM)],
        out_specs=(pl.BlockSpec(memory_space=pl.ANY), pl.BlockSpec(memory_space=pltpu.VMEM)),
        scratch_shapes=[
            pltpu.VMEM((layers, ny, nz, units, RS, LN), F32),
            pltpu.VMEM((2, ny - 1, layers, nz, a, RS, LN), F32),
            pltpu.VMEM((2, nz - 1, layers, ny, b, RS, LN), F32),
            pltpu.VMEM((2, nz - 1, layers, a, RS, LN), F32),
            pltpu.VMEM((2, ny - 1, layers, b, RS, LN), F32),
            pltpu.VMEM((layers, 2 * nf, RS, LN), F32),
            pltpu.VMEM((3, max(nf, ny, nz)) + gr.shape, F32),
            pltpu.SemaphoreType.DMA((copies,)), pltpu.SemaphoreType.DMA((copies,)),
            pltpu.SemaphoreType.DMA((copies,)), pltpu.SemaphoreType.DMA((copies,)),
            pltpu.SemaphoreType.DMA((2, nf)), pltpu.SemaphoreType.DMA((2, nf)),
            pltpu.SemaphoreType.DMA((3, max(nf, ny, nz))), pltpu.SemaphoreType.DMA((3, max(nf, ny, nz))),
            pltpu.SemaphoreType.DMA, pltpu.SemaphoreType.DMA, pltpu.SemaphoreType.REGULAR,
        ],
        compiler_params=pltpu.CompilerParams(collective_id=0, has_side_effects=True, vmem_limit_bytes=52 * 2**20),
        name="grad_all_reduce",
    )(*views, gr)
    return out, gain_out


def unpack_kernel(g_ref, o_ref):
    ny, nf = g_ref.shape[0], g_ref.shape[1]
    for j in range(nf):
        for i in range(ny):
            o_ref[:, (j * ny + i) * LN:(j * ny + i + 1) * LN] = g_ref[i, j]


def unpack_down_kernel(g_ref, o_ref):
    ny, nf = g_ref.shape[0], g_ref.shape[1]
    for i in range(ny):
        for h in range(2):
            for r in range(nf // 2):
                o_ref[r * RS:(r + 1) * RS, (2 * i + h) * LN:(2 * i + h + 1) * LN] = g_ref[i, h * (nf // 2) + r]


def unpack(out, dims):
    layers, ny, nz, nf = dims
    res = []
    for m in range(3):
        spec_in = pl.BlockSpec((None, ny, None, nf, RS, LN), functools.partial(lambda m, l, z: (l, 0, z, m, 0, 0), m))
        if m < 2:
            shape, block, body = (layers, nz * RS, nf * ny * LN), (None, RS, nf * ny * LN), unpack_kernel
        else:
            shape, block, body = (layers, nz * (nf // 2) * RS, 2 * ny * LN), (None, (nf // 2) * RS, 2 * ny * LN), unpack_down_kernel
        res.append(pl.pallas_call(
            body, grid=(layers, nz), in_specs=[spec_in],
            out_specs=pl.BlockSpec(block, lambda l, z: (l, z, 0)),
            out_shape=jax.ShapeDtypeStruct(shape, F32), name="unpack_%d" % m)(out))
    return res


NORM_EPS = 1e-6
TOKEN_AXES = ("dp", "replica", "fsdp")
CONTRACT_ROWS = (((0,), (0,)), ((), ()))
CONTRACT_COLS = (((1,), (1,)), ((), ()))


def dot(a, b, dims=(((1,), (0,)), ((), ()))):
    return lax.dot_general(a, b, dims, preferred_element_type=F32)


def solution(mesh):
    shards = mesh.shape["fsdp"]
    tok_spec = P(TOKEN_AXES, None)
    shard_spec = P(None, "fsdp", None)
    full_spec = P(None, None)

    def to_columns(w_rows):
        layers, rows, cols = w_rows.shape
        split = w_rows.reshape(layers, rows, shards, cols // shards)
        moved = lax.all_to_all(split, "fsdp", split_axis=2, concat_axis=1, tiled=True)
        return moved.reshape(layers, rows * shards, cols // shards)

    def device_step(x_local, dy_local, w_gate_sh, w_up_sh, w_down_sh, norm_gain):
        layers = w_gate_sh.shape[0]
        both = to_columns(jnp.concatenate([w_gate_sh, w_up_sh], axis=0))
        w_gate, w_up, w_down = both[:layers], both[layers:], w_down_sh
        hidden = x_local
        saved = []
        for layer in range(layers):
            hidden_f = hidden.astype(F32)
            inv_rms = lax.rsqrt(jnp.mean(hidden_f * hidden_f, axis=-1, keepdims=True) + NORM_EPS)
            normed = (hidden_f * inv_rms * norm_gain[layer]).astype(BF16)
            normed = lax.all_gather(normed, "fsdp", axis=0, tiled=True)
            gate = dot(normed, w_gate[layer]).astype(BF16)
            up = dot(normed, w_up[layer]).astype(BF16)
            prod = (jax.nn.silu(gate.astype(F32)) * up.astype(F32)).astype(BF16)
            out = lax.psum_scatter(dot(prod, w_down[layer]), "fsdp", scatter_dimension=0, tiled=True)
            saved.append((hidden_f, inv_rms, normed, gate, up, prod))
            hidden = (hidden_f + out).astype(BF16)
        cot = dy_local
        grads = [None] * layers
        for layer in reversed(range(layers)):
            hidden_f, inv_rms, normed, gate, up, prod = saved[layer]
            cot_all = lax.all_gather(cot, "fsdp", axis=0, tiled=True)
            d_prod = dot(cot_all, w_down[layer], CONTRACT_COLS).astype(BF16).astype(F32)
            gate_f = gate.astype(F32)
            sig = jax.nn.sigmoid(gate_f)
            d_gate = (d_prod * up.astype(F32) * sig * (1.0 + gate_f * (1.0 - sig))).astype(BF16)
            d_up = (d_prod * gate_f * sig).astype(BF16)
            part = dot(d_gate, w_gate[layer], CONTRACT_COLS) + dot(d_up, w_up[layer], CONTRACT_COLS)
            d_normed = lax.psum_scatter(part, "fsdp", scatter_dimension=0, tiled=True).astype(BF16).astype(F32)
            d_gain = jnp.sum(d_normed * hidden_f * inv_rms, axis=0)
            scaled = d_normed * norm_gain[layer]
            d_hidden = cot.astype(F32) + inv_rms * scaled - hidden_f * (inv_rms * inv_rms * inv_rms) * jnp.mean(scaled * hidden_f, axis=-1, keepdims=True)
            cot = d_hidden.astype(BF16)
            grads[layer] = (
                dot(normed, d_gate, CONTRACT_ROWS),
                dot(normed, d_up, CONTRACT_ROWS),
                dot(prod, cot_all, CONTRACT_ROWS),
                d_gain,
            )
        flat = [grads[layer][part] for layer in range(layers) for part in range(3)]
        gain = jnp.stack([grads[layer][3] for layer in range(layers)])
        dims = (layers, mesh.shape["replica"], mesh.shape["dp"], shards)
        blocks, gain_sum = all_reduce(flat, gain, dims)
        dw_gate, dw_up, dw_down = unpack(blocks, dims)
        return (hidden, dw_gate, dw_up, dw_down, gain_sum.reshape(gain.shape))

    return jax.shard_map(device_step, mesh=mesh, in_specs=(tok_spec, tok_spec, shard_spec, shard_spec, shard_spec, full_spec), out_specs=(tok_spec, shard_spec, shard_spec, shard_spec, full_spec), check_vma=False)
```

time: 1800 us -> 895 us (0.50)
  waiting for transfers between devices: 1480 us -> 423 us
  Pallas kernels: 0 us -> 307 us
  matrix products: 188 us -> 83.1 us
  blocking collectives: 79.9 us -> 0 us
    reduce_scatter x9 -> x6, waiting for transfers between devices: 782 us -> 198 us  [the longest x3 116 us: device_step(): lax.psum_scatter(dot(prod, w_down[layer]), 'fsdp', scatter_dimension=0, t...]
    pallas_call x0 -> x4, Pallas kernels: none -> 307 us  [the longest x1 263 us: all_reduce(): pl.pallas_call(functools.partial(ar_kernel, dims), out_shape=(jax.ShapeDt...]
    all_gather x9 -> x6, waiting for transfers between devices: 434 us -> 146 us  [the longest x3 89.1 us: device_step(): cot_all = lax.all_gather(cot, 'fsdp', axis=0, tiled=True)]
    psum x1 -> x0, waiting for transfers between devices: 257 us -> none  [reduce_grad(): return lax.psum(grad_shard, COPY_AXES)]
    dot_general x27, matrix products: 188 us -> 83.1 us  [dot(): return lax.dot_general(a, b, dims, preferred_element_type=F32)]
    psum x1 -> x0, blocking collectives: 79.9 us -> none  [device_step(): gain_sum = lax.psum(stacked[3], TOKEN_AXES)]
    all_to_all x0 -> x1, waiting for transfers between devices: none -> 78.4 us  [to_columns(): lax.all_to_all(split, 'fsdp', split_axis=2, concat_axis=1, tiled=True)]
  transfers between devices with their start and end apart: 19 -> 13, of which waited for: 19 -> 12; matrix products, arithmetic and copies ran while one was open for 9% -> 6% of each run, Pallas kernels for 0% -> 0%
where the time goes in v1:
time: 895 us; the launch traced here: 882 us
  waiting for transfers between devices  423 us (47%)
  Pallas kernels  307 us (34%)
  matrix products  83.1 us (9%)
  local copies, waits for them, and re-layouts  30.7 us (3%)
  other arithmetic  15.4 us (2%)
  between operations  15.1 us (2%)
    pallas_call x1, Pallas kernels, all_reduce(): pl.pallas_call(functools.partial(ar_kernel, dims), out_shape=(jax.ShapeDt...  263 us
    reduce_scatter x3, waiting for transfers between devices, device_step(): lax.psum_scatter(dot(prod, w_down[layer]), 'fsdp', scatter_dimension=0, t...  116 us
    all_gather x3, waiting for transfers between devices, device_step(): cot_all = lax.all_gather(cot, 'fsdp', axis=0, tiled=True)  89.1 us
    dot_general x27, matrix products, dot(): return lax.dot_general(a, b, dims, preferred_element_type=F32)  83.1 us
    reduce_scatter x3, waiting for transfers between devices, device_step(): lax.psum_scatter(part, 'fsdp', scatter_dimension=0, tiled=True).astype(BF16)  81.6 us
    all_to_all x1, waiting for transfers between devices, to_columns(): lax.all_to_all(split, 'fsdp', split_axis=2, concat_axis=1, tiled=True)  78.4 us
    all_gather x3, waiting for transfers between devices, device_step(): normed = lax.all_gather(normed, 'fsdp', axis=0, tiled=True)  56.7 us
    pallas_call x3, Pallas kernels, unpack(): pl.pallas_call(body, grid=(layers, nz), in_specs=[spec_in], out_specs=pl....  44 us
  transfers between devices with their start and end apart: 13, of which 12 were waited for; matrix products, arithmetic and copies ran while one was open for 6% of the time, Pallas kernels for 0%

profile of v1, /device:TPU:1, one launch (start us, length us, event | category | flops | bytes accessed | tf_op | source)
XLA Modules:
  0.0 882.4 jit_solution(7384096000407300903)
XLA Ops:
  7.2 3.5 copy.19
  10.7 4.6 copy.20
  15.3 2.4 pad_maximum_fusion
  17.7 3.4 copy.21
  21.1 7.9 all-to-all-start
  30.2 78.4 %all-to-all-done = bf16[6,128,8,512]{1,3,0,2:T(8,128)(2,1)} async-done(((bf16[6,128,8,512]{1,3,0,2:T(8,128)(2,1)}), bf16[6,128,8,512]{1,3,0,2:T(8,128)(2,1)}, u32[]{:S(2)}, u32[]{:S(2)}) %all-to-all-start) | async-done | bytes 6291488 | tf_op jit(solution)/shard_map/all_to_all | solution.py:327
  108.6 8.6 copy.22
  117.2 5.1 fusion.95
  122.3 3.0 convolution_convert_fusion.8
  127.6 4.6 fusion.37
  132.3 37.7 %reduce-scatter.7.cloned.1.call-done = f32[128,1024]{1,0:T(8,128)} async-done(((f32[1024,1024]{1,0:T(8,128)}), f32[128,1024]{1,0:T(8,128)}) %reduce-scatter.7.cloned.1.call-update) | async-done | bytes 524304 | tf_op jit(solution)/shard_map/reduce_scatter | solution.py:344
  172.1 30.2 %all-gather.9.cloned.1.call-done = bf16[1024,1024]{1,0:T(8,128)(2,1)} async-done(((bf16[128,1024]{1,0:T(8,128)(2,1)}), bf16[1024,1024]{1,0:T(8,128)(2,1)}) %all-gather.9.cloned.1.call-update) | async-done | bytes 2097168 | tf_op jit(solution)/shard_map/all_gather | solution.py:340
  202.4 3.2 convolution_convert_fusion.6
  207.9 4.6 fusion.34
  213.2 37.2 %reduce-scatter.9.cloned.1.call-done = f32[128,1024]{1,0:T(8,128)} async-done(((f32[1024,1024]{1,0:T(8,128)}), f32[128,1024]{1,0:T(8,128)}) %reduce-scatter.9.cloned.1.call-update) | async-done | bytes 524304 | tf_op jit(solution)/shard_map/reduce_scatter | solution.py:344
  252.8 29.4 %all-gather.13.cloned.1.call-done = bf16[1024,1024]{1,0:T(8,128)(2,1)} async-done(((bf16[128,1024]{1,0:T(8,128)(2,1)}), bf16[1024,1024]{1,0:T(8,128)(2,1)}) %all-gather.13.cloned.1.call-update) | async-done | bytes 2097168 | tf_op jit(solution)/shard_map/all_gather | solution.py:351
  282.2 4.1 convolution_convert_fusion.2
  286.3 26.4 %all-gather.11.cloned.1.call-done = bf16[1024,1024]{1,0:T(8,128)(2,1)} async-done(((bf16[128,1024]{1,0:T(8,128)(2,1)}), bf16[1024,1024]{1,0:T(8,128)(2,1)}) %all-gather.11.cloned.1.call-update) | async-done | bytes 2097168 | tf_op jit(solution)/shard_map/all_gather | solution.py:340
  312.8 3.2 convolution_convert_fusion.4
  316.1 2.8 fusion.5
  321.2 3.4 convolution_add_fusion.2
  324.7 5.3 fusion.31
  330.0 32.6 %reduce-scatter.13.cloned.1.call-done = f32[128,1024]{1,0:T(8,128)} async-done(((f32[1024,1024]{1,0:T(8,128)}), f32[128,1024]{1,0:T(8,128)}) %reduce-scatter.13.cloned.1.call-update) | async-done | bytes 524304 | tf_op jit(solution)/shard_map/reduce_scatter | solution.py:358
  363.8 41.3 %reduce-scatter.11.cloned.1.call-done = f32[128,1024]{1,0:T(8,128)} async-done(((f32[1024,1024]{1,0:T(8,128)}), f32[128,1024]{1,0:T(8,128)}) %reduce-scatter.11.cloned.1.call-update) | async-done | bytes 524304 | tf_op jit(solution)/shard_map/reduce_scatter | solution.py:344
  405.1 2.3 fusion.52
  407.5 30.0 %all-gather.15.cloned.1.call-done = bf16[1024,1024]{1,0:T(8,128)(2,1)} async-done(((bf16[128,1024]{1,0:T(8,128)(2,1)}), bf16[1024,1024]{1,0:T(8,128)(2,1)}) %all-gather.15.cloned.1.call-update) | async-done | bytes 2097168 | tf_op jit(solution)/shard_map/all_gather | solution.py:351
  437.5 4.5 fusion.8
  444.3 3.4 convolution_add_fusion.1
  447.8 37.9 %reduce-scatter.15.cloned.1.call-done = f32[128,1024]{1,0:T(8,128)} async-done(((f32[1024,1024]{1,0:T(8,128)}), f32[128,1024]{1,0:T(8,128)}) %reduce-scatter.15.cloned.1.call-update) | async-done | bytes 524304 | tf_op jit(solution)/shard_map/reduce_scatter | solution.py:358
  486.9 2.0 fusion.49
  489.2 29.7 %all-gather.17.cloned.1.call-done = bf16[1024,1024]{1,0:T(8,128)(2,1)} async-done(((bf16[128,1024]{1,0:T(8,128)(2,1)}), bf16[1024,1024]{1,0:T(8,128)(2,1)}) %all-gather.17.cloned.1.call-update) | async-done | bytes 2097168 | tf_op jit(solution)/shard_map/all_gather | solution.py:351
  518.9 4.4 fusion.11
  523.3 1.3 fusion.102
  525.3 3.4 convolution_add_fusion
  528.8 4.6 fusion.101
  533.5 2.8 fusion.84
  536.3 2.8 fusion.75
  539.1 2.6 fusion.100
  541.7 2.8 fusion.87
  544.5 2.7 fusion.78
  547.2 2.9 fusion.99
  550.1 2.7 fusion.90
  552.9 2.7 fusion.82
  555.6 11.1 %reduce-scatter.17.cloned.1.call-done = f32[128,1024]{1,0:T(8,128)} async-done(((f32[1024,1024]{1,0:T(8,128)}), f32[128,1024]{1,0:T(8,128)}) %reduce-scatter.17.cloned.1.call-update) | async-done | bytes 524304 | tf_op jit(solution)/shard_map/reduce_scatter | solution.py:358
  567.9 262.6 %grad_all_reduce.1 = (f32[3,4,8,24,16,128]{5,4,3,2,1,0:T(8,128)}, f32[24,128]{1,0:T(8,128)S(1)}) custom-call(f32[8,8,16,512]{3,2,1,0:T(8,128)} %bitcast.88, f32[8,8,16,512]{3,2,1,0:T(8,128)} %bitcast.90, f32[8,4,16,1024]{3,2,1,0:T(8,128)} %bitcast.89, f32[8,8,16,512]{3,2,1,0:T(8,128)} %bitcast.85, f32[8,8,16,512]{3,2,1,0:T(8,128)} %bitcast.87, ...), custom_call_target="tpu_custom_call" | custom-call | tf_op jit(solution)/shard_map/grad_all_reduce/pallas_call | solution.py:252
  830.5 14.7 %unpack_2.1 = f32[3,512,1024]{2,1,0:T(8,128)} custom-call(f32[3,4,8,24,16,128]{5,4,3,2,1,0:T(8,128)} %get-tuple-element.7.g_ref), custom_call_target="tpu_custom_call" | custom-call | tf_op jit(solution)/shard_map/unpack_2/pallas_call | solution.py:301
  845.2 14.7 %unpack_1.1 = f32[3,128,4096]{2,1,0:T(8,128)} custom-call(f32[3,4,8,24,16,128]{5,4,3,2,1,0:T(8,128)} %get-tuple-element.7.g_ref), custom_call_target="tpu_custom_call" | custom-call | tf_op jit(solution)/shard_map/unpack_1/pallas_call | solution.py:301
  859.9 14.7 %unpack_0.1 = f32[3,128,4096]{2,1,0:T(8,128)} custom-call(f32[3,4,8,24,16,128]{5,4,3,2,1,0:T(8,128)} %get-tuple-element.7.g_ref), custom_call_target="tpu_custom_call" | custom-call | tf_op jit(solution)/shard_map/unpack_0/pallas_call | solution.py:301
  (131 shorter events, 20.7 us)
Async XLA Ops:
  21.1 7.9 copy-start
  21.1 8.1 copy-start.8
  21.1 87.4 %all-to-all-start = ((bf16[6,128,8,512]{1,3,0,2:T(8,128)(2,1)}), bf16[6,128,8,512]{1,3,0,2:T(8,128)(2,1)}, u32[]{:S(2)}, u32[]{:S(2)}) async-start(bf16[6,128,8,512]{1,3,0,2:T(8,128)(2,1)} %copy.21), calls=%async_computation | async-start | bytes 12582912 | tf_op jit(solution)/shard_map/all_to_all | solution.py:327
  29.1 93.3 %all-gather.7.cloned.1.call-start = ((), (), s32[]{:S(2)}) async-start(), calls=%async_computation.7 | async-start | bytes 2359296 | tf_op jit(solution)/shard_map/all_gather | solution.py:340
  30.1 139.9 %reduce-scatter.7.cloned.1.call-start = ((), (), s32[]{:S(2)}) async-start(), calls=%async_computation.8 | async-start | bytes 4718592 | tf_op jit(solution)/shard_map/reduce_scatter | solution.py:344
  122.3 3.0 copy-start.9
  132.3 70.1 %all-gather.9.cloned.1.call-start = ((), (), s32[]{:S(2)}) async-start(), calls=%async_computation.9 | async-start | bytes 2359296 | tf_op jit(solution)/shard_map/all_gather | solution.py:340
  172.1 78.4 %reduce-scatter.9.cloned.1.call-start = ((), (), s32[]{:S(2)}) async-start(), calls=%async_computation.10 | async-start | bytes 4718592 | tf_op jit(solution)/shard_map/reduce_scatter | solution.py:344
  202.4 3.3 copy-start.2
  202.4 3.3 copy-start.11
  212.6 69.6 %all-gather.13.cloned.1.call-start = ((), (), s32[]{:S(2)}) async-start(), calls=%async_computation.13 | async-start | bytes 2359296 | tf_op jit(solution)/shard_map/all_gather | solution.py:351
  213.2 99.6 %all-gather.11.cloned.1.call-start = ((), (), s32[]{:S(2)}) async-start(), calls=%async_computation.11 | async-start | bytes 2359296 | tf_op jit(solution)/shard_map/all_gather | solution.py:340
  252.6 110.0 %reduce-scatter.13.cloned.1.call-start = ((), (), s32[]{:S(2)}) async-start(), calls=%async_computation.14 | async-start | bytes 4718592 | tf_op jit(solution)/shard_map/reduce_scatter | solution.py:358
  312.8 3.3 copy-start.5
  312.8 3.3 copy-start.14
  312.8 3.3 copy-start.29
  316.0 5.2 copy-start.31
  316.1 3.8 copy-start.6
  324.6 80.5 %reduce-scatter.11.cloned.1.call-start = ((), (), s32[]{:S(2)}) async-start(), calls=%async_computation.12 | async-start | bytes 4718592 | tf_op jit(solution)/shard_map/reduce_scatter | solution.py:344
  329.9 75.2 %copy-start.7 = (bf16[128,1024]{1,0:T(8,128)(2,1)S(1)}, bf16[128,1024]{1,0:T(8,128)(2,1)}, u32[]{:S(2)}) copy-start(bf16[128,1024]{1,0:T(8,128)(2,1)} %param.7) | copy-start | bytes 786436
  329.9 107.5 %all-gather.15.cloned.1.call-start = ((), (), s32[]{:S(2)}) async-start(), calls=%async_computation.15 | async-start | bytes 2359296 | tf_op jit(solution)/shard_map/all_gather | solution.py:351
  407.4 78.2 %reduce-scatter.15.cloned.1.call-start = ((), (), s32[]{:S(2)}) async-start(), calls=%async_computation.16 | async-start | bytes 4718592 | tf_op jit(solution)/shard_map/reduce_scatter | solution.py:358
  437.5 4.5 copy-start.4
  442.0 1.3 copy-start.19
  442.0 1.3 copy-start.33
  442.0 2.0 copy-start.3
  442.0 2.3 copy-start.27
  447.7 39.2 %copy-start.1 = (bf16[128,1024]{1,0:T(8,128)(2,1)S(1)}, bf16[128,1024]{1,0:T(8,128)(2,1)}, u32[]{:S(2)}) copy-start(bf16[128,1024]{1,0:T(8,128)(2,1)} %get-tuple-element.23) | copy-start | bytes 786436
  447.7 71.2 %all-gather.17.cloned.1.call-start = ((), (), s32[]{:S(2)}) async-start(), calls=%async_computation.17 | async-start | bytes 2359296 | tf_op jit(solution)/shard_map/all_gather | solution.py:351
  489.0 77.8 %reduce-scatter.17.cloned.1.call-start = ((), (), s32[]{:S(2)}) async-start(), calls=%async_computation.18 | async-start | bytes 4718592 | tf_op jit(solution)/shard_map/reduce_scatter | solution.py:358
  523.3 2.0 copy-start.24
  528.8 4.7 copy-start.13
  528.8 4.7 copy-start.32
  528.8 4.7 copy-start.41
  533.4 2.8 copy-start.15
  533.5 2.8 copy-start.30
  536.3 2.8 copy-start.12
  536.3 2.8 copy-start.20
  539.1 2.6 copy-start.16
  539.1 2.6 copy-start.28
  539.1 2.6 copy-start.40
  541.7 2.9 copy-start.34
  544.5 2.7 copy-start.10
  544.5 2.7 copy-start.22
  547.2 2.9 copy-start.17
  547.2 2.9 copy-start.25
  547.2 2.9 copy-start.38
  550.1 2.7 copy-start.36
  (7 other events, 8.2 us)
Sparse Core Ops, SparseCore 0:
  32.3 35.9 all-gather.6
  132.4 37.5 reduce-scatter.6
  172.5 29.8 all-gather.8
  212.7 37.7 reduce-scatter.8
  252.2 29.9 all-gather.12
  284.5 28.2 all-gather.10
  324.7 37.7 reduce-scatter.12
  365.7 39.3 reduce-scatter.10
  407.6 29.8 all-gather.14
  447.8 37.7 reduce-scatter.14
  489.1 29.7 all-gather.16
  528.9 37.7 reduce-scatter.16

commit v2 on v1

--- a/solution.py
+++ b/solution.py
@@ -66,11 +66,9 @@
 def ar_kernel(dims, *refs):
     layers, ny, nz, nf = dims
     units = 3 * nf
-    grads = refs[:3 * layers]
-    gain_ref = refs[3 * layers]
-    out_ref, gain_out = refs[3 * layers + 1:3 * layers + 3]
+    grad_ref, gain_ref, out_ref, gain_out = refs[:4]
     (G, st_ay, st_bz, st_az, st_by, R, gain_buf, rs_send, rs_recv, ag_send, ag_recv,
-     x_send, x_recv, g_send, g_recv, in_sem, out_sem, ready) = refs[3 * layers + 3:]
+     x_send, x_recv, g_send, g_recv, in_sem, out_sem, ready) = refs[4:]
     y, z, f = lax.axis_index("replica"), lax.axis_index("dp"), lax.axis_index("fsdp")
 
     barrier = pltpu.get_barrier_semaphore()
@@ -81,19 +79,10 @@
             pl.semaphore_signal(barrier, inc=1, device_id={axis: wrap(pos + j, size)}, device_id_type=MESH)
             count += 1
 
-    def load(i, carry):
-        yy, zz = i // nz, i % nz
-        for layer in range(layers):
-            for m in range(2):
-                src = grads[3 * layer + m].at[:, zz, :, pl.ds(pl.multiple_of(yy * LN, LN), LN)]
-                pltpu.make_async_copy(src, G.at[layer, yy, zz, pl.ds(m * nf, nf)], in_sem).start()
-            for h in range(2):
-                src = grads[3 * layer + 2].at[zz, :, :, pl.ds(pl.multiple_of((2 * yy + h) * LN, LN), LN)]
-                pltpu.make_async_copy(src, G.at[layer, yy, zz, pl.ds(2 * nf + h * (nf // 2), nf // 2)], in_sem).start()
-        return carry
-    lax.fori_loop(0, ny * nz, load, 0)
+    load = pltpu.make_async_copy(grad_ref, G, in_sem)
+    load.start()
     pl.semaphore_wait(barrier, count)
-    pltpu.make_async_copy(out_ref, G, in_sem).wait()
+    load.wait()
 
     streams = split_units(units)
     hops, base = [], 0
@@ -242,17 +231,11 @@
     streams = split_units(units)
     a, b = streams[0][1], max(streams[2][1], streams[3][1])
     copies = layers * 2 * 2 * ((ny - 1) + (nz - 1))
-    views = []
-    for i, g in enumerate(grads):
-        if i % 3 < 2:
-            views.append(g.reshape(nf, nz, RS, ny * LN))
-        else:
-            views.append(g.reshape(nz, nf // 2, RS, 2 * ny * LN))
     gr = gain.reshape(-1, LN)
     out, gain_out = pl.pallas_call(
         functools.partial(ar_kernel, dims),
         out_shape=(jax.ShapeDtypeStruct((layers, ny, nz, units, RS, LN), F32), jax.ShapeDtypeStruct(gr.shape, F32)),
-        in_specs=[pl.BlockSpec(memory_space=pl.ANY)] * len(views) + [pl.BlockSpec(memory_space=pltpu.VMEM)],
+        in_specs=[pl.BlockSpec(memory_space=pl.ANY), pl.BlockSpec(memory_space=pltpu.VMEM)],
         out_specs=(pl.BlockSpec(memory_space=pl.ANY), pl.BlockSpec(memory_space=pltpu.VMEM)),
         scratch_shapes=[
             pltpu.VMEM((layers, ny, nz, units, RS, LN), F32),
@@ -270,107 +253,456 @@
         ],
         compiler_params=pltpu.CompilerParams(collective_id=0, has_side_effects=True, vmem_limit_bytes=52 * 2**20),
         name="grad_all_reduce",
-    )(*views, gr)
+    )(grads, gr)
     return out, gain_out
 
 
-def unpack_kernel(g_ref, o_ref):
-    ny, nf = g_ref.shape[0], g_ref.shape[1]
-    for j in range(nf):
+def unpack_kernel(g_ref, gate_ref, up_ref, down_ref):
+    ny, nzb, units = g_ref.shape[:3]
+    nf = units // 3
+    for k in range(nzb):
         for i in range(ny):
-            o_ref[:, (j * ny + i) * LN:(j * ny + i + 1) * LN] = g_ref[i, j]
-
-
-def unpack_down_kernel(g_ref, o_ref):
-    ny, nf = g_ref.shape[0], g_ref.shape[1]
-    for i in range(ny):
-        for h in range(2):
-            for r in range(nf // 2):
-                o_ref[r * RS:(r + 1) * RS, (2 * i + h) * LN:(2 * i + h + 1) * LN] = g_ref[i, h * (nf // 2) + r]
-
-
-def unpack(out, dims):
+            for m, ref in enumerate((gate_ref, up_ref)):
+                for j in range(nf):
+                    col = (j * ny + i) * LN
+                    ref[k * RS:(k + 1) * RS, col:col + LN] = g_ref[i, k, m * nf + j]
+            for h in range(2):
+                for r in range(nf // 2):
+                    row, col = (k * (nf // 2) + r) * RS, (2 * i + h) * LN
+                    down_ref[row:row + RS, col:col + LN] = g_ref[i, k, 2 * nf + h * (nf // 2) + r]
+
+
+def unpack(out, dims, steps=2):
     layers, ny, nz, nf = dims
-    res = []
-    for m in range(3):
-        spec_in = pl.BlockSpec((None, ny, None, nf, RS, LN), functools.partial(lambda m, l, z: (l, 0, z, m, 0, 0), m))
-        if m < 2:
-            shape, block, body = (layers, nz * RS, nf * ny * LN), (None, RS, nf * ny * LN), unpack_kernel
+    nzb = nz // steps
+    wide, tall = nf * ny * LN, (nf // 2) * RS
+    return pl.pallas_call(
+        unpack_kernel, grid=(layers, steps),
+        in_specs=[pl.BlockSpec((None, ny, nzb, 3 * nf, RS, LN), lambda l, z: (l, 0, z, 0, 0, 0))],
+        out_specs=[pl.BlockSpec((None, nzb * RS, wide), lambda l, z: (l, z, 0))] * 2
+        + [pl.BlockSpec((None, nzb * tall, 2 * ny * LN), lambda l, z: (l, z, 0))],
+        out_shape=[jax.ShapeDtypeStruct((layers, nz * RS, wide), F32)] * 2
+        + [jax.ShapeDtypeStruct((layers, nz * tall, 2 * ny * LN), F32)],
+        name="unpack")(out)
+
+
+NORM_EPS = 1e-6
+NN = (((1,), (0,)), ((), ()))
+NT = (((1,), (1,)), ((), ()))
+TN = (((0,), (0,)), ((), ()))
+
+
+def dot(a, b, dims=NN):
+    return lax.dot_general(a, b, dims, preferred_element_type=F32)
+
+
+def fb_kernel(dims, x_ref, dy_ref, wg_ref, wu_ref, wd_ref, gain_ref, y_ref, grad_ref, dgain_ref,
+              WB, WD, N, GA, UA, PA, DH, O, DS, MS, H, DGU, GL,
+              ag_send, ag_recv, rs_send, rs_recv, wx_send, wx_recv, wy_send, wy_recv, w_sem, wd_sem, out_sem):
+    layers, ny, nz, nf, tok, depth, hid = dims
+    nx, half, q = nf // 2, tok // 2, depth // nf // ny
+    f, y = lax.axis_index("fsdp"), lax.axis_index("replica")
+    x, c = f // 2, f % 2
+    partner = 2 * x + (1 - c)
+    tile = min(256, depth)
+
+    def dev(off, core=None):
+        return 2 * wrap(x + off, nx) + (c if core is None else core)
+
+    h0, h1 = pl.ds(0, half), pl.ds(half, half)
+    whole = pl.ds(0, tok)
+
+    barrier = pltpu.get_barrier_semaphore()
+    for j in range(1, nf):
+        pl.semaphore_signal(barrier, inc=1, device_id={"fsdp": wrap(f + j, nf)}, device_id_type=MESH)
+    for j in (1, ny - 1):
+        pl.semaphore_signal(barrier, inc=1, device_id={"replica": wrap(y + j, ny)}, device_id_type=MESH)
+
+    wd_copies = [pltpu.make_async_copy(wd_ref.at[l], WD.at[l], wd_sem.at[l]) for l in range(layers)]
+    mine = pl.ds(y * q, q)
+    weights = (wg_ref, wu_ref)
+
+    def own_rows(l, m):
+        src = weights[m].at[l, mine, pl.ds(pl.multiple_of(f * hid, hid), hid)]
+        return pltpu.make_async_copy(src, WB.at[l, m, f, mine], w_sem.at[l, m])
+
+    for l in range(layers):
+        for m in range(2):
+            own_rows(l, m).start()
+        wd_copies[l].start()
+    pl.semaphore_wait(barrier, nf + 1)
+
+    def wx_copy(l, m, j, peer, sender):
+        return pltpu.make_async_remote_copy(
+            src_ref=weights[m].at[l, mine, pl.ds(pl.multiple_of(peer * hid, hid), hid)], dst_ref=WB.at[l, m, sender, mine],
+            send_sem=wx_send.at[l, m, j], recv_sem=wx_recv.at[l, m, sender], device_id={"fsdp": peer}, device_id_type=MESH)
+
+    def wx_start(l):
+        for m in range(2):
+            for j in range(1, nf):
+                wx_copy(l, m, j, wrap(f + j, nf), f).start()
+
+    parts = (pl.ds(0, nf // 2), pl.ds(nf // 2, nf // 2))
+
+    def wy_copy(l, m, k, owner, part, step):
+        view = WB.at[l, m, parts[part], pl.ds(wrap(owner, ny) * q, q)]
+        return pltpu.make_async_remote_copy(
+            src_ref=view, dst_ref=view, send_sem=wy_send.at[l, m, k], recv_sem=wy_recv.at[l, m, k],
+            device_id={"replica": wrap(y + step, ny)}, device_id_type=MESH)
+
+    def wy_sends(l, m):
+        args = [(0, y, 0, 1), (2, y, 1, -1), (1, y, 1, 1), (3, y, 0, -1), (4, y - 1, 0, 1), (5, y + 1, 1, -1)]
+        return [functools.partial(wy_copy, l, m, *a) for a in args]
+
+    def wy_start(l):
+        for m in range(2):
+            own_rows(l, m).wait()
+            for j in range(1, nf):
+                wx_copy(l, m, j, wrap(f + j, nf), wrap(f + j, nf)).wait_recv()
+            for copy in wy_sends(l, m)[:4]:
+                copy().start()
+
+    def wy_mid(l):
+        for m in range(2):
+            sends = wy_sends(l, m)
+            wy_copy(l, m, 0, y - 1, 0, 1).wait_recv()
+            sends[4]().start()
+            wy_copy(l, m, 2, y + 1, 1, -1).wait_recv()
+            sends[5]().start()
+
+    def wy_end(l):
+        for m in range(2):
+            wy_copy(l, m, 1, y - 1, 1, 1).wait_recv()
+            wy_copy(l, m, 3, y + 1, 0, -1).wait_recv()
+            wy_copy(l, m, 4, y - 2, 0, 1).wait_recv()
+            wy_copy(l, m, 5, y + 2, 1, -1).wait_recv()
+
+    class Gather:
+        def __init__(self, r, buf):
+            self.r, self.buf = r, buf
+
+        def copy(self, k, block, rows, target):
+            view = self.buf.at[block, rows]
+            return pltpu.make_async_remote_copy(
+                src_ref=view, dst_ref=view, send_sem=ag_send.at[self.r, k], recv_sem=ag_recv.at[self.r, k],
+                device_id={"fsdp": target}, device_id_type=MESH)
+
+        def sends(self):
+            args = [(0, f, whole, partner), (1, f, h0, dev(1)), (2, f, h1, dev(1)), (3, f, h1, dev(-1)), (4, f, h0, dev(-1)),
+                    (5, dev(-1), h0, dev(1)), (6, dev(1), h1, dev(-1)), (7, dev(-1), whole, partner), (8, dev(1), whole, partner),
+                    (9, dev(2), h0, partner), (10, dev(2), h1, partner)]
+            return [functools.partial(self.copy, *a) for a in args]
+
+        def wait(self, k):
+            o = 1 - c
+            block, rows = [(partner, whole), (dev(-1), h0), (dev(-1), h1), (dev(1), h1), (dev(1), h0), (dev(2), h0), (dev(2), h1),
+                           (dev(-1, o), whole), (dev(1, o), whole), (dev(2, o), h0), (dev(2, o), h1)][k]
+            self.copy(k, block, rows, partner).wait_recv()
+
+        def start(self):
+            sends = self.sends()
+            for k in (1, 3, 0, 2, 4):
+                sends[k]().start()
+
+        def mid(self):
+            sends = self.sends()
+            for k, nxt in ((1, 5), (3, 6), (2, 7), (4, 8)):
+                self.wait(k)
+                sends[nxt]().start()
+
+        def end(self):
+            sends = self.sends()
+            for k, nxt in ((5, 9), (6, 10)):
+                self.wait(k)
+                sends[nxt]().start()
+
+        def near(self):
+            self.wait(7)
+            self.wait(8)
+
+        def far(self):
+            self.wait(9)
+            self.wait(10)
+
+        def drain(self):
+            for copy in self.sends():
+                copy().wait_send()
+
+    def rs_d2d(r, i, xp, core):
+        return pltpu.make_async_remote_copy(
+            src_ref=O.at[xp, core], dst_ref=DS.at[r % 2, xp], send_sem=rs_send.at[r, i], recv_sem=rs_recv.at[r, i],
+            device_id={"fsdp": partner}, device_id_type=MESH)
+
+    quarter = half // 2
+
+    def rs_msg(r, k, d):
+        off, side = (2, d) if k == 0 else (1 - 2 * d, d if k == 3 else 1 - d)
+        start, size, slot, at = side * half, half, (0 if k == 0 else 2), 0
+        if k in (1, 2):
+            at = (k - 1) * quarter
+            start, size, slot = side * half + at, quarter, 1
+        return pltpu.make_async_remote_copy(
+            src_ref=O.at[wrap(x + off, nx), c, pl.ds(start, size)], dst_ref=MS.at[r % 2, d, slot, pl.ds(at, size)],
+            send_sem=rs_send.at[r, 4 + 2 * k + d], recv_sem=rs_recv.at[r, 4 + 2 * k + d],
+            device_id={"fsdp": dev(1 - 2 * d)}, device_id_type=MESH)
+
+    def combine(r, i, off):
+        xp = wrap(x + off, nx)
+        rs_d2d(r, i, xp, c).wait_recv()
+        O[xp, c] += DS[r % 2, xp]
+
+    def rs_start(r):
+        combine(r, 1, 1)
+        rs_msg(r, 1, 0).start()
+        combine(r, 2, 3)
+        rs_msg(r, 1, 1).start()
+        combine(r, 3, 2)
+        for k in (0, 2):
+            for d in range(2):
+                rs_msg(r, k, d).start()
+        combine(r, 0, 0)
+
+    def rs_mid(r):
+        for d in range(2):
+            rs_msg(r, 0, d).wait_recv()
+            O[wrap(x + 1 - 2 * d, nx), c, pl.ds(d * half, half)] += MS[r % 2, d, 0]
+            rs_msg(r, 3, d).start()
+
+    def rs_end(r):
+        for k in (1, 2, 3):
+            for d in range(2):
+                rs_msg(r, k, d).wait_recv()
+        s = r % 2
+        top = O[x, c, h0] + (MS[s, 0, 2] + MS[s, 1, 1])
+        bottom = O[x, c, h1] + (MS[s, 0, 1] + MS[s, 1, 2])
+        for i in range(nx):
+            rs_d2d(r, i, x, 1 - c).wait_send()
+        for k in range(4):
+            for d in range(2):
+                rs_msg(r, k, d).wait_send()
+        return jnp.concatenate([top, bottom], axis=0)
+
+    def pairs(r, gather, body, waited):
+        def step(i, carry):
+            if not waited:
+                @pl.when(i == 1)
+                def _():
+                    gather.mid()
+                    gather.near()
+
+                @pl.when(i == 3)
+                def _():
+                    gather.end()
+                    gather.far()
+            xp = wrap(x + i + i // 2 - 2 * (i // 3), nx)
+            body(xp)
+            rs_d2d(r, i, xp, 1 - c).start()
+            return carry
+        lax.fori_loop(0, nx, step, 0)
+
+    def rms(hidden):
+        return lax.rsqrt(jnp.mean(hidden * hidden, axis=-1, keepdims=True) + NORM_EPS)
+
+    fwd = [Gather(l, N.at[l]) for l in range(layers)]
+    bwd = [Gather(2 * layers - 1 - l, DH.at[l]) for l in range(layers)]
+    last = layers - 1
+
+    H[0] = x_ref[...]
+    DH[last, f] = dy_ref[...]
+    wx_start(0)
+    for l in range(layers):
+        hidden = H[l].astype(F32)
+        N[l, f] = (hidden * rms(hidden) * gain_ref[l:l + 1]).astype(BF16)
+        gather = fwd[l]
+        gather.start()
+        if l == 0:
+            for other in range(1, layers):
+                wx_start(other)
+            bwd[last].start()
+            wy_start(0)
+            gather.mid()
+            wy_mid(0)
+            for other in range(1, layers):
+                wy_start(other)
+            gather.near()
+            gather.end()
+            gather.far()
+            bwd[last].mid()
+            gather.wait(0)
+            wy_end(0)
         else:
-            shape, block, body = (layers, nz * (nf // 2) * RS, 2 * ny * LN), (None, (nf // 2) * RS, 2 * ny * LN), unpack_down_kernel
-        res.append(pl.pallas_call(
-            body, grid=(layers, nz), in_specs=[spec_in],
-            out_specs=pl.BlockSpec(block, lambda l, z: (l, z, 0)),
-            out_shape=jax.ShapeDtypeStruct(shape, F32), name="unpack_%d" % m)(out))
-    return res
-
-
-NORM_EPS = 1e-6
+            wy_end(l)
+            gather.wait(0)
+        wd_copies[l].wait()
+
+        def forward(xp, l=l):
+            tokens = N[l, pl.ds(2 * xp, 2)].reshape(2 * tok, depth)
+            for j in range(hid // tile):
+                cols = pl.ds(j * tile, tile)
+                gate = dot(tokens, WB[l, 0, :, :, cols].reshape(depth, tile)).astype(BF16)
+                up = dot(tokens, WB[l, 1, :, :, cols].reshape(depth, tile)).astype(BF16)
+                GA[l, xp, :, cols] = gate
+                UA[l, xp, :, cols] = up
+                PA[l, xp, :, cols] = (jax.nn.silu(gate.astype(F32)) * up.astype(F32)).astype(BF16)
+            prod = PA[l, xp]
+            for j in range(depth // tile):
+                cols = pl.ds(j * tile, tile)
+                O[xp, :, :, cols] = dot(prod, WD[l, :, cols]).reshape(2, tok, tile)
+
+        pairs(l, gather, forward, l == 0)
+        rs_start(l)
+        if l == 0:
+            bwd[last].near()
+            bwd[last].end()
+            bwd[last].far()
+            bwd[last].wait(0)
+            for other in range(1, layers):
+                wy_mid(other)
+        rs_mid(l)
+        hidden = (H[l].astype(F32) + rs_end(l)).astype(BF16)
+        if l < last:
+            H[l + 1] = hidden
+        else:
+            y_ref[...] = hidden
+
+    grad_copy = None
+    for l in reversed(range(layers)):
+        r = 2 * layers - 1 - l
+        gather = bwd[l]
+        if l != last:
+            gather.start()
+            gather.wait(0)
+
+        def backward(xp, l=l):
+            cot = DH[l, pl.ds(2 * xp, 2)].reshape(2 * tok, depth)
+            for j in range(hid // tile):
+                cols = pl.ds(j * tile, tile)
+                d_prod = dot(cot, WD[l, cols, :], NT).astype(BF16).astype(F32)
+                gate = GA[l, xp, :, cols].astype(F32)
+                sig = jax.nn.sigmoid(gate)
+                d_up = d_prod * gate * sig
+                d_gate = d_prod * UA[l, xp, :, cols].astype(F32) * sig * (1.0 + gate * (1.0 - sig))
+                DGU[0, xp, :, cols] = d_gate.astype(BF16)
+                DGU[1, xp, :, cols] = d_up.astype(BF16)
+            d_gate, d_up = DGU[0, xp], DGU[1, xp]
+            rows = depth // nf
+            for j in range(depth // tile):
+                sub = pl.ds(j * tile // rows, tile // rows)
+                part = dot(d_gate, WB[l, 0, sub].reshape(tile, hid), NT) + dot(d_up, WB[l, 1, sub].reshape(tile, hid), NT)
+                O[xp, :, :, pl.ds(j * tile, tile)] = part.reshape(2, tok, tile)
+
+        pairs(r, gather, backward, l == last)
+        rs_start(r)
+
+        if grad_copy is not None:
+            grad_copy.wait()
+        group = nf // 2
+        zs = tile // (group * RS)
+
+        def down_grad(j, carry, l=l):
+            lhs = PA[l, :, :, pl.ds(pl.multiple_of(j * tile, tile), tile)].reshape(nf * tok, tile)
+            for i in range(depth // tile):
+                res = dot(lhs, DH[l, :, :, pl.ds(i * tile, tile)].reshape(nf * tok, tile), TN)
+                for h in range(tile // LN):
+                    col = i * (tile // LN) + h
+                    for zi in range(zs):
+                        for g in range(group):
+                            row = (zi * group + g) * RS
+                            GL[col // 2, j * zs + zi, 2 * nf + (col % 2) * group + g] = res[row:row + RS, h * LN:(h + 1) * LN]
+            return carry
+        lax.fori_loop(0, hid // tile, down_grad, 0)
+        rs_mid(r)
+
+        fs = tile // (nz * RS)
+
+        def up_grad(j, carry, l=l):
+            lhs = N[l, :, :, pl.ds(pl.multiple_of(j * tile, tile), tile)].reshape(nf * tok, tile)
+            for m in range(2):
+                for i in range(hid // tile):
+                    res = dot(lhs, DGU[m, :, :, pl.ds(i * tile, tile)].reshape(nf * tok, tile), TN)
+                    for h in range(tile // LN):
+                        for fi in range(fs):
+                            for zi in range(nz):
+                                row = (fi * nz + zi) * RS
+                                GL[i * (tile // LN) + h, zi, m * nf + j * fs + fi] = res[row:row + RS, h * LN:(h + 1) * LN]
+            return carry
+        lax.fori_loop(0, depth // tile, up_grad, 0)
+        grad_copy = pltpu.make_async_copy(GL, grad_ref.at[l], out_sem)
+        grad_copy.start()
+
+        d_normed = rs_end(r).astype(BF16).astype(F32)
+        hidden = H[l].astype(F32)
+        inv = rms(hidden)
+        dgain_ref[l:l + 1] = jnp.sum(d_normed * hidden * inv, axis=0, keepdims=True)
+        if l > 0:
+            scaled = d_normed * gain_ref[l:l + 1]
+            cot = DH[l, f].astype(F32)
+            d_hidden = cot + inv * scaled - hidden * (inv * inv * inv) * jnp.mean(scaled * hidden, axis=-1, keepdims=True)
+            DH[l - 1, f] = d_hidden.astype(BF16)
+
+    for gather in fwd + bwd:
+        gather.drain()
+    for l in range(layers):
+        for m in range(2):
+            for j in range(1, nf):
+                wx_copy(l, m, j, wrap(f + j, nf), f).wait_send()
+            for copy in wy_sends(l, m):
+                copy().wait_send()
+    grad_copy.wait()
+
+
+def forward_backward(x, dy, wg, wu, wd, gain, dims):
+    layers, ny, nz, nf, tok, depth, hid = dims
+    nx = nf // 2
+    vm, hbm = pl.BlockSpec(memory_space=pltpu.VMEM), pl.BlockSpec(memory_space=pl.ANY)
+    dma = pltpu.SemaphoreType.DMA
+    return pl.pallas_call(
+        functools.partial(fb_kernel, dims),
+        out_shape=(jax.ShapeDtypeStruct((tok, depth), BF16),
+                   jax.ShapeDtypeStruct((layers, ny, nz, 3 * nf, RS, LN), F32),
+                   jax.ShapeDtypeStruct((layers, depth), F32)),
+        in_specs=[vm, vm, hbm, hbm, hbm, vm],
+        out_specs=(vm, hbm, vm),
+        scratch_shapes=[
+            pltpu.VMEM((layers, 2, nf, depth // nf, hid), BF16),
+            pltpu.VMEM((layers, hid, depth), BF16),
+            pltpu.VMEM((layers, nf, tok, depth), BF16),
+            pltpu.VMEM((layers, nx, 2 * tok, hid), BF16),
+            pltpu.VMEM((layers, nx, 2 * tok, hid), BF16),
+            pltpu.VMEM((layers, nx, 2 * tok, hid), BF16),
+            pltpu.VMEM((layers, nf, tok, depth), BF16),
+            pltpu.VMEM((nx, 2, tok, depth), F32),
+            pltpu.VMEM((2, nx, tok, depth), F32),
+            pltpu.VMEM((2, 2, 3, tok // 2, depth), F32),
+            pltpu.VMEM((layers, tok, depth), BF16),
+            pltpu.VMEM((2, nx, 2 * tok, hid), BF16),
+            pltpu.VMEM((ny, nz, 3 * nf, RS, LN), F32),
+            dma((2 * layers, 11)), dma((2 * layers, 11)),
+            dma((2 * layers, 12)), dma((2 * layers, 12)),
+            dma((layers, 2, nf)), dma((layers, 2, nf)),
+            dma((layers, 2, 6)), dma((layers, 2, 6)),
+            dma((layers, 2)), dma((layers,)), dma,
+        ],
+        compiler_params=pltpu.CompilerParams(collective_id=1, has_side_effects=True, vmem_limit_bytes=60 * 2**20),
+        name="forward_backward",
+    )(x, dy, wg, wu, wd, gain)
+
+
 TOKEN_AXES = ("dp", "replica", "fsdp")
-CONTRACT_ROWS = (((0,), (0,)), ((), ()))
-CONTRACT_COLS = (((1,), (1,)), ((), ()))
-
-
-def dot(a, b, dims=(((1,), (0,)), ((), ()))):
-    return lax.dot_general(a, b, dims, preferred_element_type=F32)
 
 
 def solution(mesh):
-    shards = mesh.shape["fsdp"]
-    tok_spec = P(TOKEN_AXES, None)
-    shard_spec = P(None, "fsdp", None)
-    full_spec = P(None, None)
-
-    def to_columns(w_rows):
-        layers, rows, cols = w_rows.shape
-        split = w_rows.reshape(layers, rows, shards, cols // shards)
-        moved = lax.all_to_all(split, "fsdp", split_axis=2, concat_axis=1, tiled=True)
-        return moved.reshape(layers, rows * shards, cols // shards)
-
-    def device_step(x_local, dy_local, w_gate_sh, w_up_sh, w_down_sh, norm_gain):
-        layers = w_gate_sh.shape[0]
-        both = to_columns(jnp.concatenate([w_gate_sh, w_up_sh], axis=0))
-        w_gate, w_up, w_down = both[:layers], both[layers:], w_down_sh
-        hidden = x_local
-        saved = []
-        for layer in range(layers):
-            hidden_f = hidden.astype(F32)
-            inv_rms = lax.rsqrt(jnp.mean(hidden_f * hidden_f, axis=-1, keepdims=True) + NORM_EPS)
-            normed = (hidden_f * inv_rms * norm_gain[layer]).astype(BF16)
-            normed = lax.all_gather(normed, "fsdp", axis=0, tiled=True)
-            gate = dot(normed, w_gate[layer]).astype(BF16)
-            up = dot(normed, w_up[layer]).astype(BF16)
-            prod = (jax.nn.silu(gate.astype(F32)) * up.astype(F32)).astype(BF16)
-            out = lax.psum_scatter(dot(prod, w_down[layer]), "fsdp", scatter_dimension=0, tiled=True)
-            saved.append((hidden_f, inv_rms, normed, gate, up, prod))
-            hidden = (hidden_f + out).astype(BF16)
-        cot = dy_local
-        grads = [None] * layers
-        for layer in reversed(range(layers)):
-            hidden_f, inv_rms, normed, gate, up, prod = saved[layer]
-            cot_all = lax.all_gather(cot, "fsdp", axis=0, tiled=True)
-            d_prod = dot(cot_all, w_down[layer], CONTRACT_COLS).astype(BF16).astype(F32)
-            gate_f = gate.astype(F32)
-            sig = jax.nn.sigmoid(gate_f)
-            d_gate = (d_prod * up.astype(F32) * sig * (1.0 + gate_f * (1.0 - sig))).astype(BF16)
-            d_up = (d_prod * gate_f * sig).astype(BF16)
-            part = dot(d_gate, w_gate[layer], CONTRACT_COLS) + dot(d_up, w_up[layer], CONTRACT_COLS)
-            d_normed = lax.psum_scatter(part, "fsdp", scatter_dimension=0, tiled=True).astype(BF16).astype(F32)
-            d_gain = jnp.sum(d_normed * hidden_f * inv_rms, axis=0)
-            scaled = d_normed * norm_gain[layer]
-            d_hidden = cot.astype(F32) + inv_rms * scaled - hidden_f * (inv_rms * inv_rms * inv_rms) * jnp.mean(scaled * hidden_f, axis=-1, keepdims=True)
-            cot = d_hidden.astype(BF16)
-            grads[layer] = (
-                dot(normed, d_gate, CONTRACT_ROWS),
-                dot(normed, d_up, CONTRACT_ROWS),
-                dot(prod, cot_all, CONTRACT_ROWS),
-                d_gain,
-            )
-        flat = [grads[layer][part] for layer in range(layers) for part in range(3)]
-        gain = jnp.stack([grads[layer][3] for layer in range(layers)])
-        dims = (layers, mesh.shape["replica"], mesh.shape["dp"], shards)
-        blocks, gain_sum = all_reduce(flat, gain, dims)
+    ny, nz, nf = mesh.shape["replica"], mesh.shape["dp"], mesh.shape["fsdp"]
+    tok_spec, shard_spec, full_spec = P(TOKEN_AXES, None), P(None, "fsdp", None), P(None, None)
+
+    def device_step(x, dy, wg, wu, wd, gain):
+        layers, depth = gain.shape
+        dims = (layers, ny, nz, nf)
+        out, grads, d_gain = forward_backward(x, dy, wg, wu, wd, gain, dims + (x.shape[0], depth, wd.shape[1]))
+        blocks, gain_sum = all_reduce(grads, d_gain, dims)
         dw_gate, dw_up, dw_down = unpack(blocks, dims)
-        return (hidden, dw_gate, dw_up, dw_down, gain_sum.reshape(gain.shape))
-
-    return jax.shard_map(device_step, mesh=mesh, in_specs=(tok_spec, tok_spec, shard_spec, shard_spec, shard_spec, full_spec), out_specs=(tok_spec, shard_spec, shard_spec, shard_spec, full_spec), check_vma=False)
+        return out, dw_gate, dw_up, dw_down, gain_sum.reshape(gain.shape)
+
+    return jax.shard_map(
+        device_step, mesh=mesh, in_specs=(tok_spec, tok_spec, shard_spec, shard_spec, shard_spec, full_spec),
+        out_specs=(tok_spec, shard_spec, shard_spec, shard_spec, full_spec), check_vma=False)

time: 895 us -> 515 us (0.58); the launches traced: 882 us -> 514 us
  waiting for transfers between devices: 423 us -> 0 us
  Pallas kernels: 307 us -> 511 us
  matrix products: 83.1 us -> 0 us
  local copies, waits for them, and re-layouts: 30.7 us -> 2.05 us
  other arithmetic: 15.4 us -> 0 us
  between operations: 15.1 us -> 0.66 us
    pallas_call x3 -> x2, Pallas kernels: 44 us -> 246 us  [the longest x1 232 us: forward_backward(): pl.pallas_call(functools.partial(fb_kernel, dims), out_shape=(jax.ShapeDt...]
    reduce_scatter x6 -> x0, waiting for transfers between devices: 198 us -> none  [the longest x3 116 us: device_step(): lax.psum_scatter(dot(prod, w_down[layer]), 'fsdp', scatter_dimension=0, t...]
    all_gather x6 -> x0, waiting for transfers between devices: 146 us -> none  [the longest x3 89.1 us: device_step(): cot_all = lax.all_gather(cot, 'fsdp', axis=0, tiled=True)]
    dot_general x27 -> x0, matrix products: 83.1 us -> none  [dot(): return lax.dot_general(a, b, dims, preferred_element_type=F32)]
    all_to_all x1 -> x0, waiting for transfers between devices: 78.4 us -> none  [to_columns(): lax.all_to_all(split, 'fsdp', split_axis=2, concat_axis=1, tiled=True)]
    unnamed x86 -> x3, local copies, waits for them, and re-layouts: 12.8 us -> 0.71 us
  transfers between devices with their start and end apart: 13 -> 0, of which waited for: 12 -> 0; matrix products, arithmetic and copies ran while one was open for 6% -> 0% of each run, Pallas kernels for 0% -> 0%
where the time goes in v2:
time: 515 us; the launch traced here: 514 us
  Pallas kernels  511 us (99%)
    pallas_call x1, Pallas kernels, all_reduce(): pl.pallas_call(functools.partial(ar_kernel, dims), out_shape=(jax.ShapeDt...  265 us
    pallas_call x1, Pallas kernels, forward_backward(): pl.pallas_call(functools.partial(fb_kernel, dims), out_shape=(jax.ShapeDt...  232 us
    pallas_call x1, Pallas kernels, unpack(): pl.pallas_call(unpack_kernel, grid=(layers, steps), in_specs=[pl.BlockSpe...  14 us

profile of v2, /device:TPU:1, one launch (start us, length us, event | category | flops | bytes accessed | tf_op | source)
XLA Modules:
  0.0 513.6 jit_solution(2597973733324526333)
XLA Ops:
  0.6 232.3 %forward_backward.1 = (bf16[128,1024]{1,0:T(8,128)(2,1)}, f32[3,4,8,24,16,128]{5,4,3,2,1,0:T(8,128)}, f32[3,1024]{1,0:T(4,128)}) custom-call(bf16[128,1024]{1,0:T(8,128)(2,1)} %x_ref.1, bf16[128,1024]{1,0:T(8,128)(2,1)} %dy_ref.1, bf16[3,128,4096]{2,1,0:T(8,128)(2,1)} %wg_ref.1, bf16[3,128,4096]{2,1,0:T(8,128)(2,1)} %wu_ref.1, bf16[3,512,1024]{2,1,0:T(8,128)(2,1)} %wd_ref.1, ...), custom_call_target="tpu_custom_call" | custom-call | tf_op jit(solution)/shard_map/forward_backward/pallas_call | solution.py:659
  232.9 0.7 reshape.16.refs_1_
  233.7 264.5 %grad_all_reduce.1 = (f32[3,4,8,24,16,128]{5,4,3,2,1,0:T(8,128)}, f32[24,128]{1,0:T(8,128)S(1)}) custom-call(f32[3,4,8,24,16,128]{5,4,3,2,1,0:T(8,128)} %get-tuple-element.14.refs_0_, f32[24,128]{1,0:T(8,128)S(1)} %reshape.16.refs_1_), custom_call_target="tpu_custom_call" | custom-call | tf_op jit(solution)/shard_map/grad_all_reduce/pallas_call | solution.py:235
  498.2 0.0 copy-start
  498.2 14.0 %unpack.1 = (f32[3,128,4096]{2,1,0:T(8,128)}, f32[3,128,4096]{2,1,0:T(8,128)}, f32[3,512,1024]{2,1,0:T(8,128)}) custom-call(f32[3,4,8,24,16,128]{5,4,3,2,1,0:T(8,128)} %get-tuple-element.16.g_ref), custom_call_target="tpu_custom_call" | custom-call | tf_op jit(solution)/shard_map/unpack/pallas_call | solution.py:279
  512.3 0.6 reshape.17
  512.9 0.0 copy-done
  512.9 0.7 copy.12
Async XLA Ops:
  498.2 14.7 %copy-start = (bf16[128,1024]{1,0:T(8,128)(2,1)S(1)}, bf16[128,1024]{1,0:T(8,128)(2,1)}, u32[]{:S(2)}) copy-start(bf16[128,1024]{1,0:T(8,128)(2,1)} %get-tuple-element.26) | copy-start | bytes 786436

commit v3 on v0

v3 whole, which is shorter than its diff:
```python
import functools
import heapq
import jax
import jax.numpy as jnp
from jax import lax
from jax.sharding import PartitionSpec as P
from jax.experimental import pallas as pl
from jax.experimental.pallas import tpu as pltpu

F32 = jnp.float32
BF16 = jnp.bfloat16
LOGICAL = pl.DeviceIdType.LOGICAL
RS, LN = 16, 128
UNIT_BYTES = RS * LN * 4
NORM_EPS = 1e-6
NN = (((1,), (0,)), ((), ()))
NT = (((1,), (1,)), ((), ()))
TN = (((0,), (0,)), ((), ()))
LINK_RATE, CORE_RATE, HOP, CORE_HOP, STEP_COST = 46.6e3, 500e3, 2.2, 0.9, 0.15
CORES = "cores"
BOTH, SIGN, BF16_BYTES = (0, 1), (1, -1), 2
FIRST, SECOND, PASS, RELAY, FAR, OWN = range(6)
FORWARD, BACKWARD, DOWN, ADD, EXCHANGE = 1.2, 1.7, 2.2, 0.2, 5.0


def dot(a, b, dims=NN):
    return lax.dot_general(a, b, dims, preferred_element_type=F32)


def repeat(start, stop, work):
    def step(i, carry):
        work(i)
        return carry
    lax.fori_loop(start, stop, step, 0)


def wrap(value, size):
    return lax.rem(value + 4 * size, size)


class Clock:
    def __init__(self):
        self.now, self.queue, self.count, self.links = 0.0, [], 0, {}

    def send(self, link, size):
        near = link == CORES
        start = max(self.now, self.links.get(link, 0.0))
        self.links[link] = start + size / (CORE_RATE if near else LINK_RATE)
        return self.links[link] + (CORE_HOP if near else HOP)

    def after(self, ready, work):
        self.count += 1
        heapq.heappush(self.queue, (ready, self.count, work))

    def step(self):
        ready, _, work = heapq.heappop(self.queue)
        self.now = max(self.now, ready) + STEP_COST
        work()

    def run(self, until):
        while self.queue and self.queue[0][0] <= until:
            self.step()

    def busy(self, spent):
        self.now += spent
        self.run(self.now)

    def idle(self, until):
        self.run(until)
        self.now = max(self.now, until)


class Job:
    def __init__(self, env, layer, part, start, offsets, swap):
        sizes = PART_SIZES[part]
        self.env, self.layer, self.part, self.swap = env, layer, part, swap
        self.sizes, self.offsets, self.starts = sizes, offsets, (start, start + sizes[0])
        self.units = pl.ds(start, sum(sizes))
        self.left, self.arrived, self.early = 2, {}, {}
        rings = (env.ny // 2, env.nz // 2)
        self.slots = {}
        for gather in (False, True):
            for phase in BOTH:
                for k in BOTH:
                    for d in BOTH:
                        half = rings[phase ^ k]
                        self.slots[gather, phase, k, d] = env.slots[gather]
                        env.slots[gather] += half if gather else half + 1

    def ring(self, phase, k):
        return ("replica", "dp")[phase ^ k]

    def half_ring(self, phase, k):
        return self.env.size[self.ring(phase, k)] // 2

    def block(self, phase, k, index, side=None):
        env, G, layer = self.env, self.env.G, self.layer
        start, size = self.starts[k], self.sizes[k]
        if side is not None:
            start, size = start + side * (size // 2), size // 2
        units = pl.ds(start, size)
        if phase == 0:
            return G.at[layer, index, :, units] if k == 0 else G.at[layer, :, index, units]
        return G.at[layer, env.y, index, units] if k == 0 else G.at[layer, index, env.z, units]

    def stage(self, phase, k, d, step, side=None):
        env = self.env
        buf = env.G.at[0] if self.layer == env.last else env.S
        first = 0 if k == 0 else env.split
        offset, size = self.offsets[k], self.sizes[k]
        half_total = ((env.units - env.split) if k else env.split) // 2
        at = 2 * (step - 1) + d
        if step == 0:
            units = pl.ds(first + d * half_total + offset // 2, size // 2)
            at = env.nz - 2 if self.ring(phase, k) == "dp" else 2
        elif side is None:
            units = pl.ds(first + offset, size)
        else:
            units = pl.ds(first + offset + side * (size // 2), size // 2)
        if phase == 0:
            return buf.at[at, :, units] if k == 0 else buf.at[:, at, units]
        return buf.at[env.ny - 1, at, units] if k == 0 else buf.at[at, env.nz - 1, units]

    def copy(self, gather, phase, k, d, slot, src, dst):
        env = self.env
        send, recv = (env.ag_send, env.ag_recv) if gather else (env.rs_send, env.rs_recv)
        slot = self.slots[gather, phase, k, d] + slot
        return pltpu.make_async_remote_copy(
            src_ref=src, dst_ref=dst, send_sem=send.at[slot], recv_sem=recv.at[slot],
            device_id=env.device(self.ring(phase, k), SIGN[d]), device_id_type=LOGICAL)

    def send_time(self, phase, k, d, units):
        env = self.env
        other = (env.nz if k == 0 else env.ny) if phase == 0 else 1
        return env.clock.send((self.ring(phase, k), d), units * other * UNIT_BYTES)

    def piece(self, phase, k, d, step, early):
        if step == 0:
            return 0, d
        if step == 1:
            return (1, 1 - d) if early else (2, d)
        return step + 1, None

    def reduce_copy(self, phase, k, d, step, early=False):
        slot, side = self.piece(phase, k, d, step, early)
        index = self.env.near(self.ring(phase, k), SIGN[d] * (self.half_ring(phase, k) - step))
        stage = self.stage(phase, k, d, step, None if step == 0 else side)
        return self.copy(False, phase, k, d, slot, self.block(phase, k, index, side), stage)

    def reduce_send(self, phase, k, d, step, early=False):
        self.reduce_copy(phase, k, d, step, early).start()
        ready = self.send_time(phase, k, d, self.sizes[k] if step > 1 else self.sizes[k] // 2)
        if early:
            self.early[phase, k, d] = ready
        else:
            if step == 1:
                ready = max(ready, self.early[phase, k, d])
            self.env.clock.after(ready, functools.partial(self.reduce_step, phase, k, d, step))

    def reduce_start(self, phase, k):
        for d in BOTH:
            self.reduce_send(phase, k, d, 0)
        for d in BOTH:
            self.reduce_send(phase, k, d, 1, True)

    def start(self):
        for k in BOTH:
            self.reduce_start(0, k)

    def reduce_step(self, phase, k, d, step):
        half = self.half_ring(phase, k)
        if step == 1:
            self.reduce_copy(phase, k, d, step, True).wait_recv()
        self.reduce_copy(phase, k, d, step).wait_recv()
        index = self.env.near(self.ring(phase, k), SIGN[d] * (half - 1 - step))
        self.block(phase, k, index, d if step == 0 else None)[...] += self.stage(phase, k, d, step)[...]
        if step + 1 < half:
            self.reduce_send(phase, k, d, step + 1)
        elif self.both(False, phase, k):
            if phase == 0:
                self.reduce_start(1, k)
            else:
                self.left -= 1
                if self.left == 0:
                    self.reduced()

    def both(self, gather, phase, k):
        key = gather, phase, k
        self.arrived[key] = self.arrived.get(key, 0) + 1
        return self.arrived[key] == 2

    def wait_sends(self, gather):
        for phase in BOTH:
            for k in BOTH:
                half = self.half_ring(phase, k)
                for d in BOTH:
                    some, all_units = self.block(phase, k, 0, d), self.block(phase, k, 0)

                    def done(slot, view):
                        self.copy(gather, phase, k, d, slot, view, view).wait_send()
                    if gather:
                        repeat(0, half - 1, lambda slot: done(slot, all_units))
                        done(half - 1, some)
                    else:
                        repeat(0, 3, lambda slot: done(slot, some))
                        if half > 2:
                            repeat(3, half + 1, lambda slot: done(slot, all_units))

    def x_copy(self, m, j, peer, sender):
        env = self.env
        return pltpu.make_async_remote_copy(
            src_ref=env.G.at[self.layer, env.y, env.z, m * env.nf + peer], dst_ref=env.R.at[self.layer, m * env.nf + sender],
            send_sem=env.x_send.at[self.layer, m, j], recv_sem=env.x_recv.at[self.layer, m, sender],
            device_id=env.row + peer, device_id_type=LOGICAL)

    def reduced(self):
        env = self.env
        self.wait_sends(False)
        for axis in ("replica", "dp"):
            for sign in (1, -1):
                pl.semaphore_signal(env.ready.at[self.layer, self.part], device_id=env.device(axis, sign), device_id_type=LOGICAL)
        for m in self.swap:
            repeat(1, env.nf, lambda j: self.x_copy(m, j, wrap(env.f + j, env.nf), env.f).start())
        env.reduced.add((self.layer, self.part))
        env.clock.after(env.clock.now + (EXCHANGE if self.swap else HOP), self.exchanged)

    def exchanged(self):
        env = self.env
        f, nf = env.f, env.nf
        for m in self.swap:
            env.R[self.layer, m * nf + f] = env.G[self.layer, env.y, env.z, m * nf + f]
        for m in self.swap:
            repeat(1, nf, lambda j: self.x_copy(m, j, wrap(f + j, nf), f).wait_send())
            repeat(1, nf, lambda j: self.x_copy(m, j, wrap(f + j, nf), wrap(f + j, nf)).wait_recv())
        for m in self.swap:
            env.G[self.layer, env.y, env.z, pl.ds(m * nf, nf)] = env.R[self.layer, pl.ds(m * nf, nf)]
        pl.semaphore_wait(env.ready.at[self.layer, self.part], 4)
        self.left = 2
        for k in BOTH:
            self.gather_start(1, k)
        env.exchanged.add((self.layer, self.part))
        env.begin_waiting()

    def gather_copy(self, phase, k, d, step, index):
        side = d if step + 1 == self.half_ring(phase, k) else None
        view = self.block(phase, k, self.env.near(self.ring(phase, k), index), side)
        return self.copy(True, phase, k, d, step, view, view)

    def gather_send(self, phase, k, d, step):
        self.gather_copy(phase, k, d, step, -SIGN[d] * step).start()
        units = self.sizes[k] if step + 1 < self.half_ring(phase, k) else self.sizes[k] // 2
        ready = self.send_time(phase, k, d, units)
        self.env.clock.after(ready, functools.partial(self.gather_step, phase, k, d, step))

    def gather_start(self, phase, k):
        for d in BOTH:
            self.gather_send(phase, k, d, 0)

    def gather_step(self, phase, k, d, step):
        env = self.env
        self.gather_copy(phase, k, d, step, -SIGN[d] * (step + 1)).wait_recv()
        if step + 1 < self.half_ring(phase, k):
            self.gather_send(phase, k, d, step + 1)
        elif self.both(True, phase, k):
            if phase == 1:
                self.gather_start(0, k)
            else:
                self.left -= 1
                if self.left == 0:
                    here = (self.layer, slice(None), slice(None), self.units)
                    pltpu.make_async_copy(env.G.at[here], env.out_ref.at[here], env.out_sem).start()


class Env:
    def __init__(self, dims):
        self.exchanged, self.reduced, self.waiting, self.clock = set(), set(), [], Clock()
        self.slots = {False: 0, True: 0}
        self.ny, self.nz, self.nf = dims[1:4]
        self.last = dims[0] - 1
        self.f, self.y, self.z = lax.axis_index("fsdp"), lax.axis_index("replica"), lax.axis_index("dp")
        self.size = {"fsdp": self.nf, "replica": self.ny, "dp": self.nz}
        self.pos = {"fsdp": self.f, "replica": self.y, "dp": self.z}
        stride = {"fsdp": 1, "replica": self.nf, "dp": self.nf * self.ny}
        me = self.f + stride["replica"] * self.y + stride["dp"] * self.z
        self.row = me - self.f
        self.shift = {a: [wrap(self.pos[a] + k, n) for k in range(n)] for a, n in self.size.items()}
        self.ids = {a: [me + (p - self.pos[a]) * stride[a] for p in self.shift[a]] for a in self.size}

    def near(self, axis, k):
        return self.shift[axis][k % self.size[axis]]

    def device(self, axis, k):
        return self.ids[axis][k % self.size[axis]]

    def begin(self, job):
        self.waiting.append(job)
        self.begin_waiting()

    def begin_waiting(self):
        for job in list(self.waiting):
            above = job.layer + 1, job.part
            if above[0] >= self.last or above in self.exchanged:
                self.waiting.remove(job)
                job.start()

    def settle(self, layer):
        while not {(layer, part) for part in BOTH} <= self.reduced:
            self.clock.step()


PART_SIZES = ((10, 6), (4, 4))
GATE_UP, DOWN_PART = BOTH


def step_kernel(dims, x_ref, dy_ref, wg_ref, wu_ref, wd_ref, gain_ref, y_ref, out_ref, gain_out,
                WB, WD, N, GA, UA, DH, O, DS, MS, H, DGU, G, S, R, gain_buf, gain_row,
                ag_send, ag_recv, rs_send, rs_recv, wx_send, wx_recv, wy_send, wy_recv, w_sem, wd_sem,
                jr_send, jr_recv, jg_send, jg_recv, x_send, x_recv, g_send, g_recv, out_sem, io_sem, ready, credit):
    layers, ny, nz, nf, tok, depth, hid = dims
    nx, half, q = nf // 2, tok // 2, depth // nf // ny
    tile = min(256, depth)
    last = layers - 1

    env = Env(dims)
    f, y, z = env.f, env.y, env.z
    x, c = f // 2, f % 2
    env.G, env.S, env.R, env.out_ref = G, S, R, out_ref
    env.rs_send, env.rs_recv, env.ag_send, env.ag_recv = jr_send, jr_recv, jg_send, jg_recv
    env.x_send, env.x_recv, env.ready, env.out_sem = x_send, x_recv, ready, out_sem
    env.units, env.split = 3 * nf, sum(sizes[0] for sizes in PART_SIZES)
    clock = env.clock
    jobs = {}
    for l in reversed(range(layers)):
        jobs[l, GATE_UP] = Job(env, l, GATE_UP, 0, (0, 0), BOTH)
        jobs[l, DOWN_PART] = Job(env, l, DOWN_PART, sum(PART_SIZES[GATE_UP]), PART_SIZES[GATE_UP], ())

    chips = [wrap(x + k, nx) for k in range(nx)]
    same, opposite_core = [2 * p + c for p in chips], [2 * p + (1 - c) for p in chips]
    fid = {id(v): env.row + v for v in same + opposite_core}

    def dev(off, opposite=False):
        return (opposite_core if opposite else same)[off % nx]

    partner = dev(0, True)
    halves = (pl.ds(0, half), pl.ds(half, half))
    whole = pl.ds(0, tok)
    axes = [("fsdp", f, nf), ("replica", y, ny), ("dp", z, nz)]

    barrier = pltpu.get_barrier_semaphore()
    for axis, pos, size in axes:
        for j in range(1, size):
            pl.semaphore_signal(barrier, device_id=env.device(axis, j), device_id_type=LOGICAL)

    x_copy = pltpu.make_async_copy(x_ref, H.at[0], io_sem.at[0])
    dy_copy = pltpu.make_async_copy(dy_ref, DH.at[last % 2, f], io_sem.at[1])
    x_copy.start()
    dy_copy.start()
    wd_copies = [pltpu.make_async_copy(wd_ref.at[l], WD.at[l], wd_sem.at[l]) for l in range(layers)]
    mine = pl.ds(y * q, q)
    weights = (wg_ref, wu_ref)

    def own_rows(l, m):
        src = weights[m].at[l, mine, pl.ds(pl.multiple_of(f * hid, hid), hid)]
        return pltpu.make_async_copy(src, WB.at[l, m, f, mine], w_sem.at[l, m])

    for l in range(layers):
        for m in BOTH:
            own_rows(l, m).start()
        wd_copies[l].start()
    pl.semaphore_wait(barrier, nf + ny + nz - 3)

    def wx_copy(l, m, j, peer, sender):
        return pltpu.make_async_remote_copy(
            src_ref=weights[m].at[l, mine, pl.ds(pl.multiple_of(peer * hid, hid), hid)], dst_ref=WB.at[l, m, sender, mine],
            send_sem=wx_send.at[l, m, j], recv_sem=wx_recv.at[l, m, sender], device_id=env.row + peer, device_id_type=LOGICAL)

    def wx_start(l):
        for m in BOTH:
            repeat(1, nf, lambda j: wx_copy(l, m, j, wrap(f + j, nf), f).start())

    y_rows = [env.near("replica", k) * q for k in range(ny)]
    parts = (pl.ds(0, nf // 2), pl.ds(nf // 2, nf // 2))

    def wy_copy(l, m, kind, d, arrived=False):
        hops = (kind == PASS) + arrived
        part = parts[BOTH[d - (kind == SECOND)]]
        view = WB.at[l, m, part, pl.ds(y_rows[-SIGN[d] * hops % ny], q)]
        return pltpu.make_async_remote_copy(
            src_ref=view, dst_ref=view, send_sem=wy_send.at[l, m, kind, d], recv_sem=wy_recv.at[l, m, kind, d],
            device_id=env.device("replica", SIGN[d]), device_id_type=LOGICAL)

    def wy_each(l, kinds, work):
        for m in BOTH:
            for kind in kinds:
                for d in BOTH:
                    work(l, m, kind, d)

    def wy_send_one(*args):
        wy_copy(*args).start()

    def wy_take(*args):
        wy_copy(*args, True).wait_recv()

    def wy_start(l):
        for m in BOTH:
            own_rows(l, m).wait()
            repeat(1, nf, lambda j: wx_copy(l, m, j, wrap(f + j, nf), wrap(f + j, nf)).wait_recv())
            for kind in (FIRST, SECOND):
                for d in BOTH:
                    wy_send_one(l, m, kind, d)

    def wy_mid(l):
        for m in BOTH:
            for d in BOTH:
                wy_take(l, m, FIRST, d)
                wy_send_one(l, m, PASS, d)

    def wy_end(l):
        wy_each(l, (SECOND, PASS), wy_take)

    class Gather:
        def __init__(self, r, buf):
            self.r, self.buf, self.ready = r, buf, {}

        def copy(self, kind, d, arrived=False):
            hops = (kind in (PASS, RELAY)) + (kind == FAR) * nx // len(BOTH)
            local = kind in (RELAY, FAR, OWN)
            block = dev(-SIGN[d] * (hops + (arrived and not local)), arrived and local)
            rows = whole if kind in (RELAY, OWN) else halves[d - (kind == SECOND)]
            target = partner if local else dev(SIGN[d])
            view = self.buf.at[block, rows]
            return rows.size, pltpu.make_async_remote_copy(
                src_ref=view, dst_ref=view, send_sem=ag_send.at[self.r, kind, d], recv_sem=ag_recv.at[self.r, kind, d],
                device_id=fid[id(target)], device_id_type=LOGICAL)

        def send(self, kind, d):
            size, copy = self.copy(kind, d)
            copy.start()
            self.ready[kind, d] = clock.send(CORES if kind in (RELAY, FAR, OWN) else d, size * depth * BF16_BYTES)

        def wait(self, kind, d=0):
            clock.idle(self.ready[kind, d])
            self.copy(kind, d, True)[-1].wait_recv()

        def start(self):
            for kind in (FIRST, OWN, SECOND):
                for d in BOTH[:1] if kind == OWN else BOTH:
                    self.send(kind, d)

        def forward(self, kind, onward):
            for d in BOTH:
                self.wait(kind, d)
                self.send(onward, d)

        def mid(self):
            self.forward(FIRST, PASS)
            self.forward(SECOND, RELAY)

        def end(self):
            self.forward(PASS, FAR)

        def take(self, kind):
            for d in BOTH:
                self.wait(kind, d)

        def near(self):
            self.take(RELAY)

        def far(self):
            self.take(FAR)

        def drain(self):
            for kind, d in self.ready:
                self.copy(kind, d)[-1].wait_send()

    def rs_d2d(r, i, xp, core):
        return pltpu.make_async_remote_copy(
            src_ref=O.at[xp, core], dst_ref=DS.at[xp], send_sem=rs_send.at[r, i], recv_sem=rs_recv.at[r, i],
            device_id=fid[id(partner)], device_id_type=LOGICAL)

    quarter = half // 2
    chunk = min(16, half)
    arrive = {}

    def rs_msg(r, k, d):
        off, side = (2, d) if k == 0 else (SIGN[d], d if k == 3 else 1 - d)
        start, size, slot, at = side * half, half, (0 if k == 0 else 2), 0
        if k in (1, 2):
            at = (k - 1) * quarter
            start, size, slot = side * half + at, quarter, 1
        return pltpu.make_async_remote_copy(
            src_ref=O.at[chips[off % nx], c, pl.ds(start, size)], dst_ref=MS.at[d, slot, pl.ds(at, size)],
            send_sem=rs_send.at[r, 4 + 2 * k + d], recv_sem=rs_recv.at[r, 4 + 2 * k + d],
            device_id=fid[id(dev(SIGN[d]))], device_id_type=LOGICAL)

    def rs_post(r, k, d):
        rs_msg(r, k, d).start()
        arrive[k, d] = clock.send(d, (quarter if k in (1, 2) else half) * depth * 4)

    def rs_take(r, k, d):
        clock.idle(arrive[k, d])
        rs_msg(r, k, d).wait_recv()

    def rows_at(start, j):
        return pl.ds(pl.multiple_of(start + j * chunk, chunk), chunk)

    def combine(r, i, off):
        xp = chips[off % nx]
        clock.idle(arrive[i])
        rs_d2d(r, i, xp, c).wait_recv()

        def add(j):
            rows = rows_at(0, j)
            O[xp, c, rows] += DS[xp, rows]
        repeat(0, tok // chunk, add)
        clock.busy(ADD)

    def rs_start(r):
        for i, d in ((1, 0), (2, 1)):
            combine(r, i, SIGN[d])
            rs_post(r, 1, d)
        combine(r, 3, 2)
        for k in (0, 2):
            for d in BOTH:
                rs_post(r, k, d)
        combine(r, 0, 0)

    def rs_mid(r):
        for d in BOTH:
            rs_take(r, 0, d)

            def add(j):
                rows = rows_at(d * half, j)
                O[chips[SIGN[d] % nx], c, rows] += MS[d, 0, rows_at(0, j)]
            repeat(0, half // chunk, add)
            rs_post(r, 3, d)

    def rs_end(r, body):
        for k in (1, 2, 3):
            for d in BOTH:
                rs_take(r, k, d)
        for side in BOTH:
            def step(j):
                rows, local = rows_at(side * half, j), rows_at(0, j)
                body(rows, O[x, c, rows] + (MS[0, 2 - side, local] + MS[1, 1 + side, local]))
            repeat(0, half // chunk, step)
        clock.busy(5 * ADD)
        for i in range(nx):
            rs_d2d(r, i, x, 1 - c).wait_send()
        for k in range(4):
            for d in BOTH:
                rs_msg(r, k, d).wait_send()

    def pairs(r, gather, body, cost):
        def step(i):
            xp = wrap(x + i + i // 2 - 2 * (i // 3), nx)
            body(xp)
            rs_d2d(r, i, xp, 1 - c).start()

        def go(first, stop):
            repeat(first, stop, step)
            for i in range(first, stop):
                clock.now += cost
                arrive[i] = clock.send(CORES, tok * depth * 4)
            clock.busy(0.0)

        if gather is None:
            go(0, nx)
            return
        go(0, 1)
        gather.mid()
        gather.near()
        go(1, 3)
        gather.end()
        gather.far()
        go(3, nx)

    def rms(hidden):
        return lax.rsqrt(jnp.mean(hidden * hidden, axis=-1, keepdims=True) + NORM_EPS)

    def down_grad(l):
        group = nf // 2
        zs = tile // (group * RS)

        def body(j, carry):
            lhs = GA[l, :, :, pl.ds(pl.multiple_of(j * tile, tile), tile)].reshape(-1, tile)
            for i in range(depth // tile):
                res = dot(lhs, DH[l % 2, :, :, pl.ds(i * tile, tile)].reshape(-1, tile), TN)
                for h in range(tile // LN):
                    col = i * (tile // LN) + h
                    for zi in range(zs):
                        rows = res[zi * group * RS:(zi + 1) * group * RS, h * LN:(h + 1) * LN]
                        G[l, col // 2, j * zs + zi, pl.ds(2 * nf + (col % 2) * group, group)] = rows.reshape(group, RS, LN)
            return carry
        lax.fori_loop(0, hid // tile, body, 0)

    def up_grad(l):
        fs = tile // (nz_rows * RS)

        def body(j, carry):
            lhs = N[l, :, :, pl.ds(pl.multiple_of(j * tile, tile), tile)].reshape(-1, tile)
            for m in BOTH:
                for i in range(hid // tile):
                    res = dot(lhs, DGU[m, :, :, pl.ds(i * tile, tile)].reshape(-1, tile), TN)
                    for h in range(tile // LN):
                        for fi in range(fs):
                            rows = res[fi * nz_rows * RS:(fi + 1) * nz_rows * RS, h * LN:(h + 1) * LN]
                            G[l, i * (tile // LN) + h, :, m * nf + j * fs + fi] = rows.reshape(nz_rows, RS, LN)
            return carry
        lax.fori_loop(0, depth // tile, body, 0)

    nz_rows = depth // nf // RS
    fwd = [Gather(l, N.at[l]) for l in range(layers)]
    bwd = [Gather(2 * layers - 1 - l, DH.at[l % 2]) for l in range(layers)]

    def activations(l, xp, cols):
        tokens = N[l, pl.ds(2 * xp, 2)].reshape(-1, depth)
        gate = dot(tokens, WB[l, 0, :, :, cols].reshape(depth, tile)).astype(BF16)
        up = dot(tokens, WB[l, 1, :, :, cols].reshape(depth, tile)).astype(BF16)
        return gate, up

    def product(xp, prod, l):
        for j in range(depth // tile):
            cols = pl.ds(j * tile, tile)
            O[xp, :, :, cols] = dot(prod, WD[l, :, cols]).reshape(-1, tok, tile)

    def forward(l, xp):
        for j in range(hid // tile):
            cols = pl.ds(j * tile, tile)
            gate, up = activations(l, xp, cols)
            GA[l, xp, :, cols] = gate
            UA[l, xp, :, cols] = up
            DGU[0, xp, :, cols] = (jax.nn.silu(gate.astype(F32)) * up.astype(F32)).astype(BF16)
        product(xp, DGU[0, xp], l)

    def backward(l, xp):
        cot = DH[l % 2, pl.ds(2 * xp, 2)].reshape(-1, depth)
        for j in range(hid // tile):
            cols = pl.ds(j * tile, tile)
            gate, up = activations(l, xp, cols) if l == last else (GA[l, xp, :, cols], UA[l, xp, :, cols])
            gate, up = gate.astype(F32), up.astype(F32)
            d_prod = dot(cot, WD[l, cols, :], NT).astype(BF16).astype(F32)
            sig = jax.nn.sigmoid(gate)
            GA[l, xp, :, cols] = (gate * sig * up).astype(BF16)
            DGU[0, xp, :, cols] = (d_prod * up * sig * (1.0 + gate * (1.0 - sig))).astype(BF16)
            DGU[1, xp, :, cols] = (d_prod * gate * sig).astype(BF16)
        d_gate, d_up = DGU[0, xp], DGU[1, xp]
        rows = depth // nf
        for j in range(depth // tile):
            sub = pl.ds(j * tile // rows, tile // rows)
            part = dot(d_gate, WB[l, 0, sub].reshape(tile, hid), NT) + dot(d_up, WB[l, 1, sub].reshape(tile, hid), NT)
            O[xp, :, :, pl.ds(j * tile, tile)] = part.reshape(-1, tok, tile)

    wx_start(0)
    x_copy.wait()
    dy_copy.wait()

    def normalize(l, rows, hidden):
        N[l, f, rows] = (hidden * rms(hidden) * gain_ref[l:l + 1]).astype(BF16)
    repeat(0, tok // chunk, lambda j: normalize(0, rows_at(0, j), H[0, rows_at(0, j)].astype(F32)))
    for l in range(last):
        gather = fwd[l]
        gather.start()
        if l == 0:
            for k in range(1, layers):
                wx_start(k)
            bwd[last].start()
            wy_start(0)
            gather.mid()
            wy_mid(0)
            for k in range(1, layers):
                wy_start(k)
            gather.near()
            gather.end()
            gather.far()
            bwd[last].mid()
        gather.wait(OWN)
        wy_end(l)
        wd_copies[l].wait()
        pairs(l, None if l == 0 else gather, functools.partial(forward, l), FORWARD)
        rs_start(l)
        if l == 0:
            bwd[last].near()
            bwd[last].end()
            bwd[last].far()
            bwd[last].wait(OWN)
            for k in range(1, layers):
                wy_mid(k)
        rs_mid(l)

        def next_hidden(rows, total, l=l):
            hidden = (H[l, rows].astype(F32) + total).astype(BF16)
            H[l + 1, rows] = hidden
            normalize(l + 1, rows, hidden.astype(F32))
        rs_end(l, next_hidden)

    for l in reversed(range(layers)):
        r = 2 * last - l
        gather = fwd[l] if l == last else bwd[l]
        gather.start()
        gather.wait(OWN)
        if l == last:
            wy_end(l)
            wd_copies[l].wait()
        pairs(r, gather, functools.partial(backward, l), FORWARD + BACKWARD if l == last else BACKWARD)
        rs_start(r)
        if l == 0:
            env.settle(last)
        down_grad(l)
        clock.busy(DOWN)
        env.begin(jobs[l, DOWN_PART])
        up_grad(l)
        clock.busy(2 * DOWN)
        env.begin(jobs[l, GATE_UP])
        rs_mid(r)
        bwd[l].drain()

        def next_cot(rows, total, l=l):
            d_normed = total.astype(BF16).astype(F32)
            hidden = H[l, rows].astype(F32)
            inv = rms(hidden)
            if l > 0:
                scaled = d_normed * gain_ref[l:l + 1]
                cot = DH[l % 2, f, rows].astype(F32)
                d_hidden = cot + inv * scaled - hidden * (inv * inv * inv) * jnp.mean(scaled * hidden, axis=-1, keepdims=True)
                DH[(l - 1) % 2, f, rows] = d_hidden.astype(BF16)
            gain_row[...] += jnp.sum(d_normed * hidden * inv, axis=0, keepdims=True)
        gain_row[...] = jnp.zeros((1, depth), F32)
        rs_end(r, next_cot)
        lanes = depth // LN
        for j in range(lanes):
            gain_buf[0, f, l * lanes + j:l * lanes + j + 1] = gain_row[:, j * LN:(j + 1) * LN]

    def gain_copy(stage, j):
        axis, pos, size = axes[stage]
        return pltpu.make_async_remote_copy(
            src_ref=gain_buf.at[stage, pos], dst_ref=gain_buf.at[stage, pos],
            send_sem=g_send.at[stage, j], recv_sem=g_recv.at[stage, pos],
            device_id=env.device(axis, j), device_id_type=LOGICAL)

    def gain_send(stage):
        for j in range(1, axes[stage][2]):
            gain_copy(stage, j).start()
        clock.after(clock.now + 2 * EXCHANGE, functools.partial(gain_sum, stage))

    def gain_sum(stage):
        axis, pos, size = axes[stage]
        for j in range(1, size):
            peer = env.near(axis, j)
            pltpu.make_async_remote_copy(
                src_ref=gain_buf.at[stage, peer], dst_ref=gain_buf.at[stage, peer],
                send_sem=g_send.at[stage, j], recv_sem=g_recv.at[stage, peer],
                device_id=env.device(axis, j), device_id_type=LOGICAL).wait_recv()
        total = gain_buf[stage, 0]
        for i in range(1, size):
            total = total + gain_buf[stage, i]
        if stage == 2:
            gain_out[...] = total
        else:
            gain_buf[stage + 1, axes[stage + 1][1]] = total
            gain_send(stage + 1)

    gain_send(0)

    for target in (partner, dev(1), dev(-1)):
        pl.semaphore_signal(credit, device_id=fid[id(target)], device_id_type=LOGICAL)
    r = 2 * layers - 1
    pl.semaphore_wait(credit, 3)
    pairs(r, None, lambda xp: product(xp, GA[last, xp], last), FORWARD)
    rs_start(r)
    rs_mid(r)

    def output(rows, total):
        H[0, rows] = (H[last, rows].astype(F32) + total).astype(BF16)
    rs_end(r, output)
    y_copy = pltpu.make_async_copy(H.at[0], y_ref, io_sem.at[2])
    y_copy.start()
    while clock.queue:
        clock.step()

    y_copy.wait()
    for gather in fwd:
        gather.drain()
    for l in range(layers):
        for m in BOTH:
            repeat(1, nf, lambda j: wx_copy(l, m, j, wrap(f + j, nf), f).wait_send())
            for kind in (FIRST, SECOND, PASS):
                for d in BOTH:
                    wy_copy(l, m, kind, d).wait_send()
    for job in jobs.values():
        job.wait_sends(True)
    for stage in range(3):
        for j in range(1, axes[stage][2]):
            gain_copy(stage, j).wait_send()
    pltpu.make_async_copy(G, out_ref, out_sem).wait()


def fused_step(x, dy, wg, wu, wd, gain, dims):
    layers, ny, nz, nf, tok, depth, hid = dims
    nx = nf // 2
    vm, hbm = pl.BlockSpec(memory_space=pltpu.VMEM), pl.BlockSpec(memory_space=pl.ANY)
    dma = pltpu.SemaphoreType.DMA
    blocks = (layers, ny, nz, 3 * nf, RS, LN)
    lines = layers * depth // LN
    steps = layers * 2 * 2 * (ny + nz)
    wide = max(nf, ny, nz)
    return pl.pallas_call(
        functools.partial(step_kernel, dims),
        out_shape=(jax.ShapeDtypeStruct((tok, depth), BF16), jax.ShapeDtypeStruct(blocks, F32), jax.ShapeDtypeStruct((lines, LN), F32)),
        in_specs=[hbm, hbm, hbm, hbm, hbm, vm],
        out_specs=(hbm, hbm, vm),
        scratch_shapes=[
            pltpu.VMEM((layers, 2, nf, depth // nf, hid), BF16),
            pltpu.VMEM((layers, hid, depth), BF16),
            pltpu.VMEM((layers, nf, tok, depth), BF16),
            pltpu.VMEM((layers, nx, 2 * tok, hid), BF16),
            pltpu.VMEM((layers, nx, 2 * tok, hid), BF16),
            pltpu.VMEM((2, nf, tok, depth), BF16),
            pltpu.VMEM((nx, 2, tok, depth), F32),
            pltpu.VMEM((nx, tok, depth), F32),
            pltpu.VMEM((2, 3, tok // 2, depth), F32),
            pltpu.VMEM((layers, tok, depth), BF16),
            pltpu.VMEM((2, nx, 2 * tok, hid), BF16),
            pltpu.VMEM(blocks, F32),
            pltpu.VMEM(blocks[1:], F32),
            pltpu.VMEM((layers, 2 * nf, RS, LN), F32),
            pltpu.VMEM((3, wide, lines, LN), F32),
            pltpu.VMEM((1, depth), F32),
            dma((2 * layers, OWN + 1, 2)), dma((2 * layers, OWN + 1, 2)),
            dma((2 * layers, 12)), dma((2 * layers, 12)),
            dma((layers, 2, nf)), dma((layers, 2, nf)),
            dma((layers, 2, PASS + 1, 2)), dma((layers, 2, PASS + 1, 2)),
            dma((layers, 2)), dma((layers,)),
            dma((steps + 8 * layers * 2,)), dma((steps + 8 * layers * 2,)), dma((steps,)), dma((steps,)),
            dma((layers, 2, nf)), dma((layers, 2, nf)),
            dma((3, wide)), dma((3, wide)), dma, dma((3,)),
            pltpu.SemaphoreType.REGULAR((layers, 2)), pltpu.SemaphoreType.REGULAR,
        ],
        compiler_params=pltpu.CompilerParams(collective_id=0, has_side_effects=True, vmem_limit_bytes=67043328),
        name="fused_step",
    )(x, dy, wg, wu, wd, gain)


def unpack_kernel(g_ref, gate_ref, up_ref, down_ref):
    ny, nzb, units = g_ref.shape[:3]
    nf = units // 3
    for k in range(nzb):
        for i in range(ny):
            for m, ref in enumerate((gate_ref, up_ref)):
                for j in range(nf):
                    col = (j * ny + i) * LN
                    ref[k * RS:(k + 1) * RS, col:col + LN] = g_ref[i, k, m * nf + j]
            for h in BOTH:
                for r in range(nf // 2):
                    row, col = (k * (nf // 2) + r) * RS, (2 * i + h) * LN
                    down_ref[row:row + RS, col:col + LN] = g_ref[i, k, 2 * nf + h * (nf // 2) + r]


def unpack(out, dims, steps=2):
    layers, ny, nz, nf = dims
    nzb = nz // steps
    wide, tall = nf * ny * LN, (nf // 2) * RS
    return pl.pallas_call(
        unpack_kernel, grid=(layers, steps),
        in_specs=[pl.BlockSpec((None, ny, nzb, 3 * nf, RS, LN), lambda l, z: (l, 0, z, 0, 0, 0))],
        out_specs=[pl.BlockSpec((None, nzb * RS, wide), lambda l, z: (l, z, 0))] * 2
        + [pl.BlockSpec((None, nzb * tall, 2 * ny * LN), lambda l, z: (l, z, 0))],
        out_shape=[jax.ShapeDtypeStruct((layers, nz * RS, wide), F32)] * 2
        + [jax.ShapeDtypeStruct((layers, nz * tall, 2 * ny * LN), F32)],
        name="unpack")(out)


TOKEN_AXES = ("dp", "replica", "fsdp")


def solution(mesh):
    ny, nz, nf = mesh.shape["replica"], mesh.shape["dp"], mesh.shape["fsdp"]
    tok_spec, shard_spec, full_spec = P(TOKEN_AXES, None), P(None, "fsdp", None), P(None, None)

    def device_step(x, dy, wg, wu, wd, gain):
        layers, depth = gain.shape
        dims = (layers, ny, nz, nf)
        out, blocks, gain_sum = fused_step(x, dy, wg, wu, wd, gain, dims + (x.shape[0], depth, wd.shape[1]))
        dw_gate, dw_up, dw_down = unpack(blocks, dims)
        return out, dw_gate, dw_up, dw_down, gain_sum.reshape(gain.shape)

    return jax.shard_map(
        device_step, mesh=mesh, in_specs=(tok_spec, tok_spec, shard_spec, shard_spec, shard_spec, full_spec),
        out_specs=(tok_spec, shard_spec, shard_spec, shard_spec, full_spec), check_vma=False)
```

time: 1800 us -> 397 us (0.22)
  waiting for transfers between devices: 1480 us -> 0 us
  Pallas kernels: 0 us -> 391 us
  matrix products: 188 us -> 0 us
  blocking collectives: 79.9 us -> 0 us
    reduce_scatter x9 -> x0, waiting for transfers between devices: 782 us -> none  [reduce_grad(): lax.psum_scatter(grad_local, 'fsdp', scatter_dimension=0, tiled=True)]
    all_gather x9 -> x0, waiting for transfers between devices: 434 us -> none  [the longest x3 146 us: gather_layer(): up_full = lax.all_gather(w_up_sh[layer_idx], 'fsdp', axis=0, tiled=True)]
    pallas_call x0 -> x2, Pallas kernels: none -> 391 us  [the longest x1 377 us: fused_step(): pl.pallas_call(functools.partial(step_kernel, dims), out_shape=(jax.Shape...]
    psum x1 -> x0, waiting for transfers between devices: 257 us -> none  [reduce_grad(): return lax.psum(grad_shard, COPY_AXES)]
    dot_general x27 -> x0, matrix products: 188 us -> none  [the longest x3 28.2 us: layer_backward(): lax.dot_general(normed, d_up, CONTRACT_ROWS, preferred_element_type=jnp.f...]
    psum x1 -> x0, blocking collectives: 79.9 us -> none  [device_step(): gain_sum = lax.psum(stacked[3], TOKEN_AXES)]
  transfers between devices with their start and end apart: 19 -> 0, of which waited for: 19 -> 0; matrix products, arithmetic and copies ran while one was open for 9% -> 0% of each run, Pallas kernels for 0% -> 0%
where the time goes in v3:
time: 397 us; the launch traced here: 393 us
  Pallas kernels  391 us (98%)
    pallas_call x1, Pallas kernels, fused_step(): pl.pallas_call(functools.partial(step_kernel, dims), out_shape=(jax.Shape...  377 us
    pallas_call x1, Pallas kernels, unpack(): pl.pallas_call(unpack_kernel, grid=(layers, steps), in_specs=[pl.BlockSpe...  14 us

profile of v3, /device:TPU:1, one launch (start us, length us, event | category | flops | bytes accessed | tf_op | source)
XLA Modules:
  0.0 392.6 jit_solution(14493739192412264138)
XLA Ops:
  0.6 376.6 %fused_step.1 = (bf16[128,1024]{1,0:T(8,128)(2,1)}, f32[3,4,8,24,16,128]{5,4,3,2,1,0:T(8,128)}, f32[24,128]{1,0:T(8,128)}) custom-call(bf16[128,1024]{1,0:T(8,128)(2,1)} %x_ref.1, bf16[128,1024]{1,0:T(8,128)(2,1)} %dy_ref.1, bf16[3,128,4096]{2,1,0:T(8,128)(2,1)} %wg_ref.1, bf16[3,128,4096]{2,1,0:T(8,128)(2,1)} %wu_ref.1, bf16[3,512,1024]{2,1,0:T(8,128)(2,1)} %wd_ref.1, ...), custom_call_target="tpu_custom_call" | custom-call | tf_op jit(solution)/shard_map/fused_step/pallas_call | solution.py:807
  377.3 0.0 copy-start.1
  377.3 0.0 copy-start
  377.3 14.0 %unpack.1 = (f32[3,128,4096]{2,1,0:T(8,128)}, f32[3,128,4096]{2,1,0:T(8,128)}, f32[3,512,1024]{2,1,0:T(8,128)}) custom-call(f32[3,4,8,24,16,128]{5,4,3,2,1,0:T(8,128)} %get-tuple-element.12.g_ref), custom_call_target="tpu_custom_call" | custom-call | tf_op jit(solution)/shard_map/unpack/pallas_call | solution.py:863
  391.3 0.0 copy-done.1
  391.3 0.6 reshape.13
  391.9 0.0 copy-done
  391.9 0.7 copy.12
Async XLA Ops:
  377.3 14.1 %copy-start.1 = (f32[24,128]{1,0:T(8,128)S(1)}, f32[24,128]{1,0:T(8,128)}, u32[]{:S(2)}) copy-start(f32[24,128]{1,0:T(8,128)} %get-tuple-element.16) | copy-start | bytes 36868
  377.3 14.7 %copy-start = (bf16[128,1024]{1,0:T(8,128)(2,1)S(1)}, bf16[128,1024]{1,0:T(8,128)(2,1)}, u32[]{:S(2)}) copy-start(bf16[128,1024]{1,0:T(8,128)(2,1)} %get-tuple-element.22) | copy-start | bytes 786436

commit v4 on v3

--- a/solution.py
+++ b/solution.py
@@ -16,11 +16,12 @@
 NN = (((1,), (0,)), ((), ()))
 NT = (((1,), (1,)), ((), ()))
 TN = (((0,), (0,)), ((), ()))
-LINK_RATE, CORE_RATE, HOP, CORE_HOP, STEP_COST = 46.6e3, 500e3, 2.2, 0.9, 0.15
+LINK_RATE, CORE_RATE, HOP, CORE_HOP, STEP_COST, HBM_READ, ENTRY = 46.6e3, 500e3, 2.2, 0.9, 0.15, 1.1, 3.5
 CORES = "cores"
 BOTH, SIGN, BF16_BYTES = (0, 1), (1, -1), 2
 FIRST, SECOND, PASS, RELAY, FAR, OWN = range(6)
-FORWARD, BACKWARD, DOWN, ADD, EXCHANGE = 1.2, 1.7, 2.2, 0.2, 5.0
+DIRECT = "direct"
+FORWARD, BACKWARD, WEIGHT, ADD, EXCHANGE = 1.2, 1.7, 2.2, 0.2, 5.0
 
 
 def dot(a, b, dims=NN):
@@ -71,12 +72,15 @@
 
 
 class Job:
-    def __init__(self, env, layer, part, start, offsets, swap):
+    def __init__(self, env, layer, part):
         sizes = PART_SIZES[part]
+        start = part * env.nf
+        offsets = [sum(p[k] for p in PART_SIZES[:part]) for k in BOTH]
+        swap = () if part == DOWN else (part,)
         self.env, self.layer, self.part, self.swap = env, layer, part, swap
         self.sizes, self.offsets, self.starts = sizes, offsets, (start, start + sizes[0])
         self.units = pl.ds(start, sum(sizes))
-        self.left, self.arrived, self.early = 2, {}, {}
+        self.left, self.turned, self.arrived, self.early = 2, 0, {}, {}
         rings = (env.ny // 2, env.nz // 2)
         self.slots = {}
         for gather in (False, True):
@@ -105,7 +109,7 @@
 
     def stage(self, phase, k, d, step, side=None):
         env = self.env
-        buf = env.G.at[0] if self.layer == env.last else env.S
+        ref, lead = (env.G, (0,)) if self.layer == env.last else (env.S, ())
         first = 0 if k == 0 else env.split
         offset, size = self.offsets[k], self.sizes[k]
         half_total = ((env.units - env.split) if k else env.split) // 2
@@ -117,9 +121,12 @@
             units = pl.ds(first + offset, size)
         else:
             units = pl.ds(first + offset + side * (size // 2), size // 2)
+        every = slice(None)
         if phase == 0:
-            return buf.at[at, :, units] if k == 0 else buf.at[:, at, units]
-        return buf.at[env.ny - 1, at, units] if k == 0 else buf.at[at, env.nz - 1, units]
+            place = (at, every) if k == 0 else (every, at)
+        else:
+            place = (env.ny - 1, at) if k == 0 else (at, env.nz - 1)
+        return ref.at[(*lead, *place, units)]
 
     def copy(self, gather, phase, k, d, slot, src, dst):
         env = self.env
@@ -163,9 +170,11 @@
         for d in BOTH:
             self.reduce_send(phase, k, d, 1, True)
 
-    def start(self):
-        for k in BOTH:
-            self.reduce_start(0, k)
+    def start(self, phase, k):
+        env = self.env
+        if phase == 0 and k == 0 and env.above(self):
+            pl.semaphore_wait(env.freed.at[env.above(self)], 4)
+        self.reduce_start(phase, k)
 
     def reduce_step(self, phase, k, d, step):
         half = self.half_ring(phase, k)
@@ -178,11 +187,26 @@
             self.reduce_send(phase, k, d, step + 1)
         elif self.both(False, phase, k):
             if phase == 0:
-                self.reduce_start(1, k)
+                self.halfway()
+                self.env.begin(self, 1, k)
             else:
                 self.left -= 1
                 if self.left == 0:
                     self.reduced()
+
+    def halfway(self):
+        env, here = self.env, (self.layer, self.part)
+        self.turned += 1
+        if self.turned == len(BOTH):
+            if 0 < self.layer < env.last:
+                self.tell(env.freed)
+            env.half.add(here)
+            env.begin_waiting()
+
+    def tell(self, flags):
+        for axis in ("replica", "dp"):
+            for sign in SIGN:
+                pl.semaphore_signal(flags.at[self.layer, self.part], device_id=self.env.device(axis, sign), device_id_type=LOGICAL)
 
     def both(self, gather, phase, k):
         key = gather, phase, k
@@ -208,17 +232,16 @@
 
     def x_copy(self, m, j, peer, sender):
         env = self.env
+        lane = (2 * self.layer + m) * env.nf
         return pltpu.make_async_remote_copy(
             src_ref=env.G.at[self.layer, env.y, env.z, m * env.nf + peer], dst_ref=env.R.at[self.layer, m * env.nf + sender],
-            send_sem=env.x_send.at[self.layer, m, j], recv_sem=env.x_recv.at[self.layer, m, sender],
+            send_sem=env.x_send.at[lane + j], recv_sem=env.x_recv.at[lane + sender],
             device_id=env.row + peer, device_id_type=LOGICAL)
 
     def reduced(self):
         env = self.env
         self.wait_sends(False)
-        for axis in ("replica", "dp"):
-            for sign in (1, -1):
-                pl.semaphore_signal(env.ready.at[self.layer, self.part], device_id=env.device(axis, sign), device_id_type=LOGICAL)
+        self.tell(env.ready)
         for m in self.swap:
             repeat(1, env.nf, lambda j: self.x_copy(m, j, wrap(env.f + j, env.nf), env.f).start())
         env.reduced.add((self.layer, self.part))
@@ -273,7 +296,7 @@
 
 class Env:
     def __init__(self, dims):
-        self.exchanged, self.reduced, self.waiting, self.clock = set(), set(), [], Clock()
+        self.exchanged, self.reduced, self.half, self.waiting, self.clock = set(), set(), set(), [], Clock()
         self.slots = {False: 0, True: 0}
         self.ny, self.nz, self.nf = dims[1:4]
         self.last = dims[0] - 1
@@ -292,30 +315,37 @@
     def device(self, axis, k):
         return self.ids[axis][k % self.size[axis]]
 
-    def begin(self, job):
-        self.waiting.append(job)
+    def above(self, job):
+        return (job.layer + 1, job.part) if job.layer + 1 < self.last else None
+
+    def begin(self, job, phase, k):
+        self.waiting.append((job, phase, k))
         self.begin_waiting()
 
+    def begin_job(self, job):
+        for k in BOTH:
+            self.begin(job, 0, k)
+
     def begin_waiting(self):
-        for job in list(self.waiting):
-            above = job.layer + 1, job.part
-            if above[0] >= self.last or above in self.exchanged:
-                self.waiting.remove(job)
-                job.start()
+        for item in list(self.waiting):
+            job, phase, k = item
+            if item in self.waiting and (not self.above(job) or self.above(job) in (self.exchanged if phase else self.half)):
+                self.waiting.remove(item)
+                job.start(phase, k)
 
     def settle(self, layer):
-        while not {(layer, part) for part in BOTH} <= self.reduced:
+        while not {(layer, part) for part in (GATE, UP, DOWN)} <= self.reduced:
             self.clock.step()
 
 
-PART_SIZES = ((10, 6), (4, 4))
-GATE_UP, DOWN_PART = BOTH
+GATE, UP, DOWN = range(3)
+PART_SIZES = ((6, 2), (4, 4), (4, 4))
 
 
 def step_kernel(dims, x_ref, dy_ref, wg_ref, wu_ref, wd_ref, gain_ref, y_ref, out_ref, gain_out,
                 WB, WD, N, GA, UA, DH, O, DS, MS, H, DGU, G, S, R, gain_buf, gain_row,
                 ag_send, ag_recv, rs_send, rs_recv, wx_send, wx_recv, wy_send, wy_recv, w_sem, wd_sem,
-                jr_send, jr_recv, jg_send, jg_recv, x_send, x_recv, g_send, g_recv, out_sem, io_sem, ready, credit):
+                jr_send, jr_recv, jg_send, jg_recv, x_send, x_recv, g_send, g_recv, out_sem, io_sem, ready, freed, credit):
     layers, ny, nz, nf, tok, depth, hid = dims
     nx, half, q = nf // 2, tok // 2, depth // nf // ny
     tile = min(256, depth)
@@ -326,13 +356,13 @@
     x, c = f // 2, f % 2
     env.G, env.S, env.R, env.out_ref = G, S, R, out_ref
     env.rs_send, env.rs_recv, env.ag_send, env.ag_recv = jr_send, jr_recv, jg_send, jg_recv
-    env.x_send, env.x_recv, env.ready, env.out_sem = x_send, x_recv, ready, out_sem
+    env.x_send, env.x_recv, env.ready, env.freed, env.out_sem = x_send, x_recv, ready, freed, out_sem
     env.units, env.split = 3 * nf, sum(sizes[0] for sizes in PART_SIZES)
     clock = env.clock
     jobs = {}
     for l in reversed(range(layers)):
-        jobs[l, GATE_UP] = Job(env, l, GATE_UP, 0, (0, 0), BOTH)
-        jobs[l, DOWN_PART] = Job(env, l, DOWN_PART, sum(PART_SIZES[GATE_UP]), PART_SIZES[GATE_UP], ())
+        for part in (GATE, UP, DOWN):
+            jobs[l, part] = Job(env, l, part)
 
     chips = [wrap(x + k, nx) for k in range(nx)]
     same, opposite_core = [2 * p + c for p in chips], [2 * p + (1 - c) for p in chips]
@@ -356,37 +386,59 @@
     x_copy.start()
     dy_copy.start()
     wd_copies = [pltpu.make_async_copy(wd_ref.at[l], WD.at[l], wd_sem.at[l]) for l in range(layers)]
-    mine = pl.ds(y * q, q)
     weights = (wg_ref, wu_ref)
-
-    def own_rows(l, m):
-        src = weights[m].at[l, mine, pl.ds(pl.multiple_of(f * hid, hid), hid)]
-        return pltpu.make_async_copy(src, WB.at[l, m, f, mine], w_sem.at[l, m])
-
-    for l in range(layers):
-        for m in BOTH:
-            own_rows(l, m).start()
-        wd_copies[l].start()
+    y_at = [env.near("replica", k) for k in range(ny)]
+    parts = (pl.ds(0, nf // 2), pl.ds(nf // 2, nf // 2))
+    direct = pl.ds(ny * q // 2, ny * q // 2)
+    direct_lane = 2 * layers * nf
+    shared = {}
+
+    def share(l, m, hops=0):
+        size = q // 2 if (l, m) == BOTH else q
+        return pl.ds(y_at[hops % ny] * size, size)
+
+    def own_rows(l, m, rows, sem):
+        src = weights[m].at[l, rows, pl.ds(pl.multiple_of(f * hid, hid), hid)]
+        return pltpu.make_async_copy(src, WB.at[l, m, f, rows], w_sem.at[sem])
+
+    own_copies = {(l, m): own_rows(l, m, share(l, m), 2 * l + m) for l in range(layers) for m in BOTH}
+    own_copies[DIRECT] = own_rows(*BOTH, direct, 2 * layers)
+    for copy in own_copies.values():
+        copy.start()
+    for copy in wd_copies:
+        copy.start()
     pl.semaphore_wait(barrier, nf + ny + nz - 3)
-
-    def wx_copy(l, m, j, peer, sender):
+    clock.busy(ENTRY)
+
+    def wx_copy(l, m, j, peer, sender, rows, lane):
         return pltpu.make_async_remote_copy(
-            src_ref=weights[m].at[l, mine, pl.ds(pl.multiple_of(peer * hid, hid), hid)], dst_ref=WB.at[l, m, sender, mine],
-            send_sem=wx_send.at[l, m, j], recv_sem=wx_recv.at[l, m, sender], device_id=env.row + peer, device_id_type=LOGICAL)
+            src_ref=weights[m].at[l, rows, pl.ds(pl.multiple_of(peer * hid, hid), hid)], dst_ref=WB.at[l, m, sender, rows],
+            send_sem=wx_send.at[lane + j], recv_sem=wx_recv.at[lane + sender], device_id=env.row + peer, device_id_type=LOGICAL)
+
+    def wx_sets(l):
+        return [(l, m, share(l, m), (2 * l + m) * nf) for m in BOTH]
+
+    def wx_post(key, l, m, rows, lane):
+        repeat(1, nf, lambda j: wx_copy(l, m, j, wrap(f + j, nf), f, rows, lane).start())
+        for d in BOTH:
+            shared[key] = clock.send(d, nx * rows.size * hid * BF16_BYTES) + HBM_READ
+
+    def wx_take(key, l, m, rows, lane):
+        clock.idle(shared[key])
+        own_copies[key].wait()
+        repeat(1, nf, lambda j: wx_copy(l, m, j, wrap(f + j, nf), wrap(f + j, nf), rows, lane).wait_recv())
 
     def wx_start(l):
-        for m in BOTH:
-            repeat(1, nf, lambda j: wx_copy(l, m, j, wrap(f + j, nf), f).start())
-
-    y_rows = [env.near("replica", k) * q for k in range(ny)]
-    parts = (pl.ds(0, nf // 2), pl.ds(nf // 2, nf // 2))
+        for args in wx_sets(l):
+            wx_post(args[:2], *args)
 
     def wy_copy(l, m, kind, d, arrived=False):
         hops = (kind == PASS) + arrived
+        lane = ((2 * l + m) * (PASS + 1) + kind) * 2 + d
         part = parts[BOTH[d - (kind == SECOND)]]
-        view = WB.at[l, m, part, pl.ds(y_rows[-SIGN[d] * hops % ny], q)]
+        view = WB.at[l, m, part, share(l, m, -SIGN[d] * hops)]
         return pltpu.make_async_remote_copy(
-            src_ref=view, dst_ref=view, send_sem=wy_send.at[l, m, kind, d], recv_sem=wy_recv.at[l, m, kind, d],
+            src_ref=view, dst_ref=view, send_sem=wy_send.at[lane], recv_sem=wy_recv.at[lane],
             device_id=env.device("replica", SIGN[d]), device_id_type=LOGICAL)
 
     def wy_each(l, kinds, work):
@@ -395,19 +447,20 @@
                 for d in BOTH:
                     work(l, m, kind, d)
 
-    def wy_send_one(*args):
-        wy_copy(*args).start()
+    def wy_send_one(l, m, kind, d):
+        wy_copy(l, m, kind, d).start()
+        shared[l, m, kind, d] = clock.send(("replica", d), nf // 2 * share(l, m).size * hid * BF16_BYTES)
 
     def wy_take(*args):
+        clock.idle(shared[args])
         wy_copy(*args, True).wait_recv()
 
     def wy_start(l):
-        for m in BOTH:
-            own_rows(l, m).wait()
-            repeat(1, nf, lambda j: wx_copy(l, m, j, wrap(f + j, nf), wrap(f + j, nf)).wait_recv())
+        for args in wx_sets(l):
+            wx_take(args[:2], *args)
             for kind in (FIRST, SECOND):
                 for d in BOTH:
-                    wy_send_one(l, m, kind, d)
+                    wy_send_one(*args[:2], kind, d)
 
     def wy_mid(l):
         for m in BOTH:
@@ -419,8 +472,8 @@
         wy_each(l, (SECOND, PASS), wy_take)
 
     class Gather:
-        def __init__(self, r, buf):
-            self.r, self.buf, self.ready = r, buf, {}
+        def __init__(self, r, buf, slot):
+            self.r, self.buf, self.slot, self.ready = r, buf, slot, {}
 
         def copy(self, kind, d, arrived=False):
             hops = (kind in (PASS, RELAY)) + (kind == FAR) * nx // len(BOTH)
@@ -428,9 +481,10 @@
             block = dev(-SIGN[d] * (hops + (arrived and not local)), arrived and local)
             rows = whole if kind in (RELAY, OWN) else halves[d - (kind == SECOND)]
             target = partner if local else dev(SIGN[d])
-            view = self.buf.at[block, rows]
+            lane = (self.r * (OWN + 1) + kind) * 2 + d
+            view = self.buf.at[self.slot, block, rows]
             return rows.size, pltpu.make_async_remote_copy(
-                src_ref=view, dst_ref=view, send_sem=ag_send.at[self.r, kind, d], recv_sem=ag_recv.at[self.r, kind, d],
+                src_ref=view, dst_ref=view, send_sem=ag_send.at[lane], recv_sem=ag_recv.at[lane],
                 device_id=fid[id(target)], device_id_type=LOGICAL)
 
         def send(self, kind, d):
@@ -475,7 +529,7 @@
 
     def rs_d2d(r, i, xp, core):
         return pltpu.make_async_remote_copy(
-            src_ref=O.at[xp, core], dst_ref=DS.at[xp], send_sem=rs_send.at[r, i], recv_sem=rs_recv.at[r, i],
+            src_ref=O.at[xp, core], dst_ref=DS.at[xp], send_sem=rs_send.at[12 * r + i], recv_sem=rs_recv.at[12 * r + i],
             device_id=fid[id(partner)], device_id_type=LOGICAL)
 
     quarter = half // 2
@@ -483,6 +537,7 @@
     arrive = {}
 
     def rs_msg(r, k, d):
+        lane = 12 * r + 4 + 2 * k + d
         off, side = (2, d) if k == 0 else (SIGN[d], d if k == 3 else 1 - d)
         start, size, slot, at = side * half, half, (0 if k == 0 else 2), 0
         if k in (1, 2):
@@ -490,7 +545,7 @@
             start, size, slot = side * half + at, quarter, 1
         return pltpu.make_async_remote_copy(
             src_ref=O.at[chips[off % nx], c, pl.ds(start, size)], dst_ref=MS.at[d, slot, pl.ds(at, size)],
-            send_sem=rs_send.at[r, 4 + 2 * k + d], recv_sem=rs_recv.at[r, 4 + 2 * k + d],
+            send_sem=rs_send.at[lane], recv_sem=rs_recv.at[lane],
             device_id=fid[id(dev(SIGN[d]))], device_id_type=LOGICAL)
 
     def rs_post(r, k, d):
@@ -515,10 +570,12 @@
         repeat(0, tok // chunk, add)
         clock.busy(ADD)
 
-    def rs_start(r):
+    def rs_near(r):
         for i, d in ((1, 0), (2, 1)):
             combine(r, i, SIGN[d])
             rs_post(r, 1, d)
+
+    def rs_start(r):
         combine(r, 3, 2)
         for k in (0, 2):
             for d in BOTH:
@@ -551,7 +608,7 @@
             for d in BOTH:
                 rs_msg(r, k, d).wait_send()
 
-    def pairs(r, gather, body, cost):
+    def pairs(r, gather, body, cost, after_mid=None):
         def step(i):
             xp = wrap(x + i + i // 2 - 2 * (i // 3), nx)
             body(xp)
@@ -564,15 +621,18 @@
                 arrive[i] = clock.send(CORES, tok * depth * 4)
             clock.busy(0.0)
 
-        if gather is None:
-            go(0, nx)
-            return
         go(0, 1)
-        gather.mid()
-        gather.near()
+        if gather:
+            gather.mid()
+            if after_mid:
+                after_mid()
+            gather.near()
         go(1, 3)
-        gather.end()
-        gather.far()
+        if gather:
+            gather.end()
+        rs_near(r)
+        if gather:
+            gather.far()
         go(3, nx)
 
     def rms(hidden):
@@ -610,8 +670,8 @@
         lax.fori_loop(0, depth // tile, body, 0)
 
     nz_rows = depth // nf // RS
-    fwd = [Gather(l, N.at[l]) for l in range(layers)]
-    bwd = [Gather(2 * layers - 1 - l, DH.at[l % 2]) for l in range(layers)]
+    fwd = [Gather(l, N, l) for l in range(layers)]
+    bwd = [Gather(2 * layers - 1 - l, DH, l % 2) for l in range(layers)]
 
     def activations(l, xp, cols):
         tokens = N[l, pl.ds(2 * xp, 2)].reshape(-1, depth)
@@ -658,35 +718,32 @@
     def normalize(l, rows, hidden):
         N[l, f, rows] = (hidden * rms(hidden) * gain_ref[l:l + 1]).astype(BF16)
     repeat(0, tok // chunk, lambda j: normalize(0, rows_at(0, j), H[0, rows_at(0, j)].astype(F32)))
+    clock.busy(5 * ADD)
+    straight = DIRECT, *BOTH, direct, direct_lane
     for l in range(last):
         gather = fwd[l]
         gather.start()
         if l == 0:
-            for k in range(1, layers):
-                wx_start(k)
-            bwd[last].start()
+            wx_post(*straight)
             wy_start(0)
             gather.mid()
             wy_mid(0)
             for k in range(1, layers):
-                wy_start(k)
+                wx_start(k)
             gather.near()
             gather.end()
             gather.far()
-            bwd[last].mid()
+            wx_take(*straight)
         gather.wait(OWN)
         wy_end(l)
         wd_copies[l].wait()
-        pairs(l, None if l == 0 else gather, functools.partial(forward, l), FORWARD)
+        pairs(l, gather if l else None, functools.partial(forward, l), FORWARD, bwd[last].start if l == last - 1 else None)
         rs_start(l)
-        if l == 0:
-            bwd[last].near()
-            bwd[last].end()
-            bwd[last].far()
-            bwd[last].wait(OWN)
-            for k in range(1, layers):
-                wy_mid(k)
+        wy_start(l + 1)
         rs_mid(l)
+        wy_mid(l + 1)
+        if l == last - 1:
+            bwd[last].mid()
 
         def next_hidden(rows, total, l=l):
             hidden = (H[l, rows].astype(F32) + total).astype(BF16)
@@ -700,6 +757,10 @@
         gather.start()
         gather.wait(OWN)
         if l == last:
+            bwd[l].near()
+            bwd[l].end()
+            bwd[l].far()
+            bwd[l].wait(OWN)
             wy_end(l)
             wd_copies[l].wait()
         pairs(r, gather, functools.partial(backward, l), FORWARD + BACKWARD if l == last else BACKWARD)
@@ -707,11 +768,12 @@
         if l == 0:
             env.settle(last)
         down_grad(l)
-        clock.busy(DOWN)
-        env.begin(jobs[l, DOWN_PART])
+        clock.busy(WEIGHT)
+        env.begin_job(jobs[l, DOWN])
         up_grad(l)
-        clock.busy(2 * DOWN)
-        env.begin(jobs[l, GATE_UP])
+        clock.busy(2 * WEIGHT)
+        env.begin_job(jobs[l, GATE])
+        env.begin_job(jobs[l, UP])
         rs_mid(r)
         bwd[l].drain()
 
@@ -781,12 +843,10 @@
     y_copy.wait()
     for gather in fwd:
         gather.drain()
+    for l, m, rows, lane in [straight[1:]] + [args for l in range(layers) for args in wx_sets(l)]:
+        repeat(1, nf, lambda j: wx_copy(l, m, j, wrap(f + j, nf), f, rows, lane).wait_send())
     for l in range(layers):
-        for m in BOTH:
-            repeat(1, nf, lambda j: wx_copy(l, m, j, wrap(f + j, nf), f).wait_send())
-            for kind in (FIRST, SECOND, PASS):
-                for d in BOTH:
-                    wy_copy(l, m, kind, d).wait_send()
+        wy_each(l, (FIRST, SECOND, PASS), lambda *args: wy_copy(*args).wait_send())
     for job in jobs.values():
         job.wait_sends(True)
     for stage in range(3):
@@ -802,7 +862,7 @@
     dma = pltpu.SemaphoreType.DMA
     blocks = (layers, ny, nz, 3 * nf, RS, LN)
     lines = layers * depth // LN
-    steps = layers * 2 * 2 * (ny + nz)
+    steps = layers * 3 * 2 * (ny + nz)
     wide = max(nf, ny, nz)
     return pl.pallas_call(
         functools.partial(step_kernel, dims),
@@ -826,15 +886,13 @@
             pltpu.VMEM((layers, 2 * nf, RS, LN), F32),
             pltpu.VMEM((3, wide, lines, LN), F32),
             pltpu.VMEM((1, depth), F32),
-            dma((2 * layers, OWN + 1, 2)), dma((2 * layers, OWN + 1, 2)),
-            dma((2 * layers, 12)), dma((2 * layers, 12)),
-            dma((layers, 2, nf)), dma((layers, 2, nf)),
-            dma((layers, 2, PASS + 1, 2)), dma((layers, 2, PASS + 1, 2)),
-            dma((layers, 2)), dma((layers,)),
-            dma((steps + 8 * layers * 2,)), dma((steps + 8 * layers * 2,)), dma((steps,)), dma((steps,)),
-            dma((layers, 2, nf)), dma((layers, 2, nf)),
+            dma((24 * layers,)), dma((24 * layers,)), dma((24 * layers,)), dma((24 * layers,)),
+            dma(((2 * layers + 1) * nf,)), dma(((2 * layers + 1) * nf,)), dma((12 * layers,)), dma((12 * layers,)),
+            dma((2 * layers + 1,)), dma((layers,)),
+            dma((2 * steps,)), dma((2 * steps,)), dma((steps,)), dma((steps,)),
+            dma((2 * layers * nf,)), dma((2 * layers * nf,)),
             dma((3, wide)), dma((3, wide)), dma, dma((3,)),
-            pltpu.SemaphoreType.REGULAR((layers, 2)), pltpu.SemaphoreType.REGULAR,
+            pltpu.SemaphoreType.REGULAR((layers, 3)), pltpu.SemaphoreType.REGULAR((layers, 3)), pltpu.SemaphoreType.REGULAR,
         ],
         compiler_params=pltpu.CompilerParams(collective_id=0, has_side_effects=True, vmem_limit_bytes=67043328),
         name="fused_step",

time: 397 us -> 373 us (0.940)
  Pallas kernels: 391 us -> 370 us
    pallas_call x1, Pallas kernels: 377 us -> 356 us  [fused_step(): pl.pallas_call(functools.partial(step_kernel, dims), out_shape=(jax.Shape...]
where the time goes in v4:
time: 373 us; the launch traced here: 372 us
  Pallas kernels  370 us (99%)
    pallas_call x1, Pallas kernels, fused_step(): pl.pallas_call(functools.partial(step_kernel, dims), out_shape=(jax.Shape...  356 us
    pallas_call x1, Pallas kernels, unpack(): pl.pallas_call(unpack_kernel, grid=(layers, steps), in_specs=[pl.BlockSpe...  14 us

profile of v4, /device:TPU:1, one launch (start us, length us, event | category | flops | bytes accessed | tf_op | source)
XLA Modules:
  0.0 372.4 jit_solution(791690279146675549)
XLA Ops:
  0.6 356.4 %fused_step.1 = (bf16[128,1024]{1,0:T(8,128)(2,1)}, f32[3,4,8,24,16,128]{5,4,3,2,1,0:T(8,128)}, f32[24,128]{1,0:T(8,128)}) custom-call(bf16[128,1024]{1,0:T(8,128)(2,1)} %x_ref.1, bf16[128,1024]{1,0:T(8,128)(2,1)} %dy_ref.1, bf16[3,128,4096]{2,1,0:T(8,128)(2,1)} %wg_ref.1, bf16[3,128,4096]{2,1,0:T(8,128)(2,1)} %wu_ref.1, bf16[3,512,1024]{2,1,0:T(8,128)(2,1)} %wd_ref.1, ...), custom_call_target="tpu_custom_call" | custom-call | tf_op jit(solution)/shard_map/fused_step/pallas_call | solution.py:867
  357.1 0.0 copy-start.1
  357.1 0.0 copy-start
  357.1 14.0 %unpack.1 = (f32[3,128,4096]{2,1,0:T(8,128)}, f32[3,128,4096]{2,1,0:T(8,128)}, f32[3,512,1024]{2,1,0:T(8,128)}) custom-call(f32[3,4,8,24,16,128]{5,4,3,2,1,0:T(8,128)} %get-tuple-element.12.g_ref), custom_call_target="tpu_custom_call" | custom-call | tf_op jit(solution)/shard_map/unpack/pallas_call | solution.py:921
  371.1 0.0 copy-done.1
  371.1 0.6 reshape.13
  371.7 0.0 copy-done
  371.7 0.7 copy.12
Async XLA Ops:
  357.1 14.1 %copy-start.1 = (f32[24,128]{1,0:T(8,128)S(1)}, f32[24,128]{1,0:T(8,128)}, u32[]{:S(2)}) copy-start(f32[24,128]{1,0:T(8,128)} %get-tuple-element.16) | copy-start | bytes 36868
  357.1 14.7 %copy-start = (bf16[128,1024]{1,0:T(8,128)(2,1)S(1)}, bf16[128,1024]{1,0:T(8,128)(2,1)}, u32[]{:S(2)}) copy-start(bf16[128,1024]{1,0:T(8,128)(2,1)} %get-tuple-element.22) | copy-start | bytes 786436

commit v5 on v4

v5 whole, which is shorter than its diff:
```python
import functools
import heapq
import jax
import jax.numpy as jnp
from jax import lax
from jax.sharding import PartitionSpec as P
from jax.experimental import pallas as pl
from jax.experimental.pallas import tpu as pltpu

F32 = jnp.float32
BF16 = jnp.bfloat16
LOGICAL = pl.DeviceIdType.LOGICAL
RS, LN = 16, 128
UNIT_BYTES = RS * LN * 4
NORM_EPS = 1e-6
NN = (((1,), (0,)), ((), ()))
NT = (((1,), (1,)), ((), ()))
TN = (((0,), (0,)), ((), ()))
LINK_RATE, CORE_RATE, HOP, CORE_HOP, STEP_COST, HBM_READ, ENTRY = 46.6e3, 500e3, 2.2, 0.9, 0.15, 1.1, 3.5
CORES = "cores"
BOTH, SIGN, BF16_BYTES = (0, 1), (1, -1), 2
FIRST, SECOND, PASS, RELAY, FAR, OWN = range(6)
DIRECT = "direct"
FORWARD, BACKWARD, WEIGHT, ADD, EXCHANGE = 0.7, 0.95, 0.9, 0.15, 5.0


def dot(a, b, dims=NN):
    return lax.dot_general(a, b, dims, preferred_element_type=F32)


def loop(count, work):
    repeat(0, count, work)


def repeat(start, stop, work):
    def step(i, carry):
        work(i)
        return carry
    lax.fori_loop(start, stop, step, 0)


def wait_for(view, sem, device, sent=False):
    copy = pltpu.make_async_remote_copy(
        src_ref=view, dst_ref=view, send_sem=sem, recv_sem=sem, device_id=device, device_id_type=LOGICAL)
    if sent:
        copy.wait_send()
    else:
        copy.wait_recv()


def first(count):
    return pl.ds(0, count)


def wrap(value, size):
    return lax.rem(value + 4 * size, size)


class Clock:
    def __init__(self):
        self.now, self.queue, self.count, self.links = 0.0, [], 0, {}

    def send(self, link, size):
        near = link == CORES
        start = max(self.now, self.links.get(link, 0.0))
        self.links[link] = start + size / (CORE_RATE if near else LINK_RATE)
        return self.links[link] + (CORE_HOP if near else HOP)

    def after(self, ready, work):
        self.count += 1
        heapq.heappush(self.queue, (ready, self.count, work))

    def step(self):
        ready, _, work = heapq.heappop(self.queue)
        self.now = max(self.now, ready) + STEP_COST
        work()

    def run(self, until):
        while self.queue and self.queue[0][0] <= until:
            self.step()

    def busy(self, spent):
        self.now += spent
        self.run(self.now)

    def idle(self, until):
        self.run(until)
        self.now = max(self.now, until)

    def play(self, task):
        for ready in task:
            self.idle(ready)

    def spawn(self, task):
        ready = next(task, None)
        if ready is not None:
            self.after(ready, functools.partial(self.spawn, task))

    def until(self, done):
        while not done():
            self.step()

    def known(self, times, key):
        while key not in times:
            yield self.now + STEP_COST
        yield times[key]


class Job:
    def __init__(self, env, layer, part):
        parts = LAST_SIZES if layer == env.last else PART_SIZES
        sizes, start = (parts[part], env.nf - parts[part]), part * env.nf
        before = sum(parts[:part])
        offsets = before, start - before
        self.split = sum(parts)
        swap = () if part == DOWN else (part,)
        self.env, self.layer, self.part, self.swap = env, layer, part, swap
        self.sizes, self.offsets, self.starts = sizes, offsets, (start, start + sizes[0])
        self.left, self.turned = len(BOTH), 0
        above = env.above(self)
        self.slots = dict(env.jobs[above].slots) if above else {}
        for gather in BOTH[1:] if above else BOTH:
            for phase in BOTH:
                for k in BOTH:
                    self.slots[gather, phase, k] = env.sends, env.receives
                    env.sends += 1
                    env.receives += self.half_ring(phase, k)

    def ring(self, phase, k):
        return ("replica", "dp")[phase ^ k]

    def half_ring(self, phase, k):
        return self.env.size[self.ring(phase, k)] // 2

    def block(self, phase, k, index, side=None):
        env, G, layer = self.env, self.env.G, self.layer
        start, size = self.starts[k], self.sizes[k]
        if side is not None:
            start, size = start + side * (size // 2), size // 2
        units = pl.ds(start, size)
        if phase == 0:
            return G.at[layer, index, :, units] if k == 0 else G.at[layer, :, index, units]
        return G.at[layer, env.y, index, units] if k == 0 else G.at[layer, index, env.z, units]

    def stage(self, phase, k, d, step, side=None):
        env = self.env
        ref, lead = (env.G, (0,)) if self.layer == env.last else (env.S, ())
        base = 0 if k == 0 else self.split
        offset, size = self.offsets[k], self.sizes[k]
        half_total = ((env.units - self.split) if k else self.split) // 2
        at = 2 * (step - 1) + d
        if step == 0:
            units = pl.ds(base + d * half_total + offset // 2, size // 2)
            at = env.nz - 2 if self.ring(phase, k) == "dp" else 2
        elif side is None:
            units = pl.ds(base + offset, size)
        else:
            units = pl.ds(base + offset + side * (size // 2), size // 2)
        every = slice(None)
        if phase == 0:
            place = (at, every) if k == 0 else (every, at)
        else:
            place = (env.ny - 1, at) if k == 0 else (at, env.nz - 1)
        return ref.at[(*lead, *place, units)]

    def many(self, phase, k, count):
        G, some, every = self.env.G, first(count), slice(None)
        units = pl.ds(self.starts[k], self.sizes[k])
        other = every if phase == 0 else 0
        place = (some, other) if phase == k else (other, some)
        return G.at[(self.layer, *place, units)]

    def copy(self, gather, phase, k, d, step, src, dst):
        env = self.env
        send, receive = self.slots[gather, phase, k]
        return pltpu.make_async_remote_copy(
            src_ref=src, dst_ref=dst, send_sem=env.send_sem.at[send], recv_sem=env.recv_sem.at[receive + step],
            device_id=env.device(self.ring(phase, k), SIGN[d]), device_id_type=LOGICAL)

    def take(self, gather, phase, k, step, blocks):
        receive = self.slots[gather, phase, k][1]
        wait_for(self.many(phase, k, blocks), self.env.recv_sem.at[receive + step], self.env.device(self.ring(phase, k), 1))

    def send_time(self, phase, k, d, units):
        env = self.env
        other = (env.nz if k == 0 else env.ny) if phase == 0 else 1
        return env.clock.send((self.ring(phase, k), d), units * other * UNIT_BYTES)

    def reduce_send(self, phase, k, step, early=False):
        size, ready = self.sizes[k], 0.0
        for d in BOTH:
            side = None if step > 1 else BOTH[d - 1] if early else d
            index = self.env.near(self.ring(phase, k), SIGN[d] * (self.half_ring(phase, k) - step))
            stage = self.stage(phase, k, d, step, None if step == 0 else side)
            self.copy(0, phase, k, d, step, self.block(phase, k, index, side), stage).start()
            ready = max(ready, self.send_time(phase, k, d, size if step > 1 else size // 2))
        if not early:
            self.env.clock.after(ready, functools.partial(self.reduce_step, phase, k, step))

    def reduce_start(self, phase, k):
        self.reduce_send(phase, k, 0)
        self.reduce_send(phase, k, 1, True)

    def start(self, phase, k):
        env = self.env
        if phase == 0 and k == 0 and env.above(self):
            pl.semaphore_wait(env.freed.at[env.above(self)], 4)
        self.reduce_start(phase, k)

    def reduce_step(self, phase, k, step):
        half = self.half_ring(phase, k)
        self.take(0, phase, k, step, len(BOTH) if step else 1)
        for d in BOTH:
            index = self.env.near(self.ring(phase, k), SIGN[d] * (half - 1 - step))
            self.block(phase, k, index, None if step else d)[...] += self.stage(phase, k, d, step)[...]
        if step + 1 < half:
            self.reduce_send(phase, k, step + 1)
        elif phase == 0:
            self.halfway()
            self.env.begin(self, 1, k)
        else:
            self.left -= 1
            if self.left == 0:
                self.reduced()

    def halfway(self):
        env, here = self.env, (self.layer, self.part)
        self.turned += 1
        if self.turned == len(BOTH):
            self.wait_sends(0, 0)
            if 0 < self.layer < env.last:
                self.tell(env.freed)
            env.half.add(here)
            env.begin_waiting()

    def tell(self, flags):
        for axis in ("replica", "dp"):
            for sign in SIGN:
                pl.semaphore_signal(flags.at[self.layer, self.part], device_id=self.env.device(axis, sign), device_id_type=LOGICAL)

    def wait_sends(self, gather, phase):
        for k in BOTH:
            ring = self.ring(phase, k)
            send = self.slots[gather, phase, k][0]
            wait_for(self.many(phase, k, self.env.size[ring] - 1), self.env.send_sem.at[send], self.env.device(ring, 1), True)

    def x_copy(self, m, peer, sender):
        env = self.env
        lane = 2 * self.layer + m
        return pltpu.make_async_remote_copy(
            src_ref=env.G.at[self.layer, env.y, env.z, m * env.nf + peer], dst_ref=env.R.at[self.layer, m * env.nf + sender],
            send_sem=env.x_send.at[lane], recv_sem=env.x_recv.at[lane],
            device_id=env.row + peer, device_id_type=LOGICAL)

    def reduced(self):
        env = self.env
        self.wait_sends(0, 1)
        self.tell(env.ready)
        for m in self.swap:
            repeat(1, env.nf, lambda j: self.x_copy(m, wrap(env.f + j, env.nf), env.f).start())
        env.reduced.add((self.layer, self.part))
        env.clock.after(env.clock.now + (EXCHANGE if self.swap else HOP), self.exchanged)

    def exchanged(self):
        env = self.env
        f, nf = env.f, env.nf
        for m in self.swap:
            env.R[self.layer, m * nf + f] = env.G[self.layer, env.y, env.z, m * nf + f]
        for m in self.swap:
            lane, view = 2 * self.layer + m, env.R.at[self.layer, first(nf - 1)]
            wait_for(view, env.x_send.at[lane], env.device("fsdp", 1), True)
            wait_for(view, env.x_recv.at[lane], env.device("fsdp", 1))
        for m in self.swap:
            env.G[self.layer, env.y, env.z, pl.ds(m * nf, nf)] = env.R[self.layer, pl.ds(m * nf, nf)]
        pl.semaphore_wait(env.ready.at[self.layer, self.part], 4)
        self.left = 2
        for k in BOTH:
            self.gather_send(1, k, 0)
        env.exchanged.add((self.layer, self.part))
        env.begin_waiting()

    def gather_send(self, phase, k, step):
        half, ready = self.half_ring(phase, k), 0.0
        for d in BOTH:
            side = d if step + 1 == half else None
            view = self.block(phase, k, self.env.near(self.ring(phase, k), -SIGN[d] * step), side)
            self.copy(1, phase, k, d, step, view, view).start()
            ready = max(ready, self.send_time(phase, k, d, self.sizes[k] if side is None else self.sizes[k] // 2))
        self.env.clock.after(ready, functools.partial(self.gather_step, phase, k, step))

    def gather_step(self, phase, k, step):
        env = self.env
        last = step + 1 == self.half_ring(phase, k)
        self.take(1, phase, k, step, 1 if last else len(BOTH))
        if not last:
            self.gather_send(phase, k, step + 1)
        elif phase == 1:
            self.gather_send(0, k, 0)
        else:
            self.left -= 1
            here = (self.layer, slice(None), slice(None), pl.ds(self.starts[k], self.sizes[k]))
            pltpu.make_async_copy(env.G.at[here], env.out_ref.at[here], env.out_sem).start()


class Env:
    def __init__(self, dims):
        self.exchanged, self.reduced, self.half, self.waiting, self.clock = set(), set(), set(), [], Clock()
        self.sends = self.receives = 0
        self.ny, self.nz, self.nf = dims[1:4]
        self.last = dims[0] - 1
        self.f, self.y, self.z = lax.axis_index("fsdp"), lax.axis_index("replica"), lax.axis_index("dp")
        self.size = {"fsdp": self.nf, "replica": self.ny, "dp": self.nz}
        self.pos = {"fsdp": self.f, "replica": self.y, "dp": self.z}
        stride = {"fsdp": 1, "replica": self.nf, "dp": self.nf * self.ny}
        me = self.f + stride["replica"] * self.y + stride["dp"] * self.z
        self.row = me - self.f
        self.shift = {a: [wrap(self.pos[a] + k, n) for k in range(n)] for a, n in self.size.items()}
        self.ids = {a: [me + (p - self.pos[a]) * stride[a] for p in self.shift[a]] for a in self.size}

    def near(self, axis, k):
        return self.shift[axis][k % self.size[axis]]

    def device(self, axis, k):
        return self.ids[axis][k % self.size[axis]]

    def above(self, job):
        return (job.layer + 1, job.part) if job.layer + 1 < self.last else None

    def begin(self, job, phase, k):
        self.waiting.append((job, phase, k))
        self.begin_waiting()

    def begin_job(self, job):
        for k in BOTH:
            self.begin(job, 0, k)

    def begin_waiting(self):
        for item in list(self.waiting):
            job, phase, k = item
            if item in self.waiting and (not self.above(job) or self.above(job) in (self.exchanged if phase else self.half)):
                self.waiting.remove(item)
                job.start(phase, k)

    def settle(self, layer):
        self.clock.until(lambda: {(layer, part) for part in (GATE, UP, DOWN)} <= self.reduced)


GATE, UP, DOWN = range(3)
PART_SIZES, LAST_SIZES = (4, 4, 6), (6, 4, 6)


def step_kernel(dims, x_ref, dy_ref, wg_ref, wu_ref, wd_ref, gain_ref, y_ref, out_ref, gain_out,
                WB, WD, N, GA, UA, DH, O, DS, MS, H, DGU, G, S, R, gain_buf, gain_row,
                ag_send, ag_recv, rs_send, rs_recv, wx_send, wx_recv, wz_send, wz_recv, wy_send, wy_recv, w_sem, wd_sem,
                j_send, j_recv, x_send, x_recv, g_send, g_recv, out_sem, io_sem, ready, freed, credit):
    layers, ny, nz, nf, tok, depth, hid = dims
    nx, q = nf // 2, depth // nf // ny
    tile = min(256, depth)
    last = layers - 1

    env = Env(dims)
    f, y, z = env.f, env.y, env.z
    x, c = f // 2, f % 2
    env.G, env.S, env.R, env.out_ref = G, S, R, out_ref
    env.send_sem, env.recv_sem = j_send, j_recv
    env.x_send, env.x_recv, env.ready, env.freed, env.out_sem = x_send, x_recv, ready, freed, out_sem
    env.units = 3 * nf
    clock = env.clock
    env.jobs = jobs = {}
    for l in reversed(range(layers)):
        for part in (GATE, UP, DOWN):
            jobs[l, part] = Job(env, l, part)

    chips = [wrap(x + k, nx) for k in range(nx)]
    same, opposite_core = [2 * p + c for p in chips], [2 * p + (1 - c) for p in chips]
    fid = {id(v): env.row + v for v in same + opposite_core}

    def dev(off, opposite=False):
        return (opposite_core if opposite else same)[off % nx]

    partner = dev(0, True)
    axes = [("fsdp", f, nf), ("replica", y, ny), ("dp", z, nz)]

    barrier = pltpu.get_barrier_semaphore()
    for axis, pos, size in axes:
        for j in range(1, size):
            pl.semaphore_signal(barrier, device_id=env.device(axis, j), device_id_type=LOGICAL)

    x_copy = pltpu.make_async_copy(x_ref, H.at[0], io_sem.at[0])
    dy_copy = pltpu.make_async_copy(dy_ref, DH.at[last % 2, f], io_sem.at[1])
    x_copy.start()
    dy_copy.start()
    wd_copies = [pltpu.make_async_copy(wd_ref.at[l], WD.at[l], wd_sem.at[l]) for l in range(layers)]
    weights = (wg_ref, wu_ref)
    y_at = [env.near("replica", k) for k in range(ny)]
    parts = (first(nf // 2), pl.ds(nf // 2, nf // 2))
    direct = pl.ds(ny * q // 2, ny * q // 2)
    direct_lane = 2 * layers
    shared = {}

    def share(l, m, hops=0):
        size = q // 2 if (l, m) == BOTH else q
        return pl.ds(y_at[hops % ny] * size, size)

    odd = lax.rem(z, 2)
    z_partner = env.ids["dp"][0] + (1 - 2 * odd) * nf * ny

    def fetched(l, m, other=False):
        if l == 0:
            return share(l, m)
        return pl.ds(y_at[0] * q + (1 - odd if other else odd) * (q // 2), q // 2)

    def wz_copy(l, m, other=False):
        view = WB.at[l, m, :, fetched(l, m, other)]
        return pltpu.make_async_remote_copy(
            src_ref=view, dst_ref=view, send_sem=wz_send.at[2 * l + m], recv_sem=wz_recv.at[2 * l + m],
            device_id=z_partner, device_id_type=LOGICAL)

    def own_rows(l, m, rows, sem):
        src = weights[m].at[l, rows, pl.ds(pl.multiple_of(f * hid, hid), hid)]
        return pltpu.make_async_copy(src, WB.at[l, m, f, rows], w_sem.at[sem])

    own_copies = {(l, m): own_rows(l, m, fetched(l, m), 2 * l + m) for l in range(layers) for m in BOTH}
    own_copies[DIRECT] = own_rows(*BOTH, direct, 2 * layers)
    for copy in own_copies.values():
        copy.start()
    for copy in wd_copies:
        copy.start()
    pl.semaphore_wait(barrier, nf + ny + nz - 3)
    clock.busy(ENTRY)

    def wx_copy(l, m, peer, sender, rows, lane):
        return pltpu.make_async_remote_copy(
            src_ref=weights[m].at[l, rows, pl.ds(pl.multiple_of(peer * hid, hid), hid)], dst_ref=WB.at[l, m, sender, rows],
            send_sem=wx_send.at[lane], recv_sem=wx_recv.at[lane], device_id=env.row + peer, device_id_type=LOGICAL)

    def wx_sets(l):
        return [(l, m, fetched(l, m), 2 * l + m) for m in BOTH]

    def wx_post(key, l, m, rows, lane):
        repeat(1, nf, lambda j: wx_copy(l, m, wrap(f + j, nf), f, rows, lane).start())
        for d in BOTH:
            shared[key] = clock.send(d, nx * rows.size * hid * BF16_BYTES) + HBM_READ

    def wx_take(key, l, m, rows, lane):
        yield from clock.known(shared, key)
        own_copies[key].wait()
        wait_for(WB.at[l, m, first(nf - 1), rows], wx_recv.at[lane], env.device("fsdp", 1))

    def wx_start(l):
        for args in wx_sets(l):
            wx_post(args[:2], *args)

    def wy_copy(l, m, kind, d, arrived=False):
        hops = (kind == PASS) + arrived
        lane = 2 * l + m
        part = parts[BOTH[d - (kind == SECOND)]]
        view = WB.at[l, m, part, share(l, m, -SIGN[d] * hops)]
        return pltpu.make_async_remote_copy(
            src_ref=view, dst_ref=view, send_sem=wy_send.at[lane], recv_sem=wy_recv.at[2 * lane + (kind > FIRST)],
            device_id=env.device("replica", SIGN[d]), device_id_type=LOGICAL)

    def wy_send_one(l, m, kind, d):
        wy_copy(l, m, kind, d).start()
        shared[l, m, kind, d] = clock.send(("replica", d), nf // 2 * share(l, m).size * hid * BF16_BYTES)

    def wy_take(l, m, later):
        for kind in (SECOND, PASS) if later else (FIRST,):
            for d in BOTH:
                yield from clock.known(shared, (l, m, kind, d))
        rows = first(share(l, m).size * (1 + later))
        wait_for(WB.at[l, m, :, rows], wy_recv.at[2 * (2 * l + m) + later], env.device("replica", 1))

    def weights_task():
        for l in range(layers):
            for args in wx_sets(l):
                yield from wx_take(args[:2], *args)
                if l:
                    wz_copy(*args[:2]).start()
                    yield clock.send(("dp", 0), nf * q // 2 * hid * BF16_BYTES)
                    wz_copy(*args[:2], True).wait_recv()
                for kind in (FIRST, SECOND):
                    for d in BOTH:
                        wy_send_one(*args[:2], kind, d)
            for m in BOTH:
                yield from wy_take(l, m, 0)
                for d in BOTH:
                    wy_send_one(l, m, PASS, d)

    def weights_here(l):
        while l in claimed and l not in arrived:
            yield clock.now + STEP_COST
        if l in arrived:
            return
        claimed.add(l)
        if l == 0:
            yield from wx_take(*straight)
        for m in BOTH:
            yield from wy_take(l, m, 1)
        wd_copies[l].wait()
        arrived.add(l)

    claimed, arrived = set(), set()
    straight = DIRECT, *BOTH, direct, direct_lane

    class Gather:
        def __init__(self, lanes, buf, slot, base, size):
            self.lanes, self.buf, self.slot, self.ready = lanes, buf, slot, {}
            self.whole = pl.ds(base, size)
            self.halves = (pl.ds(base, size // 2), pl.ds(base + size // 2, size // 2))

        def copy(self, kind, d):
            hops = (kind in (PASS, RELAY)) + (kind == FAR) * nx // len(BOTH)
            block = dev(-SIGN[d] * hops)
            rows = self.whole if kind in (RELAY, OWN) else self.halves[d - (kind == SECOND)]
            target = partner if kind in (RELAY, FAR, OWN) else dev(SIGN[d])
            view = self.buf.at[self.slot, block, rows]
            return rows.size, pltpu.make_async_remote_copy(
                src_ref=view, dst_ref=view, send_sem=ag_send.at[self.lanes], recv_sem=ag_recv.at[self.lanes * (OWN + 1) + kind],
                device_id=fid[id(target)], device_id_type=LOGICAL)

        def send(self, *kinds):
            for kind in kinds:
                ready = 0.0
                for d in BOTH[:1] if kind == OWN else BOTH:
                    size, copy = self.copy(kind, d)
                    copy.start()
                    ready = max(ready, clock.send(CORES if kind in (RELAY, FAR, OWN) else d, size * depth * BF16_BYTES))
                self.ready[kind] = ready

        def blocks(self, count):
            return self.buf.at[self.slot, first(count), self.whole]

        def take(self, *kinds):
            for kind in kinds:
                yield from clock.known(self.ready, kind)
                wait_for(self.blocks(2 if kind == RELAY else 1), ag_recv.at[self.lanes * (OWN + 1) + kind], fid[id(partner)])

        def start(self):
            self.send(FIRST, OWN, SECOND)

        def mid(self):
            for kind, onward in ((FIRST, PASS), (SECOND, RELAY)):
                yield from self.take(kind)
                self.send(onward)

        def end(self):
            yield from self.take(PASS)
            self.send(FAR)

        def drain(self):
            wait_for(self.blocks(nf - 1), ag_send.at[self.lanes], fid[id(partner)], True)

    chunk = min(16, tok // 8)

    def rows_at(start, j):
        return pl.ds(pl.multiple_of(start + j * chunk, chunk), chunk)

    class Reduce:
        def __init__(self, lanes, base, size):
            self.lanes, self.base, self.size, self.arrive = lanes, base, size, {}
            self.rows, self.local = pl.ds(base, size), pl.ds(base // 2, size // 2)

        def d2d(self, i, xp, core):
            return pltpu.make_async_remote_copy(
                src_ref=O.at[xp, core, self.rows], dst_ref=DS.at[xp, self.rows], send_sem=rs_send.at[2 * self.lanes],
                recv_sem=rs_recv.at[(nx + 2) * self.lanes + i], device_id=fid[id(partner)], device_id_type=LOGICAL)

        def msg(self, k, d):
            half = self.size // 2
            lane = (nx + 2) * self.lanes + nx + (k > 0)
            off, side = (2, d) if k == 0 else (SIGN[d], d if k == 3 else 1 - d)
            size, slot, at = half, (0 if k == 0 else 2), 0
            if k in (1, 2):
                size, slot = half // 2, 1
                at = (k - 1) * size
            return size, pltpu.make_async_remote_copy(
                src_ref=O.at[chips[off % nx], c, pl.ds(self.base + side * half + at, size)],
                dst_ref=MS.at[d, slot, pl.ds(self.base // 2 + at, size)],
                send_sem=rs_send.at[2 * self.lanes + 1], recv_sem=rs_recv.at[lane], device_id=fid[id(dev(SIGN[d]))], device_id_type=LOGICAL)

        def post(self, k, d):
            size, copy = self.msg(k, d)
            copy.start()
            self.arrive[k, d] = clock.send(d, size * depth * 4)

        def take(self, later):
            yield max(self.arrive[k, d] for k in ((1, 2, 3) if later else (0,)) for d in BOTH)
            view = MS.at[:, pl.ds(later, 1 + later), self.local]
            wait_for(view, rs_recv.at[(nx + 2) * self.lanes + nx + later], fid[id(partner)])

        def combine(self, i, off):
            xp = chips[off % nx]
            yield self.arrive[i]
            self.d2d(i, xp, c).wait_recv()

            def add(j):
                rows = rows_at(self.base, j)
                O[xp, c, rows] += DS[xp, rows]
            loop(self.size // chunk, add)
            clock.busy(ADD)

        def near(self):
            for i, d in ((1, 0), (2, 1)):
                yield from self.combine(i, SIGN[d])
                self.post(1, d)

        def start(self):
            yield from self.combine(3, 2)
            for k in (0, 2):
                for d in BOTH:
                    self.post(k, d)
            yield from self.combine(0, 0)

        def mid(self):
            half = self.size // 2
            yield from self.take(0)
            for d in BOTH:
                def add(j):
                    rows = rows_at(self.base + d * half, j)
                    O[chips[SIGN[d] % nx], c, rows] += MS[d, 0, rows_at(self.base // 2, j)]
                loop(half // chunk, add)
                self.post(3, d)

        def end(self, body):
            half = self.size // 2
            yield from self.take(1)
            for side in BOTH:
                def step(j):
                    rows, local = rows_at(self.base + side * half, j), rows_at(self.base // 2, j)
                    body(rows, O[x, c, rows] + (MS[0, 2 - side, local] + MS[1, 1 + side, local]))
                loop(half // chunk, step)
            clock.busy(5 * ADD)
            wait_for(O.at[:, 0, self.rows], rs_send.at[2 * self.lanes], fid[id(partner)], True)
            wait_for(O.at[first(nx - 1), 0, self.rows], rs_send.at[2 * self.lanes + 1], fid[id(partner)], True)

        def pairs(self, gathers, body, cost, after_mid=None):
            def step(i):
                xp = wrap(x + i + i // 2 - 2 * (i // 3), nx)
                body(xp, self.rows)
                self.d2d(i, xp, 1 - c).start()

            def go(start, stop):
                repeat(start, stop, step)
                for i in range(start, stop):
                    clock.now += cost
                    self.arrive[i] = clock.send(CORES, self.size * depth * 4)
                clock.busy(0.0)

            go(0, 1)
            for gather in gathers:
                yield from gather.take(RELAY)
            go(1, 3)
            late = not all(gather.ready.get(FAR, self.arrive[2]) < self.arrive[2] for gather in gathers)
            if late:
                yield from self.near()
            for gather in gathers:
                yield from gather.take(FAR)
            go(3, nx)
            if not late:
                yield from self.near()

    def rms(hidden):
        return lax.rsqrt(jnp.mean(hidden * hidden, axis=-1, keepdims=True) + NORM_EPS)

    def down_grad(l):
        group = nf // 2
        zs = tile // (group * RS)

        def body(j, carry):
            lhs = GA[l, :, :, :, pl.ds(pl.multiple_of(j * tile, tile), tile)].reshape(-1, tile)
            for i in range(depth // tile):
                res = dot(lhs, DH[l % 2, :, :, pl.ds(i * tile, tile)].reshape(-1, tile), TN)
                for h in range(tile // LN):
                    col = i * (tile // LN) + h
                    for zi in range(zs):
                        rows = res[zi * group * RS:(zi + 1) * group * RS, h * LN:(h + 1) * LN]
                        G[l, col // 2, j * zs + zi, pl.ds(2 * nf + (col % 2) * group, group)] = rows.reshape(group, RS, LN)
            return carry
        lax.fori_loop(0, hid // tile, body, 0)

    def up_grad(l):
        fs = tile // (nz_rows * RS)

        def body(j, carry):
            lhs = N[l, :, :, pl.ds(pl.multiple_of(j * tile, tile), tile)].reshape(-1, tile)
            for m in BOTH:
                for i in range(hid // tile):
                    res = dot(lhs, DGU[m, :, :, :, pl.ds(i * tile, tile)].reshape(-1, tile), TN)
                    for h in range(tile // LN):
                        for fi in range(fs):
                            rows = res[fi * nz_rows * RS:(fi + 1) * nz_rows * RS, h * LN:(h + 1) * LN]
                            G[l, i * (tile // LN) + h, :, m * nf + j * fs + fi] = rows.reshape(nz_rows, RS, LN)
            return carry
        lax.fori_loop(0, depth // tile, body, 0)

    nz_rows = depth // nf // RS
    part = tok // 2
    fwd = [[Gather(g, N, l, g * part, part) for g in BOTH] for l in range(layers)]
    bwd = [Gather(2, DH, l % 2, 0, tok) for l in range(layers)]
    dy_task = bwd[last]

    def activations(l, xp, rows, cols):
        tokens = N[l, pl.ds(2 * xp, 2), rows].reshape(-1, depth)
        gate = dot(tokens, WB[l, 0, :, :, cols].reshape(depth, tile)).astype(BF16)
        up = dot(tokens, WB[l, 1, :, :, cols].reshape(depth, tile)).astype(BF16)
        return gate, up

    def flat(ref, *index):
        value = ref[index]
        return value.reshape(-1, value.shape[-1])

    def product(l, ref, lead, xp, rows):
        prod = flat(ref, *lead, xp, slice(None), rows)
        for j in range(depth // tile):
            cols = pl.ds(j * tile, tile)
            O[xp, :, rows, cols] = dot(prod, WD[l, :, cols]).reshape(2, rows.size, tile)

    def forward(l, xp, rows):
        shape = (2, rows.size, tile)
        for j in range(hid // tile):
            cols = pl.ds(j * tile, tile)
            gate, up = activations(l, xp, rows, cols)
            GA[l, xp, :, rows, cols] = gate.reshape(shape)
            UA[l, xp, :, rows, cols] = up.reshape(shape)
            DGU[0, xp, :, rows, cols] = (jax.nn.silu(gate.astype(F32)) * up.astype(F32)).astype(BF16).reshape(shape)
        product(l, DGU, (0,), xp, rows)

    def backward(l, xp, rows):
        cot = DH[l % 2, pl.ds(2 * xp, 2)].reshape(-1, depth)
        shape = (2, tok, tile)
        for j in range(hid // tile):
            cols = pl.ds(j * tile, tile)
            here = (l, xp, slice(None), slice(None), cols)
            gate, up = activations(l, xp, rows, cols) if l == last else (flat(GA, *here), flat(UA, *here))
            gate, up = gate.astype(F32), up.astype(F32)
            d_prod = dot(cot, WD[l, cols, :], NT).astype(BF16).astype(F32)
            sig = jax.nn.sigmoid(gate)
            GA[here] = (gate * sig * up).astype(BF16).reshape(shape)
            DGU[0, xp, :, :, cols] = (d_prod * up * sig * (1.0 + gate * (1.0 - sig))).astype(BF16).reshape(shape)
            DGU[1, xp, :, :, cols] = (d_prod * gate * sig).astype(BF16).reshape(shape)
        d_gate, d_up = flat(DGU, 0, xp), flat(DGU, 1, xp)
        block = depth // nf
        for j in range(depth // tile):
            sub = pl.ds(j * tile // block, tile // block)
            total = dot(d_gate, WB[l, 0, sub].reshape(tile, hid), NT) + dot(d_up, WB[l, 1, sub].reshape(tile, hid), NT)
            O[xp, :, :, pl.ds(j * tile, tile)] = total.reshape(shape)

    def normalize(l, rows, hidden):
        N[l, f, rows] = (hidden * rms(hidden) * gain_ref[l:l + 1]).astype(BF16)

    def half_task(g):
        for l in range(last):
            gather, reduce = fwd[l][g], Reduce(g, g * part, part)
            yield from gather.mid()
            if g and l == 0:
                wx_start(1)
                dy_task.start()
                clock.spawn(dy_task.mid())
                clock.spawn(dy_task.end())
            if g and l + 2 < layers:
                wx_start(l + 2)
            clock.spawn(gather.end())
            yield from gather.take(OWN)
            yield from weights_here(l)
            yield from reduce.pairs([gather], functools.partial(forward, l), FORWARD / len(BOTH))
            yield from reduce.start()
            yield from reduce.mid()

            def next_hidden(rows, total, l=l):
                hidden = (H[l, rows].astype(F32) + total).astype(BF16)
                H[l + 1, rows] = hidden
                normalize(l + 1, rows, hidden.astype(F32))
            yield from reduce.end(next_hidden)
            gather.drain()
            fwd[l + 1][g].start()
        yield from fwd[last][g].mid()
        yield from fwd[last][g].end()
        finished.add(g)

    finished = set()
    wx_start(0)
    x_copy.wait()
    for g in BOTH:
        def enter(j):
            rows = rows_at(g * part, j)
            normalize(0, rows, H[0, rows].astype(F32))
        loop(part // chunk, enter)
        clock.busy(ADD)
        fwd[0][g].start()
    wx_post(*straight)
    dy_copy.wait()
    clock.spawn(weights_task())
    for g in BOTH:
        clock.spawn(half_task(g))
    clock.until(lambda: FAR in fwd[last][0].ready)

    for l in reversed(range(layers)):
        reduce = Reduce(2, 0, tok)
        if l == last:
            gathers = fwd[l]
            clock.play(dy_task.take(RELAY, FAR, OWN))
            clock.play(weights_here(l))
        else:
            gathers = [bwd[l]]
            bwd[l].start()
            clock.spawn(bwd[l].mid())
            clock.spawn(bwd[l].end())
        for gather in gathers:
            clock.play(gather.take(OWN))
        clock.play(reduce.pairs(gathers, functools.partial(backward, l), FORWARD + BACKWARD if l == last else BACKWARD))
        clock.play(reduce.start())
        if l == 0:
            env.settle(last)
        down_grad(l)
        clock.busy(WEIGHT)
        env.begin_job(jobs[l, DOWN])
        up_grad(l)
        clock.busy(2 * WEIGHT)
        env.begin_job(jobs[l, GATE])
        env.begin_job(jobs[l, UP])
        clock.play(reduce.mid())
        bwd[l].drain()

        def next_cot(rows, total, l=l):
            d_normed = total.astype(BF16).astype(F32)
            hidden = H[l, rows].astype(F32)
            inv = rms(hidden)
            if l > 0:
                scaled = d_normed * gain_ref[l:l + 1]
                cot = DH[l % 2, f, rows].astype(F32)
                d_hidden = cot + inv * scaled - hidden * (inv * inv * inv) * jnp.mean(scaled * hidden, axis=-1, keepdims=True)
                DH[(l - 1) % 2, f, rows] = d_hidden.astype(BF16)
            gain_row[...] += jnp.sum(d_normed * hidden * inv, axis=0, keepdims=True)
        gain_row[...] = jnp.zeros((1, depth), F32)
        clock.play(reduce.end(next_cot))
        lanes = depth // LN
        for j in range(lanes):
            gain_buf[0, f, l * lanes + j:l * lanes + j + 1] = gain_row[:, j * LN:(j + 1) * LN]

    def gain_copy(stage, j):
        axis, pos, size = axes[stage]
        return pltpu.make_async_remote_copy(
            src_ref=gain_buf.at[stage, pos], dst_ref=gain_buf.at[stage, pos],
            send_sem=g_send.at[stage], recv_sem=g_recv.at[stage],
            device_id=env.device(axis, j), device_id_type=LOGICAL)

    def gain_send(stage):
        for j in range(1, axes[stage][2]):
            gain_copy(stage, j).start()
        clock.after(clock.now + 2 * EXCHANGE, functools.partial(gain_sum, stage))

    def gain_sum(stage):
        axis, pos, size = axes[stage]
        wait_for(gain_buf.at[stage, first(size - 1)], g_recv.at[stage], env.device(axis, 1))
        total = gain_buf[stage, 0]
        for i in range(1, size):
            total = total + gain_buf[stage, i]
        if stage == 2:
            gain_out[...] = total
        else:
            gain_buf[stage + 1, axes[stage + 1][1]] = total
            gain_send(stage + 1)

    gain_send(0)

    for target in (partner, dev(1), dev(-1)):
        pl.semaphore_signal(credit, device_id=fid[id(target)], device_id_type=LOGICAL)
    pl.semaphore_wait(credit, 3)
    reduce = Reduce(2, 0, tok)
    clock.play(reduce.pairs([], functools.partial(product, last, GA, (last,)), FORWARD))
    clock.play(reduce.start())
    clock.play(reduce.mid())

    def output(rows, total):
        H[0, rows] = (H[last, rows].astype(F32) + total).astype(BF16)
    clock.play(reduce.end(output))
    y_copy = pltpu.make_async_copy(H.at[0], y_ref, io_sem.at[2])
    y_copy.start()
    while clock.queue:
        clock.step()

    y_copy.wait()
    for gather in fwd[last]:
        gather.drain()
    for l, m, rows, lane in [straight[1:]] + [args for l in range(layers) for args in wx_sets(l)]:
        wait_for(WB.at[l, m, first(nf - 1), rows], wx_send.at[lane], env.device("fsdp", 1), True)
    for l in range(layers):
        for m in BOTH:
            if l:
                wz_copy(l, m).wait_send()
            wait_for(WB.at[l, m, :, first(3 * share(l, m).size)], wy_send.at[2 * l + m], env.device("replica", 1), True)
    for job in jobs.values():
        for phase in BOTH:
            job.wait_sends(1, phase)
    for stage, (axis, _, size) in enumerate(axes):
        wait_for(gain_buf.at[stage, first(size - 1)], g_send.at[stage], env.device(axis, 1), True)
    pltpu.make_async_copy(G, out_ref, out_sem).wait()


def fused_step(x, dy, wg, wu, wd, gain, dims):
    layers, ny, nz, nf, tok, depth, hid = dims
    nx = nf // 2
    vm, hbm = pl.BlockSpec(memory_space=pltpu.VMEM), pl.BlockSpec(memory_space=pl.ANY)
    dma = pltpu.SemaphoreType.DMA
    three, two, more = (dma((n,)) for n in (layers, 2 * layers, 2 * layers + 1))
    blocks = (layers, ny, nz, 3 * nf, RS, LN)
    lines = layers * depth // LN
    wide = max(nf, ny, nz)
    return pl.pallas_call(
        functools.partial(step_kernel, dims),
        out_shape=(jax.ShapeDtypeStruct((tok, depth), BF16), jax.ShapeDtypeStruct(blocks, F32), jax.ShapeDtypeStruct((lines, LN), F32)),
        in_specs=[hbm] * 5 + [vm],
        out_specs=(hbm, hbm, vm),
        scratch_shapes=[
            pltpu.VMEM((layers, 2, nf, depth // nf, hid), BF16),
            pltpu.VMEM((layers, hid, depth), BF16),
            pltpu.VMEM((layers, nf, tok, depth), BF16),
            pltpu.VMEM((layers, nx, 2, tok, hid), BF16),
            pltpu.VMEM((layers, nx, 2, tok, hid), BF16),
            pltpu.VMEM((2, nf, tok, depth), BF16),
            pltpu.VMEM((nx, 2, tok, depth), F32),
            pltpu.VMEM((nx, tok, depth), F32),
            pltpu.VMEM((2, 3, tok // 2, depth), F32),
            pltpu.VMEM((layers, tok, depth), BF16),
            pltpu.VMEM((2, nx, 2, tok, hid), BF16),
            pltpu.VMEM(blocks, F32),
            pltpu.VMEM(blocks[1:], F32),
            pltpu.VMEM((layers, 2 * nf, RS, LN), F32),
            pltpu.VMEM((3, wide, lines, LN), F32),
            pltpu.VMEM((1, depth), F32),
            three, dma((3 * (OWN + 1),)), two, dma((3 * (nx + 2),)),
            more, more, two, two, two, dma((4 * layers,)), more, three,
            dma((20 * layers,)), dma((10 * layers * (ny // 2 + nz // 2),)),
            two, two, three, three, dma, three,
            *[pltpu.SemaphoreType.REGULAR((layers, DOWN + 1))] * 2, pltpu.SemaphoreType.REGULAR,
        ],
        compiler_params=pltpu.CompilerParams(collective_id=0, has_side_effects=True, vmem_limit_bytes=67043328),
        name="fused_step",
    )(x, dy, wg, wu, wd, gain)


def unpack_kernel(g_ref, gate_ref, up_ref, down_ref):
    ny, nzb, units = g_ref.shape[:3]
    nf = units // 3
    for k in range(nzb):
        for i in range(ny):
            for m, ref in enumerate((gate_ref, up_ref)):
                for j in range(nf):
                    col = (j * ny + i) * LN
                    ref[k * RS:(k + 1) * RS, col:col + LN] = g_ref[i, k, m * nf + j]
            for h in BOTH:
                for r in range(nf // 2):
                    row, col = (k * (nf // 2) + r) * RS, (2 * i + h) * LN
                    down_ref[row:row + RS, col:col + LN] = g_ref[i, k, 2 * nf + h * (nf // 2) + r]


def unpack(out, dims, steps=4):
    layers, ny, nz, nf = dims
    nzb = nz // steps
    wide, tall = nf * ny * LN, (nf // 2) * RS
    return pl.pallas_call(
        unpack_kernel, grid=(layers, steps),
        in_specs=[pl.BlockSpec((None, ny, nzb, 3 * nf, RS, LN), lambda l, z: (l, 0, z, 0, 0, 0))],
        out_specs=[pl.BlockSpec((None, nzb * RS, wide), lambda l, z: (l, z, 0))] * 2
        + [pl.BlockSpec((None, nzb * tall, 2 * ny * LN), lambda l, z: (l, z, 0))],
        out_shape=[jax.ShapeDtypeStruct((layers, nz * RS, wide), F32)] * 2
        + [jax.ShapeDtypeStruct((layers, nz * tall, 2 * ny * LN), F32)],
        name="unpack")(out)


TOKEN_AXES = ("dp", "replica", "fsdp")


def solution(mesh):
    ny, nz, nf = mesh.shape["replica"], mesh.shape["dp"], mesh.shape["fsdp"]
    tok_spec, shard_spec, full_spec = P(TOKEN_AXES, None), P(None, "fsdp", None), P(None, None)

    def device_step(x, dy, wg, wu, wd, gain):
        layers, depth = gain.shape
        dims = (layers, ny, nz, nf)
        out, blocks, gain_sum = fused_step(x, dy, wg, wu, wd, gain, dims + (x.shape[0], depth, wd.shape[1]))
        dw_gate, dw_up, dw_down = unpack(blocks, dims)
        return out, dw_gate, dw_up, dw_down, gain_sum.reshape(gain.shape)

    return jax.shard_map(
        device_step, mesh=mesh, in_specs=(tok_spec, tok_spec, shard_spec, shard_spec, shard_spec, full_spec),
        out_specs=(tok_spec, shard_spec, shard_spec, shard_spec, full_spec), check_vma=False)
```

time: 373 us -> 354 us (0.949)
  Pallas kernels: 370 us -> 350 us
    pallas_call x1, Pallas kernels: 356 us -> 333 us  [fused_step(): pl.pallas_call(functools.partial(step_kernel, dims), out_shape=(jax.Shape...]
where the time goes in v5:
time: 354 us; the launch traced here: 352 us
  Pallas kernels  350 us (99%)
    pallas_call x1, Pallas kernels, fused_step(): pl.pallas_call(functools.partial(step_kernel, dims), out_shape=(jax.Shape...  333 us
    pallas_call x1, Pallas kernels, unpack(): pl.pallas_call(unpack_kernel, grid=(layers, steps), in_specs=[pl.BlockSpe...  17.2 us

profile of v5, /device:TPU:1, one launch (start us, length us, event | category | flops | bytes accessed | tf_op | source)
XLA Modules:
  0.0 351.9 jit_solution(8836550446904133745)
XLA Ops:
  0.6 332.8 %fused_step.1 = (bf16[128,1024]{1,0:T(8,128)(2,1)}, f32[3,4,8,24,16,128]{5,4,3,2,1,0:T(8,128)}, f32[24,128]{1,0:T(8,128)}) custom-call(bf16[128,1024]{1,0:T(8,128)(2,1)} %x_ref.1, bf16[128,1024]{1,0:T(8,128)(2,1)} %dy_ref.1, bf16[3,128,4096]{2,1,0:T(8,128)(2,1)} %wg_ref.1, bf16[3,128,4096]{2,1,0:T(8,128)(2,1)} %wu_ref.1, bf16[3,512,1024]{2,1,0:T(8,128)(2,1)} %wd_ref.1, ...), custom_call_target="tpu_custom_call" | custom-call | tf_op jit(solution)/shard_map/fused_step/pallas_call | solution.py:910
  333.4 0.0 copy-start.1
  333.4 0.0 copy-start
  333.5 17.2 %unpack.1 = (f32[3,128,4096]{2,1,0:T(8,128)}, f32[3,128,4096]{2,1,0:T(8,128)}, f32[3,512,1024]{2,1,0:T(8,128)}) custom-call(f32[3,4,8,24,16,128]{5,4,3,2,1,0:T(8,128)} %get-tuple-element.12.g_ref), custom_call_target="tpu_custom_call" | custom-call | tf_op jit(solution)/shard_map/unpack/pallas_call | solution.py:962
  350.6 0.0 copy-done.1
  350.6 0.6 reshape.13
  351.2 0.0 copy-done
  351.2 0.7 copy.12
Async XLA Ops:
  333.4 17.2 %copy-start.1 = (f32[24,128]{1,0:T(8,128)S(1)}, f32[24,128]{1,0:T(8,128)}, u32[]{:S(2)}) copy-start(f32[24,128]{1,0:T(8,128)} %get-tuple-element.16) | copy-start | bytes 36868
  333.4 17.8 %copy-start = (bf16[128,1024]{1,0:T(8,128)(2,1)S(1)}, bf16[128,1024]{1,0:T(8,128)(2,1)}, u32[]{:S(2)}) copy-start(bf16[128,1024]{1,0:T(8,128)(2,1)} %get-tuple-element.22) | copy-start | bytes 786436

commit v6 on v5

--- a/solution.py
+++ b/solution.py
@@ -346,7 +346,7 @@
 
 
 GATE, UP, DOWN = range(3)
-PART_SIZES, LAST_SIZES = (4, 4, 6), (6, 4, 6)
+PART_SIZES, LAST_SIZES = (4, 6, 6), (6, 4, 4)
 
 
 def step_kernel(dims, x_ref, dy_ref, wg_ref, wu_ref, wd_ref, gain_ref, y_ref, out_ref, gain_out,
@@ -809,12 +809,12 @@
         for gather in gathers:
             clock.play(gather.take(OWN))
         clock.play(reduce.pairs(gathers, functools.partial(backward, l), FORWARD + BACKWARD if l == last else BACKWARD))
-        clock.play(reduce.start())
         if l == 0:
             env.settle(last)
         down_grad(l)
         clock.busy(WEIGHT)
         env.begin_job(jobs[l, DOWN])
+        clock.play(reduce.start())
         up_grad(l)
         clock.busy(2 * WEIGHT)
         env.begin_job(jobs[l, GATE])
@@ -940,32 +940,55 @@
     )(x, dy, wg, wu, wd, gain)
 
 
-def unpack_kernel(g_ref, gate_ref, up_ref, down_ref):
-    ny, nzb, units = g_ref.shape[:3]
+def unpack_kernel(blocks_ref, gate_ref, up_ref, down_ref, blocks, gate, up, down, in_sem, out_sem):
+    layers, ny, nz, units = blocks.shape[:4]
     nf = units // 3
-    for k in range(nzb):
-        for i in range(ny):
-            for m, ref in enumerate((gate_ref, up_ref)):
+    pairs, tall = nz // 2, nf // 2 * RS
+    count = layers * pairs
+
+    def load(i):
+        here = (i // pairs, slice(None), pl.ds(i % pairs * 2, 2))
+        return pltpu.make_async_copy(blocks_ref.at[here], blocks.at[here], in_sem.at[i])
+
+    def stores(i):
+        for ref, buf, rows in ((gate_ref, gate, RS), (up_ref, up, RS), (down_ref, down, tall)):
+            here = (i // pairs, pl.ds(pl.multiple_of(i % pairs * (2 * rows), 2 * rows), 2 * rows))
+            yield pltpu.make_async_copy(buf.at[here], ref.at[here], out_sem)
+
+    loop(count, lambda i: load(i).start())
+
+    def move(i):
+        load(i).wait()
+        l = i // pairs
+        for k in BOTH:
+            z = i % pairs * 2 + k
+            rows = pl.ds(pl.multiple_of(z * RS, RS), RS)
+            for y in range(ny):
                 for j in range(nf):
-                    col = (j * ny + i) * LN
-                    ref[k * RS:(k + 1) * RS, col:col + LN] = g_ref[i, k, m * nf + j]
-            for h in BOTH:
-                for r in range(nf // 2):
-                    row, col = (k * (nf // 2) + r) * RS, (2 * i + h) * LN
-                    down_ref[row:row + RS, col:col + LN] = g_ref[i, k, 2 * nf + h * (nf // 2) + r]
-
-
-def unpack(out, dims, steps=4):
+                    cols = pl.ds((j * ny + y) * LN, LN)
+                    gate[l, rows, cols] = blocks[l, y, z, j]
+                    up[l, rows, cols] = blocks[l, y, z, nf + j]
+                for j in range(nf):
+                    h, r = j // (nf // 2), j % (nf // 2)
+                    down[l, pl.ds(pl.multiple_of(z * tall + r * RS, RS), RS), pl.ds((2 * y + h) * LN, LN)] = blocks[l, y, z, 2 * nf + j]
+        for copy in stores(i):
+            copy.start()
+    loop(count, move)
+    for buf, ref in ((gate, gate_ref), (up, up_ref), (down, down_ref)):
+        pltpu.make_async_copy(buf, ref, out_sem).wait()
+
+
+def unpack(out, dims):
     layers, ny, nz, nf = dims
-    nzb = nz // steps
-    wide, tall = nf * ny * LN, (nf // 2) * RS
+    wide, tall = (layers, nz * RS, nf * ny * LN), (layers, nz * nf // 2 * RS, 2 * ny * LN)
+    shapes = (wide, wide, tall)
+    hbm = pl.BlockSpec(memory_space=pl.ANY)
     return pl.pallas_call(
-        unpack_kernel, grid=(layers, steps),
-        in_specs=[pl.BlockSpec((None, ny, nzb, 3 * nf, RS, LN), lambda l, z: (l, 0, z, 0, 0, 0))],
-        out_specs=[pl.BlockSpec((None, nzb * RS, wide), lambda l, z: (l, z, 0))] * 2
-        + [pl.BlockSpec((None, nzb * tall, 2 * ny * LN), lambda l, z: (l, z, 0))],
-        out_shape=[jax.ShapeDtypeStruct((layers, nz * RS, wide), F32)] * 2
-        + [jax.ShapeDtypeStruct((layers, nz * tall, 2 * ny * LN), F32)],
+        unpack_kernel, in_specs=[hbm], out_specs=[hbm] * len(shapes),
+        out_shape=[jax.ShapeDtypeStruct(shape, F32) for shape in shapes],
+        scratch_shapes=[pltpu.VMEM(out.shape, F32), *[pltpu.VMEM(shape, F32) for shape in shapes],
+                        pltpu.SemaphoreType.DMA((layers * nz // 2,)), pltpu.SemaphoreType.DMA],
+        compiler_params=pltpu.CompilerParams(vmem_limit_bytes=48 * 2**20),
         name="unpack")(out)
 
 

time: 354 us -> 355 us (level); the launches traced: 352 us -> 349 us
    pallas_call x1, Pallas kernels: 17.2 us -> 13.4 us  [unpack(): pl.pallas_call(unpack_kernel, in_specs=[hbm], out_specs=[hbm] * len(shape...]
where the time goes in v6:
time: 355 us; the launch traced here: 349 us
  Pallas kernels  347 us (98%)
    pallas_call x1, Pallas kernels, fused_step(): pl.pallas_call(functools.partial(step_kernel, dims), out_shape=(jax.Shape...  334 us
    pallas_call x1, Pallas kernels, unpack(): pl.pallas_call(unpack_kernel, in_specs=[hbm], out_specs=[hbm] * len(shape...  13.4 us

profile of v6, /device:TPU:1, one launch (start us, length us, event | category | flops | bytes accessed | tf_op | source)
XLA Modules:
  0.0 348.9 jit_solution(17879610929153214315)
XLA Ops:
  0.6 333.5 %fused_step.1 = (bf16[128,1024]{1,0:T(8,128)(2,1)}, f32[3,4,8,24,16,128]{5,4,3,2,1,0:T(8,128)}, f32[24,128]{1,0:T(8,128)}) custom-call(bf16[128,1024]{1,0:T(8,128)(2,1)} %x_ref.1, bf16[128,1024]{1,0:T(8,128)(2,1)} %dy_ref.1, bf16[3,128,4096]{2,1,0:T(8,128)(2,1)} %wg_ref.1, bf16[3,128,4096]{2,1,0:T(8,128)(2,1)} %wu_ref.1, bf16[3,512,1024]{2,1,0:T(8,128)(2,1)} %wd_ref.1, ...), custom_call_target="tpu_custom_call" | custom-call | tf_op jit(solution)/shard_map/fused_step/pallas_call | solution.py:910
  334.1 0.0 copy-start.1
  334.2 0.0 copy-start
  334.2 13.4 %unpack.1 = (f32[3,128,4096]{2,1,0:T(8,128)}, f32[3,128,4096]{2,1,0:T(8,128)}, f32[3,512,1024]{2,1,0:T(8,128)}) custom-call(f32[3,4,8,24,16,128]{5,4,3,2,1,0:T(8,128)} %get-tuple-element.12.blocks_ref), custom_call_target="tpu_custom_call" | custom-call | tf_op jit(solution)/shard_map/unpack/pallas_call | solution.py:986
  347.6 0.0 copy-done.1
  347.6 0.6 reshape.13
  348.2 0.0 copy-done
  348.2 0.7 copy.12
Async XLA Ops:
  334.1 13.5 %copy-start.1 = (f32[24,128]{1,0:T(8,128)S(1)}, f32[24,128]{1,0:T(8,128)}, u32[]{:S(2)}) copy-start(f32[24,128]{1,0:T(8,128)} %get-tuple-element.16) | copy-start | bytes 36868
  334.2 14.1 %copy-start = (bf16[128,1024]{1,0:T(8,128)(2,1)S(1)}, bf16[128,1024]{1,0:T(8,128)(2,1)}, u32[]{:S(2)}) copy-start(bf16[128,1024]{1,0:T(8,128)(2,1)} %get-tuple-element.22) | copy-start | bytes 786436

commit v7 on v6

--- a/solution.py
+++ b/solution.py
@@ -346,7 +346,7 @@
 
 
 GATE, UP, DOWN = range(3)
-PART_SIZES, LAST_SIZES = (4, 6, 6), (6, 4, 4)
+PART_SIZES, LAST_SIZES = (4, 4, 6), (6, 4, 6)
 
 
 def step_kernel(dims, x_ref, dy_ref, wg_ref, wu_ref, wd_ref, gain_ref, y_ref, out_ref, gain_out,
@@ -809,12 +809,12 @@
         for gather in gathers:
             clock.play(gather.take(OWN))
         clock.play(reduce.pairs(gathers, functools.partial(backward, l), FORWARD + BACKWARD if l == last else BACKWARD))
+        clock.play(reduce.start())
         if l == 0:
             env.settle(last)
         down_grad(l)
         clock.busy(WEIGHT)
         env.begin_job(jobs[l, DOWN])
-        clock.play(reduce.start())
         up_grad(l)
         clock.busy(2 * WEIGHT)
         env.begin_job(jobs[l, GATE])

time: 355 us -> 350 us (0.986); the launches traced: 349 us -> 348 us
  no operation moved by 1% of the time
where the time goes in v7:
time: 350 us; the launch traced here: 348 us
  Pallas kernels  346 us (99%)
    pallas_call x1, Pallas kernels, fused_step(): pl.pallas_call(functools.partial(step_kernel, dims), out_shape=(jax.Shape...  333 us
    pallas_call x1, Pallas kernels, unpack(): pl.pallas_call(unpack_kernel, in_specs=[hbm], out_specs=[hbm] * len(shape...  13.4 us

profile of v7, /device:TPU:1, one launch (start us, length us, event | category | flops | bytes accessed | tf_op | source)
XLA Modules:
  0.0 348.2 jit_solution(2504148232697755003)
XLA Ops:
  0.6 332.8 %fused_step.1 = (bf16[128,1024]{1,0:T(8,128)(2,1)}, f32[3,4,8,24,16,128]{5,4,3,2,1,0:T(8,128)}, f32[24,128]{1,0:T(8,128)}) custom-call(bf16[128,1024]{1,0:T(8,128)(2,1)} %x_ref.1, bf16[128,1024]{1,0:T(8,128)(2,1)} %dy_ref.1, bf16[3,128,4096]{2,1,0:T(8,128)(2,1)} %wg_ref.1, bf16[3,128,4096]{2,1,0:T(8,128)(2,1)} %wu_ref.1, bf16[3,512,1024]{2,1,0:T(8,128)(2,1)} %wd_ref.1, ...), custom_call_target="tpu_custom_call" | custom-call | tf_op jit(solution)/shard_map/fused_step/pallas_call | solution.py:910
  333.4 0.0 copy-start.1
  333.4 0.0 copy-start
  333.5 13.4 %unpack.1 = (f32[3,128,4096]{2,1,0:T(8,128)}, f32[3,128,4096]{2,1,0:T(8,128)}, f32[3,512,1024]{2,1,0:T(8,128)}) custom-call(f32[3,4,8,24,16,128]{5,4,3,2,1,0:T(8,128)} %get-tuple-element.12.blocks_ref), custom_call_target="tpu_custom_call" | custom-call | tf_op jit(solution)/shard_map/unpack/pallas_call | solution.py:986
  346.9 0.0 copy-done.1
  346.9 0.6 reshape.13
  347.5 0.0 copy-done
  347.5 0.7 copy.12
Async XLA Ops:
  333.4 13.5 %copy-start.1 = (f32[24,128]{1,0:T(8,128)S(1)}, f32[24,128]{1,0:T(8,128)}, u32[]{:S(2)}) copy-start(f32[24,128]{1,0:T(8,128)} %get-tuple-element.16) | copy-start | bytes 36868
  333.4 14.1 %copy-start = (bf16[128,1024]{1,0:T(8,128)(2,1)S(1)}, bf16[128,1024]{1,0:T(8,128)(2,1)}, u32[]{:S(2)}) copy-start(bf16[128,1024]{1,0:T(8,128)(2,1)} %get-tuple-element.22) | copy-start | bytes 786436

commit v8 on v7

--- a/solution.py
+++ b/solution.py
@@ -809,12 +809,12 @@
         for gather in gathers:
             clock.play(gather.take(OWN))
         clock.play(reduce.pairs(gathers, functools.partial(backward, l), FORWARD + BACKWARD if l == last else BACKWARD))
-        clock.play(reduce.start())
         if l == 0:
             env.settle(last)
         down_grad(l)
         clock.busy(WEIGHT)
         env.begin_job(jobs[l, DOWN])
+        clock.play(reduce.start())
         up_grad(l)
         clock.busy(2 * WEIGHT)
         env.begin_job(jobs[l, GATE])

time: 350 us -> 346 us (0.989)
  no operation moved by 1% of the time
where the time goes in v8:
time: 346 us
  Pallas kernels  344 us (99%)
    pallas_call x1, Pallas kernels, fused_step(): pl.pallas_call(functools.partial(step_kernel, dims), out_shape=(jax.Shape...  330 us
    pallas_call x1, Pallas kernels, unpack(): pl.pallas_call(unpack_kernel, in_specs=[hbm], out_specs=[hbm] * len(shape...  13.4 us

profile of v8, /device:TPU:1, one launch (start us, length us, event | category | flops | bytes accessed | tf_op | source)
XLA Modules:
  0.0 345.9 jit_solution(13991339459444912723)
XLA Ops:
  0.6 330.5 %fused_step.1 = (bf16[128,1024]{1,0:T(8,128)(2,1)}, f32[3,4,8,24,16,128]{5,4,3,2,1,0:T(8,128)}, f32[24,128]{1,0:T(8,128)}) custom-call(bf16[128,1024]{1,0:T(8,128)(2,1)} %x_ref.1, bf16[128,1024]{1,0:T(8,128)(2,1)} %dy_ref.1, bf16[3,128,4096]{2,1,0:T(8,128)(2,1)} %wg_ref.1, bf16[3,128,4096]{2,1,0:T(8,128)(2,1)} %wu_ref.1, bf16[3,512,1024]{2,1,0:T(8,128)(2,1)} %wd_ref.1, ...), custom_call_target="tpu_custom_call" | custom-call | tf_op jit(solution)/shard_map/fused_step/pallas_call | solution.py:910
  331.1 0.0 copy-start.1
  331.1 0.0 copy-start
  331.2 13.4 %unpack.1 = (f32[3,128,4096]{2,1,0:T(8,128)}, f32[3,128,4096]{2,1,0:T(8,128)}, f32[3,512,1024]{2,1,0:T(8,128)}) custom-call(f32[3,4,8,24,16,128]{5,4,3,2,1,0:T(8,128)} %get-tuple-element.12.blocks_ref), custom_call_target="tpu_custom_call" | custom-call | tf_op jit(solution)/shard_map/unpack/pallas_call | solution.py:986
  344.6 0.0 copy-done.1
  344.6 0.6 reshape.13
  345.2 0.0 copy-done
  345.2 0.7 copy.12
Async XLA Ops:
  331.1 13.5 %copy-start.1 = (f32[24,128]{1,0:T(8,128)S(1)}, f32[24,128]{1,0:T(8,128)}, u32[]{:S(2)}) copy-start(f32[24,128]{1,0:T(8,128)} %get-tuple-element.16) | copy-start | bytes 36868
  331.1 14.1 %copy-start = (bf16[128,1024]{1,0:T(8,128)(2,1)S(1)}, bf16[128,1024]{1,0:T(8,128)(2,1)}, u32[]{:S(2)}) copy-start(bf16[128,1024]{1,0:T(8,128)(2,1)} %get-tuple-element.22) | copy-start | bytes 786436

commit v9 on v8

--- a/solution.py
+++ b/solution.py
@@ -116,10 +116,14 @@
         swap = () if part == DOWN else (part,)
         self.env, self.layer, self.part, self.swap = env, layer, part, swap
         self.sizes, self.offsets, self.starts = sizes, offsets, (start, start + sizes[0])
-        self.left, self.turned = len(BOTH), 0
+        self.left, self.turned, self.gathered = len(BOTH), 0, False
         above = env.above(self)
-        self.slots = dict(env.jobs[above].slots) if above else {}
-        for gather in BOTH[1:] if above else BOTH:
+        self.before = env.jobs[env.last, part] if above else None
+        if above:
+            self.slots = {key: (self.before if key[0] else env.jobs[above]).slots[key] for key in self.before.slots}
+            return
+        self.slots = {}
+        for gather in BOTH:
             for phase in BOTH:
                 for k in BOTH:
                     self.slots[gather, phase, k] = env.sends, env.receives
@@ -255,6 +259,10 @@
     def reduced(self):
         env = self.env
         self.wait_sends(0, 1)
+        if self.before:
+            env.clock.until(lambda: self.before.gathered)
+            for phase in BOTH:
+                self.before.wait_sends(1, phase)
         self.tell(env.ready)
         for m in self.swap:
             repeat(1, env.nf, lambda j: self.x_copy(m, wrap(env.f + j, env.nf), env.f).start())
@@ -298,6 +306,7 @@
             self.gather_send(0, k, 0)
         else:
             self.left -= 1
+            self.gathered = self.left == 0
             here = (self.layer, slice(None), slice(None), pl.ds(self.starts[k], self.sizes[k]))
             pltpu.make_async_copy(env.G.at[here], env.out_ref.at[here], env.out_sem).start()
 
@@ -890,8 +899,8 @@
             if l:
                 wz_copy(l, m).wait_send()
             wait_for(WB.at[l, m, :, first(3 * share(l, m).size)], wy_send.at[2 * l + m], env.device("replica", 1), True)
-    for job in jobs.values():
-        for phase in BOTH:
+    for (l, _), job in jobs.items():
+        for phase in BOTH if l < last else ():
             job.wait_sends(1, phase)
     for stage, (axis, _, size) in enumerate(axes):
         wait_for(gain_buf.at[stage, first(size - 1)], g_send.at[stage], env.device(axis, 1), True)
@@ -931,7 +940,7 @@
             pltpu.VMEM((1, depth), F32),
             three, dma((3 * (OWN + 1),)), two, dma((3 * (nx + 2),)),
             more, more, two, two, two, dma((4 * layers,)), more, three,
-            dma((20 * layers,)), dma((10 * layers * (ny // 2 + nz // 2),)),
+            dma((16 * layers,)), dma((8 * layers * (ny // 2 + nz // 2),)),
             two, two, three, three, dma, three,
             *[pltpu.SemaphoreType.REGULAR((layers, DOWN + 1))] * 2, pltpu.SemaphoreType.REGULAR,
         ],

time: 346 us -> 346 us (level)
  no operation moved by 1% of the time
where the time goes in v9:
time: 346 us
  Pallas kernels  344 us (99%)
    pallas_call x1, Pallas kernels, fused_step(): pl.pallas_call(functools.partial(step_kernel, dims), out_shape=(jax.Shape...  330 us
    pallas_call x1, Pallas kernels, unpack(): pl.pallas_call(unpack_kernel, in_specs=[hbm], out_specs=[hbm] * len(shape...  13.4 us

profile of v9, /device:TPU:1, one launch (start us, length us, event | category | flops | bytes accessed | tf_op | source)
XLA Modules:
  0.0 345.5 jit_solution(9996954162637525428)
XLA Ops:
  0.6 330.1 %fused_step.1 = (bf16[128,1024]{1,0:T(8,128)(2,1)}, f32[3,4,8,24,16,128]{5,4,3,2,1,0:T(8,128)}, f32[24,128]{1,0:T(8,128)}) custom-call(bf16[128,1024]{1,0:T(8,128)(2,1)} %x_ref.1, bf16[128,1024]{1,0:T(8,128)(2,1)} %dy_ref.1, bf16[3,128,4096]{2,1,0:T(8,128)(2,1)} %wg_ref.1, bf16[3,128,4096]{2,1,0:T(8,128)(2,1)} %wu_ref.1, bf16[3,512,1024]{2,1,0:T(8,128)(2,1)} %wd_ref.1, ...), custom_call_target="tpu_custom_call" | custom-call | tf_op jit(solution)/shard_map/fused_step/pallas_call | solution.py:919
  330.7 0.0 copy-start.1
  330.7 0.0 copy-start
  330.7 13.4 %unpack.1 = (f32[3,128,4096]{2,1,0:T(8,128)}, f32[3,128,4096]{2,1,0:T(8,128)}, f32[3,512,1024]{2,1,0:T(8,128)}) custom-call(f32[3,4,8,24,16,128]{5,4,3,2,1,0:T(8,128)} %get-tuple-element.12.blocks_ref), custom_call_target="tpu_custom_call" | custom-call | tf_op jit(solution)/shard_map/unpack/pallas_call | solution.py:995
  344.2 0.0 copy-done.1
  344.2 0.6 reshape.13
  344.8 0.0 copy-done
  344.8 0.7 copy.12
Async XLA Ops:
  330.7 13.5 %copy-start.1 = (f32[24,128]{1,0:T(8,128)S(1)}, f32[24,128]{1,0:T(8,128)}, u32[]{:S(2)}) copy-start(f32[24,128]{1,0:T(8,128)} %get-tuple-element.16) | copy-start | bytes 36868
  330.7 14.1 %copy-start = (bf16[128,1024]{1,0:T(8,128)(2,1)S(1)}, bf16[128,1024]{1,0:T(8,128)(2,1)}, u32[]{:S(2)}) copy-start(bf16[128,1024]{1,0:T(8,128)(2,1)} %get-tuple-element.22) | copy-start | bytes 786436
